TPU v7x, 32 devices: a whole 2x2x4 slice. The times are simulated.
32 devices in a mesh: section: 2 (over core), dp: 4 (over z), mp: 4 (over y, x).
Axes of the slice: x: 2, y: 2, z: 4, core: 2. Of those that a mesh axis runs over, the one named last changes fastest.
Arguments:
- block_input: bfloat16 [8, 1024, 1024], P('dp', None, 'mp'), may hold values from -6 to 6
- cotangent: bfloat16 [8, 1024, 1024], P('dp', None, 'mp'), may hold values from -6 to 6
- lengths: int32 [8], P('dp'), may hold values from 1 to 1024, 5120 in all
- ln_gain: float32 [2, 1024], P('section'), may hold values from 0.5 to 1.5
- ln_bias: float32 [2, 1024], P('section'), may hold values from -2 to 2
- w_qkv: bfloat16 [2, 3, 1024, 1024], P('section', None, None, 'mp'), may hold values from -0.1875 to 0.1875
- w_out: bfloat16 [2, 1024, 1024], P('section', 'mp'), may hold values from -1.5 to 1.5
- w_up: bfloat16 [2, 1024, 4096], P('section', None, 'mp'), may hold values from -0.1875 to 0.1875
- w_down: bfloat16 [2, 4096, 1024], P('section', 'mp'), may hold values from -0.09375 to 0.09375
- freq_table: bfloat16 [2, 16, 64, 64], P('section', 'mp'), may hold values from -0.75 to 0.75
- feat_weight: float32 [2, 16, 64], P('section', 'mp'), may hold values from 0.5 to 2
Outputs:
- boundary: float32 [2, 8, 1024, 1024], P('section', 'dp', None, 'mp')
- gain_grad: float32 [2, 1024], P('section', 'mp')
- bias_grad: float32 [2, 1024], P('section', 'mp')
- qkv_grad: float32 [2, 3, 1024, 1024], P('section', None, 'dp', 'mp')
- out_grad: float32 [2, 1024, 1024], P('section', 'mp', 'dp')
- up_grad: float32 [2, 1024, 4096], P('section', 'dp', 'mp')
- down_grad: float32 [2, 4096, 1024], P('section', 'mp', 'dp')
- freq_grad: float32 [2, 16, 64, 64], P('section', 'mp')
- feat_grad: float32 [2, 16, 64], P('section', 'mp')
Inputs may be any that keep to these rules, and one draw needn't show every extreme that they name: Slot n holds lengths[n] real tokens at its start; later positions are padding.
All inputs are finite; a program needn't handle non-finite values. No bound on the sum of `lengths` on one device may be relied on, other than what follows from the above.
Results may differ from a plain program's by a relative error of at most 0.03.
Values may be sent and summed in bfloat16 or wider, within the bound.
No kernel may reach another device: no remote copies, remote signals or barrier semaphores. Data moves between devices by JAX's collectives and lax.ppermute only.
A program may use at most 384 MiB of HBM per device.

v0:
```python
import functools
import math

import jax
import jax.numpy as jnp
from jax import lax
from jax.experimental import pallas as pl
from jax.experimental.pallas import tpu as pltpu
from jax.sharding import PartitionSpec as P

ROT = 16
TILE = 256
HEAD = 64
LANES = 256
EPS = 1e-05
F32 = jnp.float32
BF16 = jnp.bfloat16
RSQRT2 = math.sqrt(0.5)
RSQRT2PI = 1.0 / math.sqrt(2.0 * math.pi)
SAVED = 14


def dot_nn(a, b):
    return lax.dot_general(a, b, (((1,), (0,)), ((), ())), preferred_element_type=F32)


def dot_nt(a, b):
    return lax.dot_general(a, b, (((1,), (1,)), ((), ())), preferred_element_type=F32)


def dot_tn(a, b):
    return lax.dot_general(a, b, (((0,), (0,)), ((), ())), preferred_element_type=F32)


def split(values):
    high = values.astype(BF16)
    return high, (values - high.astype(F32)).astype(BF16)


def iota(shape, dim):
    return lax.broadcasted_iota(jnp.int32, shape, dim)


def partner(values):
    later = pltpu.roll(values, LANES - ROT // 2, 1)
    earlier = pltpu.roll(values, ROT // 2, 1)
    lower = iota(values.shape, 1) % HEAD < ROT // 2
    return jnp.where(lower, later, earlier)


def twice(table):
    return jnp.concatenate([table, table], axis=1)


def head_of(shape, dim):
    return iota(shape, dim) // HEAD


def weight_copies(refs, w_in, w_out, sems, which):
    qkv, up, out, down = refs
    ends = [(qkv.at[0, t], w_in.at[:, t * LANES:(t + 1) * LANES]) for t in range(3)] + [
        (up.at[0], w_in.at[:, 3 * LANES:]), (out.at[0], w_out.at[0:LANES, :]), (down.at[0], w_out.at[LANES:, :])]
    return [pltpu.make_async_copy(*ends[i], sems.at[i]) for i in which]


def start_weights(meta, mine, other, w_in, w_out, sems, order):
    def start(refs):
        for copy in weight_copies(refs, w_in, w_out, sems, order):
            copy.start()

    @pl.when(meta[1] == 1)
    def _():
        start(mine)

    @pl.when(meta[1] != 1)
    def _():
        start(other)


def wait_weights(step, refs, w_in, w_out, sems, which):
    @pl.when(step == 0)
    def _():
        for copy in weight_copies(refs, w_in, w_out, sems, which):
            copy.wait()


def forward_kernel(carried, phased, *refs):
    refs = list(refs)
    take = lambda n: [refs.pop(0) for _ in range(n)]
    meta, lens = take(2)
    p0, p1, p2, p3a, p3b, gain, bias, mix_hi, mix_lo, feat_w, cos_t, sin_t = take(12)
    mine, other = take(4), take(4)
    if carried:
        state_in, ksum_in = take(2)
        take(SAVED)
    parts = take(5 if phased else 4)
    normed, xhat, rstd, rq_o, rk_o, qf_o, kf_o, v_o, hcat, dgelu, invz, att_o, prior_s, prior_k = take(SAVED)
    state, ksum, w_in, w_out, sems = take(5)
    tile = pl.program_id(0)
    rank = meta[0]
    half = LANES // 2

    @pl.when(tile == 0)
    def _():
        start_weights(meta, mine, other, w_in, w_out, sems, (0, 1, 2, 3, 4, 5))
        if carried:
            state[...] = state_in[...]
            ksum[...] = ksum_in[...]
        else:
            state[...] = jnp.zeros_like(state)
            ksum[...] = jnp.zeros_like(ksum)

    pieces = [p0[...].astype(F32), p1[...].astype(F32), p2[...].astype(F32),
              jnp.concatenate([p3a[...], p3b[...]], axis=1).astype(F32)]
    width = 4 * LANES
    mean = jnp.sum(pieces[0] + pieces[1] + pieces[2] + pieces[3], axis=1, keepdims=True) * (1.0 / width)
    pieces = [piece - mean for piece in pieces]
    squares = sum(piece * piece for piece in pieces)
    factor = lax.rsqrt(jnp.sum(squares, axis=1, keepdims=True) * (1.0 / width) + EPS)
    for r in range(4):
        at = pl.ds(pl.multiple_of((rank ^ r) * LANES, LANES), LANES)
        hat = pieces[r] * factor
        if r == 0:
            xhat[...] = hat
        normed[:, at] = (hat * gain[:, at] + bias[:, at]).astype(BF16)
    rstd[...] = jnp.broadcast_to(factor, (TILE, half))
    tokens = normed[...]

    wait_weights(tile, mine, w_in, w_out, sems, (0, 1, 2))
    cosine, sine = twice(cos_t[...]), twice(sin_t[...])
    query = dot_nn(tokens, w_in[:, 0:LANES])
    key = dot_nn(tokens, w_in[:, LANES:2 * LANES])
    value = dot_nn(tokens, w_in[:, 2 * LANES:3 * LANES]).astype(BF16)
    rq = query * cosine + partner(query) * sine
    rk = key * cosine + partner(key) * sine
    weight = feat_w[...]

    def logits(rows):
        high, low = split(rows)
        return dot_nn(high, mix_hi[...]) + dot_nn(low, mix_hi[...]) + dot_nn(high, mix_lo[...])

    positions = lens[1] + tile * TILE + iota((TILE, LANES), 0)
    real = (positions < lens[0]).astype(F32)
    qf = (weight * jnp.exp(logits(rq))).astype(BF16)
    kf = (weight * jnp.exp(logits(rk)) * real).astype(BF16)
    rq_o[...] = rq.astype(BF16)
    rk_o[...] = rk.astype(BF16)
    qf_o[...] = qf
    kf_o[...] = kf
    v_o[...] = value

    square = (TILE, TILE)
    lower = iota(square, 0) >= iota(square, 1)
    same = head_of(square, 0) == head_of(square, 1)
    cumulative = dot_nn(lower.astype(BF16), kf) + ksum[0:1, :]
    high, low = split(qf.astype(F32) * cumulative)
    ones = same.astype(BF16)
    inverse = 1.0 / (dot_nn(high, ones) + dot_nn(low, ones))
    prior = jnp.where(same, state[...], 0.0)
    prior_hi, prior_lo = split(prior)
    numer = dot_nn(qf, prior_hi) + dot_nn(qf, prior_lo)
    lane_head = head_of((TILE, LANES), 1)
    zero = jnp.zeros((TILE, LANES), BF16)
    for h in range(LANES // HEAD):
        here = lane_head == h
        scores = dot_nt(qf, jnp.where(here, kf, zero))
        scores = jnp.where(lower, scores, 0.0).astype(BF16)
        numer = numer + dot_nn(scores, jnp.where(here, value, zero))
    prior_s[0] = prior
    prior_k[0] = ksum[...]
    state[...] = state[...] + dot_tn(kf, value)
    ksum[...] = jnp.broadcast_to(cumulative[TILE - 1:TILE, :], ksum.shape)
    invz[...] = inverse
    attended = numer * inverse
    att_o[...] = attended
    hcat[:, 0:LANES] = attended.astype(BF16)

    wait_weights(tile, mine, w_in, w_out, sems, (3,))
    for c in range(4):
        cols = slice(c * LANES, (c + 1) * LANES)
        up = dot_nn(tokens, w_in[:, (3 + c) * LANES:(4 + c) * LANES])
        cdf = 0.5 * (1.0 + lax.erf(up * RSQRT2))
        hcat[:, (1 + c) * LANES:(2 + c) * LANES] = (up * cdf).astype(BF16)
        dgelu[:, cols] = (cdf + up * (RSQRT2PI * jnp.exp(-0.5 * up * up))).astype(BF16)

    wait_weights(tile, mine, w_in, w_out, sems, (4, 5))
    hidden = hcat[...]
    emit(rank, lambda at: dot_nn(hidden, w_out[:, at]), parts)


def emit(rank, product, parts):
    half = LANES // 2
    for r in range(4):
        at = pl.ds(pl.multiple_of((rank ^ r) * LANES, LANES), LANES)
        part = product(at)
        if len(parts) == 4:
            parts[r][...] = part.astype(parts[r].dtype)
            continue
        sx, sy, k0, ka, kb = parts
        if r == 0:
            k0[...] = part
        elif r == 1:
            sx[0] = part[:, :half].astype(BF16)
            kb[...] = part[:, half:]
        elif r == 2:
            ka[...] = part[:, :half]
            sy[0] = part[:, half:].astype(BF16)
        else:
            sx[1] = part[:, :half].astype(BF16)
            sy[1] = part[:, half:].astype(BF16)


def backward_kernel(carried, phased, *refs):
    refs = list(refs)
    take = lambda n: [refs.pop(0) for _ in range(n)]
    meta, = take(1)
    grad, normed, rq, rk, qf_i, kf_i, v_i, att_i, dgelu, invz, prior_s, prior_k, gain, bias, mix_hi, cos_t, sin_t = take(17)
    mine, other = take(4), take(4)
    if carried:
        state_in, gsum_in, dmix_in, fsum_in = take(4)
        take(2)
    parts = take(5 if phased else 4)
    stats, dcat, state, gsum, dmix, fsum = take(6)
    w_in, w_out, sems = take(3)
    step = pl.program_id(0)
    rank = meta[0]

    @pl.when(step == 0)
    def _():
        start_weights(meta, mine, other, w_in, w_out, sems, (4, 5, 0, 1, 2, 3))
        if carried:
            state[...] = state_in[...]
            gsum[...] = gsum_in[...]
            dmix[...] = dmix_in[...]
            fsum[...] = fsum_in[...]
        else:
            state[...] = jnp.zeros_like(state)
            gsum[...] = jnp.zeros_like(gsum)
            dmix[...] = jnp.zeros_like(dmix)
            fsum[...] = jnp.zeros_like(fsum)

    wait_weights(step, mine, w_in, w_out, sems, (4, 5))
    g = grad[...]
    d_att = dot_nt(g, w_out[0:LANES, :]).astype(BF16).astype(F32)
    square = (TILE, TILE)
    same = head_of(square, 0) == head_of(square, 1)
    ones = same.astype(BF16)
    inverse = invz[...]
    dn = (d_att * inverse).astype(BF16)
    dn32 = dn.astype(F32)
    high, low = split(dn32 * att_i[...])
    dden = -(dot_nn(high, ones) + dot_nn(low, ones))
    den_hi = dden.astype(BF16).astype(F32)
    roll_hi = pltpu.roll(den_hi, HEAD, 1)
    roll_lo = pltpu.roll(dden - den_hi, HEAD, 1)
    qf, kf, value = qf_i[...], kf_i[...], v_i[...]
    zero = jnp.zeros((TILE, LANES), BF16)
    one = jnp.ones((TILE, LANES), BF16)
    lane = iota((TILE, LANES), 1)
    lane_head = lane // HEAD
    below = iota(square, 0) >= iota(square, 1)
    above = iota(square, 0) <= iota(square, 1)
    prior_hi, prior_lo = split(prior_s[0])
    later_hi, later_lo = split(jnp.where(same, state[...], 0.0))
    d_qf = dot_nt(dn, prior_hi) + dot_nt(dn, prior_lo) + prior_k[0, 0:1, :] * dden
    d_kf = dot_nt(value, later_hi) + dot_nt(value, later_lo) + gsum[0:1, :]
    d_v = dot_nn(kf, later_hi)
    heads = LANES // HEAD
    for h in range(heads):
        here = lane_head == h
        spare = HEAD * ((h + 1) % heads)
        left = jnp.where(lane == spare, roll_hi, jnp.where(lane == spare + 1, roll_lo, dn32)).astype(BF16)
        right = jnp.where(here, value, jnp.where((lane == spare) | (lane == spare + 1), one, zero))
        k_here = jnp.where(here, kf, zero)
        q_here = jnp.where(here, qf, zero)
        d_here = jnp.where(here, dn, zero)
        scores_t = jnp.where(above, dot_nt(k_here, qf), 0.0).astype(BF16)
        ds = jnp.where(below, dot_nt(left, right), 0.0).astype(BF16)
        ds_t = jnp.where(above, dot_nt(right, left), 0.0).astype(BF16)
        d_qf = d_qf + dot_nn(ds, k_here)
        d_kf = d_kf + dot_nn(ds_t, q_here)
        d_v = d_v + dot_nn(scores_t, d_here)
    state[...] = state[...] + dot_tn(qf, dn)
    gsum[...] = gsum[...] + jnp.sum(qf.astype(F32) * dden, axis=0, keepdims=True)
    dlq = d_qf * qf.astype(F32)
    dlk = d_kf * kf.astype(F32)
    fsum[...] = fsum[...] + jnp.sum(dlq + dlk, axis=0, keepdims=True)
    dlq, dlk = dlq.astype(BF16), dlk.astype(BF16)
    dmix[...] = dmix[...] + dot_tn(rq[...], dlq) + dot_tn(rk[...], dlk)
    cosine, sine = twice(cos_t[...]), twice(sin_t[...])
    for c, dl in ((0, dlq), (1, dlk)):
        dr = dot_nt(dl, mix_hi[...])
        dcat[:, c * LANES:(c + 1) * LANES] = (dr * cosine - partner(dr) * sine).astype(BF16)
    dcat[:, 2 * LANES:3 * LANES] = d_v.astype(BF16)
    for c in range(4):
        cols = slice(c * LANES, (c + 1) * LANES)
        d_act = dot_nt(g, w_out[(1 + c) * LANES:(2 + c) * LANES, :])
        dcat[:, (3 + c) * LANES:(4 + c) * LANES] = (d_act * dgelu[:, cols].astype(F32)).astype(BF16)
    wait_weights(step, mine, w_in, w_out, sems, (0, 1, 2, 3))
    wide = dcat[...]
    row = iota((8, LANES), 0)
    first, second = (row == 0).astype(BF16), (row == 1).astype(BF16)
    totals = []

    def product(at):
        part = dot_nt(wide, w_in[at, :])
        one_side = (part * gain[:, at]).astype(BF16)
        other = (part * (normed[:, at].astype(F32) - bias[:, at])).astype(BF16)
        totals.append(dot_nt(first, one_side) + dot_nt(second, other))
        return part

    emit(rank, product, parts)
    stats[...] = totals[0] + totals[1] + totals[2] + totals[3]


def product_kernel(which, left, right, out):
    out[...] = dot_tn(left[...], right[...]).astype(BF16)


def join_kernel(meta, p0, p1, p2, p3a, p3b, whole):
    half = LANES // 2
    for r, piece in enumerate((p0, p1, p2)):
        whole[:, pl.ds(pl.multiple_of((meta[0] ^ r) * LANES, LANES), LANES)] = piece[...]
    at = pl.multiple_of((meta[0] ^ 3) * LANES, LANES)
    whole[:, pl.ds(at, half)] = p3a[...]
    whole[:, pl.ds(pl.multiple_of(at + half, half), half)] = p3b[...]


def partial_outs(rows, phased, row_of):
    half = LANES // 2
    if not phased:
        shapes = [jax.ShapeDtypeStruct((rows, LANES), F32)] + [jax.ShapeDtypeStruct((rows, LANES), BF16)] * 3
        return shapes, [pl.BlockSpec((TILE, LANES), lambda *i: (row_of(*i), 0))] * 4
    shapes = [jax.ShapeDtypeStruct((2, rows, half), BF16)] * 2 + [
        jax.ShapeDtypeStruct((rows, LANES), F32), jax.ShapeDtypeStruct((rows, half), F32),
        jax.ShapeDtypeStruct((rows, half), F32)]
    specs = [pl.BlockSpec((2, TILE, half), lambda *i: (0, row_of(*i), 0))] * 2 + [
        pl.BlockSpec((TILE, width), lambda *i: (row_of(*i), 0)) for width in (LANES, half, half)]
    return shapes, specs


def fixed(shape):
    return pl.BlockSpec(shape, lambda *i: (0,) * len(shape))


def outside(count):
    return [pl.BlockSpec(memory_space=pl.ANY)] * count


def params(size):
    return pltpu.CompilerParams(dimension_semantics=("arbitrary",), vmem_limit_bytes=size << 20)


def weight_scratch(width):
    return [pltpu.VMEM((width, 3 * LANES + width), BF16), pltpu.VMEM((LANES + width, width), BF16),
            pltpu.SemaphoreType.DMA((6,))]


def forward_layer(meta, lens, pieces, weights, tables, length, first_row, phased, carry=None):
    rows = pieces[0].shape[0]
    tiles, before = rows // TILE, first_row // TILE
    half, width = LANES // 2, 4 * LANES
    local = lambda t, *_: t
    there = lambda t, *_: before + t
    by_row = lambda n, row_of: pl.BlockSpec((TILE, n), lambda *i: (row_of(*i), 0))
    (gain, bias, mix_hi, mix_lo, feat_w), mine, other = weights
    small = (gain, bias, mix_hi, mix_lo, feat_w)
    shapes, specs = partial_outs(rows, phased, local)
    extra = [(width, BF16), (LANES, F32), (half, F32)] + [(LANES, BF16)] * 5 + [
        (LANES + width, BF16), (width, BF16), (LANES, F32), (LANES, F32)]
    shapes += [jax.ShapeDtypeStruct((length, n), d) for n, d in extra]
    specs += [by_row(n, there) for n, _ in extra]
    shapes += [jax.ShapeDtypeStruct((length // TILE, LANES, LANES), F32), jax.ShapeDtypeStruct((length // TILE, 8, LANES), F32)]
    specs += [pl.BlockSpec((1, n, LANES), lambda *i: (there(*i), 0, 0)) for n in (LANES, 8)]
    states = [(LANES, LANES), (8, LANES)]
    shapes += [jax.ShapeDtypeStruct(s, F32) for s in states]
    specs += [fixed(s) for s in states]
    operands = [meta, jnp.stack([lens[0], jnp.int32(first_row)]), *pieces, *small, *tables, *mine, *other]
    in_specs = [by_row(p.shape[1], local) for p in pieces] + [fixed(w.shape) for w in small] + [by_row(half, there)] * 2 + outside(8)
    aliases = {}
    if carry is not None:
        state, saved = carry
        operands += [*state, *saved]
        in_specs += [fixed(s) for s in states] + outside(SAVED)
        aliases = {len(operands) - SAVED + i: len(shapes) - 2 - SAVED + i for i in range(SAVED)}
    outs = pl.pallas_call(
        functools.partial(forward_kernel, carry is not None, phased),
        name="layer_forward",
        out_shape=shapes,
        grid_spec=pltpu.PrefetchScalarGridSpec(
            num_scalar_prefetch=2, grid=(tiles,), in_specs=in_specs, out_specs=specs, scratch_shapes=weight_scratch(width)),
        input_output_aliases=aliases,
        compiler_params=params(56),
        cost_estimate=pl.CostEstimate(flops=rows * 20_000_000, transcendentals=rows * 5000, bytes_accessed=24 << 20),
    )(*operands)
    count = 5 if phased else 4
    return outs[:count], outs[count:count + SAVED], outs[count + SAVED:]


def backward_layer(meta, grad, saved, weights, tables, length, first_row, phased, carry=None):
    rows = grad.shape[0]
    tiles, before = rows // TILE, first_row // TILE
    half, width = LANES // 2, 4 * LANES
    local = lambda t, *_: tiles - 1 - t
    there = lambda t, *_: before + tiles - 1 - t
    by_row = lambda n, row_of=there: pl.BlockSpec((TILE, n), lambda *i: (row_of(*i), 0))
    normed, rq, rk, qf, kf, value, hcat, dgelu, invz, attended, prior_s, prior_k = saved
    (gain, bias, mix_hi, mix_lo, feat_w), mine, other = weights
    shapes, specs = partial_outs(rows, phased, local)
    shapes += [jax.ShapeDtypeStruct((8, length), F32), jax.ShapeDtypeStruct((length, 3 * LANES + width), BF16)]
    specs += [pl.BlockSpec((8, TILE), lambda *i: (0, there(*i))), by_row(3 * LANES + width)]
    states = [(LANES, LANES), (8, LANES)] * 2
    shapes += [jax.ShapeDtypeStruct(s, F32) for s in states]
    specs += [fixed(s) for s in states]
    operands = [meta, grad, normed, rq, rk, qf, kf, value, attended, dgelu, invz, prior_s, prior_k, gain, bias, mix_hi, *tables,
                *mine, *other]
    in_specs = [by_row(width, local), by_row(width)] + [by_row(LANES)] * 6 + [by_row(width), by_row(LANES)] + [
        pl.BlockSpec((1, n, LANES), lambda *i: (there(*i), 0, 0)) for n in (LANES, 8)] + [
        fixed(w.shape) for w in (gain, bias, mix_hi)] + [by_row(half)] * 2 + outside(8)
    aliases = {}
    if carry is not None:
        state, arrays = carry
        operands += [*state, *arrays]
        in_specs += [fixed(s) for s in states] + outside(2)
        aliases = {len(operands) - 2 + i: len(shapes) - 6 + i for i in range(2)}
    outs = pl.pallas_call(
        functools.partial(backward_kernel, carry is not None, phased),
        name="layer_backward",
        out_shape=shapes,
        grid_spec=pltpu.PrefetchScalarGridSpec(
            num_scalar_prefetch=1, grid=(tiles,), in_specs=in_specs, out_specs=specs, scratch_shapes=weight_scratch(width)),
        input_output_aliases=aliases,
        compiler_params=params(56),
        cost_estimate=pl.CostEstimate(flops=rows * 25_000_000, transcendentals=0, bytes_accessed=24 << 20),
    )(*operands)
    count = 5 if phased else 4
    return outs[:count], outs[count:count + 2], outs[count + 2:]


def join(meta, pieces):
    rows, block = pieces[0].shape[0], 2 * TILE
    return pl.pallas_call(
        join_kernel,
        name="join",
        out_shape=jax.ShapeDtypeStruct((rows, 4 * LANES), BF16),
        grid_spec=pltpu.PrefetchScalarGridSpec(
            num_scalar_prefetch=1,
            grid=(rows // block,),
            in_specs=[pl.BlockSpec((block, p.shape[1]), lambda i, *_: (i, 0)) for p in pieces],
            out_specs=pl.BlockSpec((block, 4 * LANES), lambda i, *_: (i, 0)),
        ),
        compiler_params=params(8),
        cost_estimate=pl.CostEstimate(flops=0, transcendentals=0, bytes_accessed=rows * 16 * LANES),
    )(meta, *pieces)


def swap(value, axis, by):
    return lax.ppermute(value, axis, [(k, k ^ by) for k in range(lax.axis_size(axis))])


def gather_pieces(shard, meanwhile=()):
    half = shard.shape[1] // 2
    from_x, from_y = after((swap(shard, "mp", 1), swap(shard, "mp", 2)), *meanwhile)
    return shard, from_x, from_y, swap(from_x[:, :half], "mp", 2), swap(from_y[:, half:], "mp", 1)


def after(values, *others):
    if not others:
        return values
    return lax.optimization_barrier((values, others))[0]


def direct_sends(parts):
    return parts[0], [swap(part, "mp", r) for r, part in enumerate(parts) if r > 0]


def scatter_start(parts):
    return swap(parts[0], "mp", 1), swap(parts[1], "mp", 2)


def scatter_turn(parts, arrived):
    _, _, _, ka, kb = parts
    in_x, in_y = arrived
    return (ka + in_x[1].astype(F32)).astype(BF16), (kb + in_y[1].astype(F32)).astype(BF16)


def scatter_end(parts, arrived, to_y, to_x):
    _, _, k0, ka, _ = parts
    in_x, in_y = arrived
    half = ka.shape[1]
    last_y, last_x = swap(to_y, "mp", 2), swap(to_x, "mp", 1)
    return jnp.concatenate(
        [k0[:, :half] + in_x[0].astype(F32) + last_y.astype(F32), k0[:, half:] + in_y[0].astype(F32) + last_x.astype(F32)],
        axis=1)


def scatter_sum(parts):
    arrived = scatter_start(parts)
    return scatter_end(parts, arrived, *scatter_turn(parts, arrived))


def mp_total(values):
    return values + swap(values, "mp", 1) + swap(values, "mp", 2) + swap(values, "mp", 3)


def ring_scatter(block_of, axis, meanwhile=()):
    count = lax.axis_size(axis)
    rank = lax.axis_index(axis)
    pairs = [(k, (k + 1) % count) for k in range(count)]
    total = block_of((rank + count - 1) % count)
    for step in range(2, count + 1):
        arrived = after(lax.ppermute(total, axis, pairs), *meanwhile)
        total = (arrived.astype(F32) + block_of((rank + count - step) % count).astype(F32)).astype(BF16)
        yield arrived, total


def dp_total(values):
    count = lax.axis_size("dp")
    if count > 8:
        return lax.psum(values, "dp")
    sent = [lax.ppermute(values, "dp", [(i, (i + k) % count) for i in range(count)]) for k in range(1, count)]
    return sum(sent, values)


def block_sends(block_of, axis):
    count = lax.axis_size(axis)
    rank = lax.axis_index(axis)
    if count > 8:
        return [list(ring_scatter(block_of, axis))[-1][1]]
    return [block_of(rank)] + [
        lax.ppermute(block_of((rank + k) % count), axis, [(i, (i + k) % count) for i in range(count)]) for k in range(1, count)]


def sum_blocks(blocks):
    total = blocks[0].astype(F32)
    for block in blocks[1:]:
        total = total + block.astype(F32)
    return total.astype(BF16)


def weight_gradient(left, right, cut_left, section):
    rows = left.shape[0]
    m, n = left.shape[1] // (2 if cut_left else 1), right.shape[1] // (1 if cut_left else 2)
    block = 128 if cut_left else 256
    steps = m // block
    left_at = (lambda i, which: (0, which[0] * steps + i)) if cut_left else (lambda i, which: (0, i))
    right_at = (lambda i, which: (0, 0)) if cut_left else (lambda i, which: (0, which[0]))

    def product(which):
        return pl.pallas_call(
            product_kernel,
            name="weight_gradient",
            out_shape=jax.ShapeDtypeStruct((m, n), BF16),
            grid_spec=pltpu.PrefetchScalarGridSpec(
                num_scalar_prefetch=1, grid=(steps,),
                in_specs=[pl.BlockSpec((rows, block), left_at), pl.BlockSpec((rows, n), right_at)],
                out_specs=pl.BlockSpec((block, n), lambda i, which: (i, 0))),
            compiler_params=params(58),
            cost_estimate=pl.CostEstimate(flops=2 * rows * m * n, transcendentals=0, bytes_accessed=2 * (rows * (m + n) + m * n)),
        )(which.reshape(1).astype(jnp.int32), left, right)

    arrived = swap(product(1 - section), "section", 1)
    return product(section), arrived


def dct_table(order):
    row_index = jnp.arange(order, dtype=F32)[:, None]
    col_index = jnp.arange(order, dtype=F32)[None, :]
    cosines = jnp.sqrt(2.0 / order) * jnp.cos(math.pi * (row_index + 0.5) * col_index / order)
    return cosines * jnp.where(col_index == 0, math.sqrt(0.5), 1.0)


def rotary_tables(length):
    column = jnp.arange(LANES // 2, dtype=jnp.int32) % HEAD
    half = ROT // 2
    index = (column % half).astype(F32)
    angles = jnp.arange(length, dtype=F32)[:, None] * (10000.0 ** (-index * 2.0 / ROT))[None, :]
    turned = (column < ROT)[None, :]
    sign = jnp.where(column < half, -1.0, 1.0)[None, :]
    return jnp.where(turned, jnp.cos(angles), 1.0), jnp.where(turned, sign * jnp.sin(angles), 0.0)


def shards(block_input, cotangent, lengths, ln_gain, ln_bias, w_qkv, w_out, w_up, w_down, freq_table, feat_weight):
    section = lax.axis_index("section")
    place = lax.axis_index("mp")
    group = lax.axis_index("dp")
    groups = lax.axis_size("dp")
    local_slots, length, shard_width = block_input.shape
    width = ln_gain.shape[1]
    heads = freq_table.shape[1]
    is_first = section == 0
    lens = lax.dynamic_slice_in_dim(lengths, section, 1, 0)
    metas = [jnp.stack([place, (section == l).astype(jnp.int32)]).astype(jnp.int32) for l in range(2)]

    def own(values):
        return lax.dynamic_index_in_dim(values, section, 0, keepdims=False)

    shard0 = own(block_input)
    pieces0 = gather_pieces(shard0)

    small = jnp.concatenate([ln_gain[0], ln_bias[0], feat_weight.reshape(-1), freq_table.astype(F32).reshape(-1)])
    small_other = swap(small, "section", 1)
    mine = (w_qkv, w_up, w_out, w_down)
    other = tuple(swap(w, "section", 1) for w in mine)

    def both(mine, other):
        return jnp.where(is_first, mine, other), jnp.where(is_first, other, mine)

    layers_small = both(small, small_other)
    table = dct_table(HEAD)
    eye = jnp.eye(heads, dtype=F32)

    def layer_weights(l):
        vec = layers_small[l]
        gain, bias = vec[:width].reshape(1, width), vec[width:2 * width].reshape(1, width)
        feat = vec[2 * width:2 * width + LANES].reshape(1, LANES)
        freq = vec[2 * width + LANES:].reshape(heads, HEAD, HEAD)
        mixed = jnp.einsum("nk,hkm->hnm", table, freq, precision=lax.Precision.HIGHEST)
        mixed = (eye[:, None, :, None] * mixed[:, :, None, :]).reshape(LANES, LANES)
        high = lax.reduce_precision(mixed, 8, 7)
        return (gain, bias, high.astype(BF16), (mixed - high).astype(BF16), feat), mine, other

    weights0, weights1 = layer_weights(0), layer_weights(1)
    tables = rotary_tables(length)

    cot = after(own(cotangent), pieces0[3], pieces0[4])
    cot_x, cot_y = swap(cot, "mp", 1), swap(cot, "mp", 2)
    part0, all0, _ = forward_layer(metas[0], lens, pieces0, weights0, tables, length, 0, True)
    part0 = after(part0, cot_x, cot_y)
    hidden = (shard0.astype(F32) + scatter_sum(part0)).astype(BF16)
    pieces1 = gather_pieces(hidden)
    cot_x, cot_y = after((cot_x, cot_y), pieces1[3], pieces1[4])
    half = shard_width // 2
    pieces_g = cot, cot_x, cot_y, swap(cot_x[:, :half], "mp", 2), swap(cot_y[:, half:], "mp", 1)
    part1, all1, _ = forward_layer(metas[1], lens, pieces1, weights1, tables, length, 0, False)
    out_kept, out_sent = direct_sends(part1)

    def saved_of(arrays):
        return (arrays[0],) + tuple(arrays[3:])

    def in_block(mine, arrived):
        n = mine.shape[0] // groups
        cut = lambda v, i: lax.dynamic_slice_in_dim(v, i * n, n, 0)
        return lambda i: (cut(mine, i).astype(F32) + cut(arrived, i).astype(F32)).astype(BF16)

    def out_block(mine, arrived):
        n = mine.shape[1] // groups
        cut = lambda v, i: lax.dynamic_slice_in_dim(v, i * n, n, 1)
        return lambda i: (cut(mine, i).astype(F32) + cut(arrived, i).astype(F32)).astype(BF16)

    def run_backward(meta, grad, saved, weights, phased):
        parts, (stats, dcat), (_, _, dmix, fsum) = backward_layer(meta, grad, saved, weights, tables, length, 0, phased)
        return parts, stats, dcat, dmix, fsum

    def norm_backward(grad_shard, d_normed, sums, norm, gain_all):
        xhat, rstd = norm
        gain = lax.dynamic_slice_in_dim(gain_all, place * shard_width, shard_width, 1)
        mean_d = (sums[0] * (1.0 / width))[:, None]
        mean_dx = (sums[1] * (1.0 / width))[:, None]
        return grad_shard.astype(F32) + rstd[:, :1] * (d_normed * gain - mean_d - xhat * mean_dx)

    def small_gradients(d_normed, norm, dmix, fsum):
        gain_part = jnp.sum(d_normed * norm[0], axis=0)
        bias_part = jnp.sum(d_normed, axis=0)
        diagonal = jnp.stack([dmix[h * HEAD:(h + 1) * HEAD, h * HEAD:(h + 1) * HEAD] for h in range(heads)])
        return jnp.concatenate([gain_part, bias_part, fsum[0], diagonal.reshape(-1)])

    saved1, saved0 = saved_of(all1), saved_of(all0)
    grad1 = join(metas[1], pieces_g)
    out_blocks1 = block_sends(out_block(*weight_gradient(saved1[6], grad1, True, section)), "dp")
    grad1_b = after(grad1, out_blocks1[0])
    parts, stats, dcat1, dmix1, fsum1 = run_backward(metas[1], grad1_b, saved1, weights1, True)
    parts, stats, dcat1, dmix1, fsum1 = after((parts, stats, dcat1, dmix1, fsum1), *out_blocks1, *out_sent)
    arrived = scatter_start(parts)
    turn = scatter_turn(parts, arrived)
    steps1 = list(ring_scatter(in_block(*weight_gradient(saved1[0], dcat1, False, section)), "dp"))
    arrivals1, red_in1 = [arrival for arrival, _ in steps1], steps1[-1][1]
    d_normed = scatter_end(parts, arrived, *turn)
    sums = mp_total(after(stats, *turn))
    g0 = norm_backward(cot, d_normed, sums, all1[1:3], weights1[0][0]).astype(BF16)
    small1 = small_gradients(d_normed, all1[1:3], dmix1, fsum1)
    pieces_g0 = gather_pieces(after(g0, arrivals1[0]), arrivals1[1:2])
    pieces_g0 = after(pieces_g0, *arrivals1[2:3])
    out = hidden.astype(F32) + out_kept + out_sent[0].astype(F32) + out_sent[1].astype(F32) + out_sent[2].astype(F32)

    grad0 = join(metas[0], pieces_g0)
    out_blocks0 = block_sends(out_block(*weight_gradient(saved0[6], grad0, True, section)), "dp")
    grad0_b = after(grad0, out_blocks0[0])
    parts, stats, dcat0, dmix0, fsum0 = run_backward(metas[0], grad0_b, saved0, weights0, False)
    parts, stats, dcat0, dmix0, fsum0 = after((parts, stats, dcat0, dmix0, fsum0), *out_blocks0)
    out_blocks1 = after(out_blocks1, dcat0)
    kept, sent = direct_sends(parts)
    mine0, arrived0 = weight_gradient(saved0[0], dcat0, False, section)
    block0 = in_block(mine0, arrived0)
    steps0 = list(ring_scatter(block0, "dp", sent))
    sums = mp_total(after(stats, steps0[0][0]))
    sent, dmix0, out_blocks0, out_blocks1 = after((sent, dmix0, out_blocks0, out_blocks1), steps0[0][0])
    d_normed = kept + sent[0].astype(F32) + sent[1].astype(F32) + sent[2].astype(F32)
    d_input = norm_backward(g0, d_normed, sums, all0[1:3], weights0[0][0])
    small0 = small_gradients(d_normed, all0[1:3], dmix0, fsum0)

    def to_owner(first, second, axis):
        mine, other = both(first, second)
        arrived = swap(other, "section", 1)
        return jnp.where(is_first, jnp.concatenate([mine, arrived], axis), jnp.concatenate([arrived, mine], axis)).astype(F32)

    grads_out = to_owner(sum_blocks(out_blocks0), sum_blocks(out_blocks1), 0)
    small_mine, small_send = both(small0, small1)
    small_sum = dp_total(small_mine + swap(small_send, "section", 1))
    feat_grad = small_sum[2 * shard_width:2 * shard_width + LANES].reshape(heads, HEAD) / feat_weight[0]
    freq_grad = jnp.einsum("nk,hnm->hkm", table, small_sum[2 * shard_width + LANES:].reshape(heads, HEAD, HEAD),
                           precision=lax.Precision.HIGHEST)
    keep, send = both(d_input, out)
    arrived = swap(send, "section", 1)
    boundary = jnp.where(is_first, jnp.stack([keep, arrived]), jnp.stack([arrived, keep]))
    grads_in = to_owner(steps0[-1][1], red_in1, 1)
    qkv_grad = jnp.stack([grads_in[:, t * shard_width:(t + 1) * shard_width] for t in range(3)])
    return (
        boundary[None],
        small_sum[None, :shard_width],
        small_sum[None, shard_width:2 * shard_width],
        qkv_grad[None],
        grads_out[None, :shard_width],
        grads_in[None, :, 3 * shard_width:],
        grads_out[None, shard_width:],
        freq_grad[None],
        feat_grad[None],
    )


def solution(mesh):
    placed = (
        P("dp", None, "mp"), P("dp", None, "mp"), P("dp"), P("section", None), P("section", None),
        P("section", None, None, "mp"), P("section", "mp", None), P("section", None, "mp"), P("section", "mp", None),
        P("section", "mp", None, None), P("section", "mp", None),
    )
    return jax.shard_map(
        shards,
        mesh=mesh,
        in_specs=placed,
        out_specs=(
            P("section", "dp", None, "mp"), P("section", "mp"), P("section", "mp"), P("section", None, "dp", "mp"),
            P("section", "mp", "dp"), P("section", "dp", "mp"), P("section", "mp", "dp"), P("section", "mp", None, None),
            P("section", "mp", None),
        ),
        check_vma=False,
    )
```

profile of v0, /device:TPU:0, one launch (start us, length us, event | category | flops | bytes accessed | tf_op | source)
XLA Modules:
  0.0 383.6 jit_solution(8530951143142603262)
XLA Ops:
  1.9 3.1 collective-permute-start.2
  10.8 2.9 multiply_select_fusion
  20.7 4.0 %collective-permute-done.3.refs_6_ = bf16[1024,128]{1,0:T(8,128)(2,1)} collective-permute-done((bf16[1024,128]{1,0:T(8,128)(2,1)S(1)}, bf16[1024,128]{1,0:T(8,128)(2,1)}, u32[]{:S(2)}, u32[]{:S(2)}) %collective-permute-start.3) | collective-permute-done | bytes 262176 | tf_op jit(solution)/shard_map/ppermute | solution.py:458
  28.4 3.0 collective-permute-done.1.refs_5_
  34.1 22.5 %layer_forward.2 = (bf16[2,1024,128]{2,1,0:T(8,128)(2,1)}, bf16[2,1024,128]{2,1,0:T(8,128)(2,1)}, f32[1024,256]{1,0:T(8,128)}, f32[1024,128]{1,0:T(8,128)}, f32[...) custom-call(s32[2]{0:T(128)} %get-tuple-element.308.refs_0_.meta, ...), custom_call_target="tpu_custom_call" | custom-call | flops 20480000000 | bytes 25165824 | tf_op jit(solution)/shard_map/layer_forward/pallas_call | solution.py:386
  58.1 9.4 %collective-permute-done.11 = bf16[2,1024,128]{2,1,0:T(8,128)(2,1)S(1)} collective-permute-done((bf16[2,1024,128]{2,1,0:T(8,128)(2,1)}, bf16[2,1024,128]{2,1,0:T(8,128)(2,1)S(1)}, u32[]{:S(2)}, u32[]{:S(2)}) %collective-permute-start.11) | collective-permute-done | bytes 524320 | tf_op jit(solution)/shard_map/ppermute | solution.py:458
  71.8 4.0 %collective-permute-done.12 = bf16[1024,128]{1,0:T(8,128)(2,1)S(1)} collective-permute-done((bf16[1024,128]{1,0:T(8,128)(2,1)S(1)}, bf16[1024,128]{1,0:T(8,128)(2,1)S(1)}, u32[]{:S(2)}, u32[]{:S(2)}) %collective-permute-start.12) | collective-permute-done | bytes 262176 | tf_op jit(solution)/shard_map/ppermute | solution.py:458
  78.1 2.6 collective-permute-start.16
  80.7 9.2 %collective-permute-done.16.refs_4_ = bf16[1024,256]{1,0:T(8,128)(2,1)} collective-permute-done((bf16[1024,256]{1,0:T(8,128)(2,1)S(1)}, bf16[1024,256]{1,0:T(8,128)(2,1)}, u32[]{:S(2)}, u32[]{:S(2)}) %collective-permute-start.16) | collective-permute-done | bytes 524320 | tf_op jit(solution)/shard_map/ppermute | solution.py:458
  97.0 2.6 collective-permute-done.18.refs_6_
  103.3 22.1 %layer_forward.3 = (f32[1024,256]{1,0:T(8,128)}, bf16[1024,256]{1,0:T(8,128)(2,1)}, bf16[1024,256]{1,0:T(8,128)(2,1)}, bf16[1024,256]{1,0:T(8,128)(2,1)}, bf16[1...) custom-call(s32[2]{0:T(128)} %pad_add_fusion.refs_0_.meta, ...), custom_call_target="tpu_custom_call" | custom-call | flops 20480000000 | bytes 25165824 | tf_op jit(solution)/shard_map/layer_forward/pallas_call | solution.py:386
  127.7 6.0 %weight_gradient.9 = bf16[640,1024]{1,0:T(8,128)(2,1)} custom-call(s32[1]{0:T(128)} %bitcast.21.which, bf16[1024,1280]{1,0:T(8,128)(2,1)} %get-tuple-element.133.left, bf16[1024,1024]{1,0:T(8,128)(2,1)} %copy-done.2), custom_call_target="tpu_custom_call" | custom-call | flops 1342177280 | bytes 4718592 | tf_op jit(solution)/shard_map/weight_gradient/pallas_call | solution.py:550
  137.2 6.0 %weight_gradient.8 = bf16[640,1024]{1,0:T(8,128)(2,1)} custom-call(s32[1]{0:T(128)} %bitcast.20.which, bf16[1024,1280]{1,0:T(8,128)(2,1)} %get-tuple-element.133.left, bf16[1024,1024]{1,0:T(8,128)(2,1)} %copy-done.2), custom_call_target="tpu_custom_call" | custom-call | flops 1342177280 | bytes 4718592 | tf_op jit(solution)/shard_map/weight_gradient/pallas_call | solution.py:550
  143.1 2.5 add_convert_fusion.21
  145.7 3.6 collective-permute-start.24
  150.3 26.6 %layer_backward.2 = (bf16[2,1024,128]{2,1,0:T(8,128)(2,1)}, bf16[2,1024,128]{2,1,0:T(8,128)(2,1)}, f32[1024,256]{1,0:T(8,128)}, f32[1024,128]{1,0:T(8,128)}, f32...) custom-call(s32[2]{0:T(128)} %pad_add_fusion.refs_0_.meta, ...), custom_call_target="tpu_custom_call" | custom-call | flops 25600000000 | bytes 25165824 | tf_op jit(solution)/shard_map/layer_backward/pallas_call | solution.py:426
  178.5 6.0 %weight_gradient.11 = bf16[1024,896]{1,0:T(8,128)(2,1)} custom-call(s32[1]{0:T(128)} %bitcast.21.which, bf16[1024,1024]{1,0:T(8,128)(2,1)} %get-tuple-element.135.refs_2_.left, bf16[1024,1792]{1,0:T(8,128)(2,1)} %get-tuple-element.167.right), custom_call_target="tpu_custom_call" | custom-call | flops 1879048192 | bytes 5767168 | tf_op jit(solution)/shard_map/weight_gradient/pallas_call | solution.py:550
  187.3 6.1 %weight_gradient.10 = bf16[1024,896]{1,0:T(8,128)(2,1)} custom-call(s32[1]{0:T(128)} %bitcast.20.which, bf16[1024,1024]{1,0:T(8,128)(2,1)} %get-tuple-element.135.refs_2_.left, bf16[1024,1792]{1,0:T(8,128)(2,1)} %get-tuple-element.167.right), custom_call_target="tpu_custom_call" | custom-call | flops 1879048192 | bytes 5767168 | tf_op jit(solution)/shard_map/weight_gradient/pallas_call | solution.py:550
  193.4 5.7 %collective-permute-done.28 = bf16[2,1024,128]{2,1,0:T(8,128)(2,1)S(1)} collective-permute-done((bf16[2,1024,128]{2,1,0:T(8,128)(2,1)}, bf16[2,1024,128]{2,1,0:T(8,128)(2,1)S(1)}, u32[]{:S(2)}, u32[]{:S(2)}) %collective-permute-start.28) | collective-permute-done | bytes 524320 | tf_op jit(solution)/shard_map/ppermute | solution.py:458
  209.8 8.3 %collective-permute-done.36 = bf16[256,896]{1,0:T(8,128)(2,1)S(1)} collective-permute-done((bf16[256,896]{1,0:T(8,128)(2,1)S(1)}, bf16[256,896]{1,0:T(8,128)(2,1)S(1)}, u32[]{:S(2)}, u32[]{:S(2)}) %collective-permute-start.36) | collective-permute-done | bytes 458784 | tf_op jit(solution)/shard_map/ppermute | solution.py:512
  223.5 7.9 %collective-permute-done.39 = bf16[256,896]{1,0:T(8,128)(2,1)S(1)} collective-permute-done((bf16[256,896]{1,0:T(8,128)(2,1)S(1)}, bf16[256,896]{1,0:T(8,128)(2,1)S(1)}, u32[]{:S(2)}, u32[]{:S(2)}) %collective-permute-start.39) | collective-permute-done | bytes 458784 | tf_op jit(solution)/shard_map/ppermute | solution.py:512
  237.1 4.0 %collective-permute-done.41.p3b = bf16[1024,128]{1,0:T(8,128)(2,1)S(1)} collective-permute-done((bf16[1024,128]{1,0:T(8,128)(2,1)S(1)}, bf16[1024,128]{1,0:T(8,128)(2,1)S(1)}, u32[]{:S(2)}, u32[]{:S(2)}) %collective-permute-start.41) | collective-permute-done | bytes 262176 | tf_op jit(solution)/shard_map/ppermute | solution.py:458
  246.2 6.0 %weight_gradient.13 = bf16[640,1024]{1,0:T(8,128)(2,1)} custom-call(s32[1]{0:T(128)} %bitcast.21.which, bf16[1024,1280]{1,0:T(8,128)(2,1)} %get-tuple-element.176.left, bf16[1024,1024]{1,0:T(8,128)(2,1)} %copy-done.3), custom_call_target="tpu_custom_call" | custom-call | flops 1342177280 | bytes 4718592 | tf_op jit(solution)/shard_map/weight_gradient/pallas_call | solution.py:550
  252.1 6.0 %weight_gradient.12 = bf16[640,1024]{1,0:T(8,128)(2,1)} custom-call(s32[1]{0:T(128)} %bitcast.20.which, bf16[1024,1280]{1,0:T(8,128)(2,1)} %get-tuple-element.176.left, bf16[1024,1024]{1,0:T(8,128)(2,1)} %copy-done.3), custom_call_target="tpu_custom_call" | custom-call | flops 1342177280 | bytes 4718592 | tf_op jit(solution)/shard_map/weight_gradient/pallas_call | solution.py:550
  262.0 26.2 %layer_backward.3 = (f32[1024,256]{1,0:T(8,128)}, bf16[1024,256]{1,0:T(8,128)(2,1)}, bf16[1024,256]{1,0:T(8,128)(2,1)}, bf16[1024,256]{1,0:T(8,128)(2,1)}, f32[8...) custom-call(s32[2]{0:T(128)} %get-tuple-element.308.refs_0_.meta, ...), custom_call_target="tpu_custom_call" | custom-call | flops 25600000000 | bytes 25165824 | tf_op jit(solution)/shard_map/layer_backward/pallas_call | solution.py:426
  290.1 6.0 %weight_gradient.15 = bf16[1024,896]{1,0:T(8,128)(2,1)} custom-call(s32[1]{0:T(128)} %bitcast.21.which, bf16[1024,1024]{1,0:T(8,128)(2,1)} %get-tuple-element.178.refs_2_.left, bf16[1024,1792]{1,0:T(8,128)(2,1)} %get-tuple-element.202.right), custom_call_target="tpu_custom_call" | custom-call | flops 1879048192 | bytes 5767168 | tf_op jit(solution)/shard_map/weight_gradient/pallas_call | solution.py:550
  301.0 6.0 %weight_gradient.14 = bf16[1024,896]{1,0:T(8,128)(2,1)} custom-call(s32[1]{0:T(128)} %bitcast.20.which, bf16[1024,1024]{1,0:T(8,128)(2,1)} %get-tuple-element.178.refs_2_.left, bf16[1024,1792]{1,0:T(8,128)(2,1)} %get-tuple-element.202.right), custom_call_target="tpu_custom_call" | custom-call | flops 1879048192 | bytes 5767168 | tf_op jit(solution)/shard_map/weight_gradient/pallas_call | solution.py:550
  313.2 9.6 %collective-permute-done.48 = bf16[1024,256]{1,0:T(8,128)(2,1)} collective-permute-done((bf16[1024,256]{1,0:T(8,128)(2,1)}, bf16[1024,256]{1,0:T(8,128)(2,1)}, u32[]{:S(2)}, u32[]{:S(2)}) %collective-permute-start.48) | collective-permute-done | bytes 524320 | tf_op jit(solution)/shard_map/ppermute | solution.py:458
  344.4 7.9 %collective-permute-done.59 = f32[17152]{0:T(1024)S(1)} collective-permute-done((f32[17152]{0:T(1024)S(1)}, f32[17152]{0:T(1024)S(1)}, u32[]{:S(2)}, u32[]{:S(2)}) %collective-permute-start.59) | collective-permute-done | bytes 68640 | tf_op jit(solution)/shard_map/ppermute | solution.py:521
  352.4 4.4 %collective-permute-done.58 = f32[17152]{0:T(1024)S(1)} collective-permute-done((f32[17152]{0:T(1024)S(1)}, f32[17152]{0:T(1024)S(1)}, u32[]{:S(2)}, u32[]{:S(2)}) %collective-permute-start.58) | collective-permute-done | bytes 68640 | tf_op jit(solution)/shard_map/ppermute | solution.py:521
  362.2 12.4 %collective-permute-done.61 = bf16[256,896]{1,0:T(8,128)(2,1)S(1)} collective-permute-done((bf16[256,896]{1,0:T(8,128)(2,1)S(1)}, bf16[256,896]{1,0:T(8,128)(2,1)S(1)}, u32[]{:S(2)}, u32[]{:S(2)}) %collective-permute-start.61) | collective-permute-done | bytes 458784 | tf_op jit(solution)/shard_map/ppermute | solution.py:512
  378.2 3.1 maximum_select_fusion
  (324 shorter events, 126.4 us)
Async XLA Ops:
  1.9 15.0 %collective-permute-start.2 = (bf16[1024,256]{1,0:T(8,128)(2,1)S(1)}, bf16[1024,256]{1,0:T(8,128)(2,1)S(1)}, u32[]{:S(2)}, u32[]{:S(2)}) collective-permute-start(bf16[1024,256]{1,0:T(8,128)(2,1)S(1)} %dynamic-slice_bitcast_fusion.refs_2_), channel_id=1, source_target_pairs={{0,2},{1,3},{2,0},{3,1},{4,6},{5,7},{6,4},{7,5},{8,10},{9,11},{10,... | collective-permute-start | bytes 1572872 | tf_op jit(solution)/shard_map/ppermute | solution.py:458
  4.9 14.4 %collective-permute-start = (bf16[1024,256]{1,0:T(8,128)(2,1)S(1)}, bf16[1024,256]{1,0:T(8,128)(2,1)}, u32[]{:S(2)}, u32[]{:S(2)}) collective-permute-start(bf16[1024,256]{1,0:T(8,128)(2,1)S(1)} %dynamic-slice_bitcast_fusion.refs_2_), channel_id=1, source_target_pairs={{0,1},{1,0},{2,3},{3,2},{4,5},{5,4},{6,7},{7,6},{8,9},{9,8},{10,11... | collective-permute-start | bytes 1572872 | tf_op jit(solution)/shard_map/ppermute | solution.py:458
  8.9 25.2 %collective-permute-start.6 = (bf16[1,1024,1024]{2,1,0:T(8,128)(2,1)}, bf16[1,1024,1024]{2,1,0:T(8,128)(2,1)}, u32[]{:S(2)}, u32[]{:S(2)}) collective-permute-start(bf16[1,1024,1024]{2,1,0:T(8,128)(2,1)} %refs_19_.3), channel_id=1, source_target_pairs={{0,16},{16,0},{1,17},{17,1},{2,18},{18,2},{3,19},{19,3},{4,20},{20... | collective-permute-start | bytes 6291464 | tf_op jit(solution)/shard_map/ppermute | solution.py:458
  9.4 24.7 %collective-permute-start.8 = (bf16[1,1024,1024]{2,1,0:T(8,128)(2,1)}, bf16[1,1024,1024]{2,1,0:T(8,128)(2,1)}, u32[]{:S(2)}, u32[]{:S(2)}) collective-permute-start(bf16[1,1024,1024]{2,1,0:T(8,128)(2,1)} %refs_21_.3), channel_id=1, source_target_pairs={{0,16},{16,0},{1,17},{17,1},{2,18},{18,2},{3,19},{19,3},{4,20},{20... | collective-permute-start | bytes 6291464 | tf_op jit(solution)/shard_map/ppermute | solution.py:458
  14.9 19.1 %collective-permute-start.5 = (bf16[1,3,1024,256]{3,2,1,0:T(8,128)(2,1)}, bf16[1,3,1024,256]{3,2,1,0:T(8,128)(2,1)}, u32[]{:S(2)}, u32[]{:S(2)}) collective-permute-start(bf16[1,3,1024,256]{3,2,1,0:T(8,128)(2,1)} %refs_18_.3), channel_id=1, source_target_pairs={{0,16},{16,0},{1,17},{17,1},{2,18},{18,2},{3,19},{19,3},{4,20},{20... | collective-permute-start | bytes 4718600 | tf_op jit(solution)/shard_map/ppermute | solution.py:458
  31.4 25.2 %collective-permute-start.10 = (bf16[1024,256]{1,0:T(8,128)(2,1)S(1)}, bf16[1024,256]{1,0:T(8,128)(2,1)S(1)}, u32[]{:S(2)}, u32[]{:S(2)}) collective-permute-start(bf16[1024,256]{1,0:T(8,128)(2,1)S(1)} %dynamic-slice_bitcast_fusion.1.p0), channel_id=1, source_target_pairs={{0,2},{1,3},{2,0},{3,1},{4,6},{5,7},{6,4},{7,5},{8,10},{9,11},{10,... | collective-permute-start | bytes 1572872 | tf_op jit(solution)/shard_map/ppermute | solution.py:458
  32.6 24.0 %collective-permute-start.9 = (bf16[1024,256]{1,0:T(8,128)(2,1)S(1)}, bf16[1024,256]{1,0:T(8,128)(2,1)S(1)}, u32[]{:S(2)}, u32[]{:S(2)}) collective-permute-start(bf16[1024,256]{1,0:T(8,128)(2,1)S(1)} %dynamic-slice_bitcast_fusion.1.p0), channel_id=1, source_target_pairs={{0,1},{1,0},{2,3},{3,2},{4,5},{5,4},{6,7},{7,6},{8,9},{9,8},{10,11... | collective-permute-start | bytes 1572872 | tf_op jit(solution)/shard_map/ppermute | solution.py:458
  101.1 24.3 %collective-permute-start.20 = (bf16[1024,128]{1,0:T(8,128)(2,1)S(1)}, bf16[1024,128]{1,0:T(8,128)(2,1)S(1)}, u32[]{:S(2)}, u32[]{:S(2)}) collective-permute-start(bf16[1024,128]{1,0:T(8,128)(2,1)S(1)} %slice.192), channel_id=1, source_target_pairs={{0,1},{1,0},{2,3},{3,2},{4,5},{5,4},{6,7},{7,6},{8,9},{9,8},{10,11... | collective-permute-start | bytes 786440 | tf_op jit(solution)/shard_map/ppermute | solution.py:458
  101.5 23.9 %collective-permute-start.19 = (bf16[1024,128]{1,0:T(8,128)(2,1)S(1)}, bf16[1024,128]{1,0:T(8,128)(2,1)S(1)}, u32[]{:S(2)}, u32[]{:S(2)}) collective-permute-start(bf16[1024,128]{1,0:T(8,128)(2,1)S(1)} %slice.191), channel_id=1, source_target_pairs={{0,2},{1,3},{2,0},{3,1},{4,6},{5,7},{6,4},{7,5},{8,10},{9,11},{10,... | collective-permute-start | bytes 786440 | tf_op jit(solution)/shard_map/ppermute | solution.py:458
  133.7 15.6 %collective-permute-start.25 = (bf16[1024,256]{1,0:T(8,128)(2,1)}, bf16[1024,256]{1,0:T(8,128)(2,1)S(1)}, u32[]{:S(2)}, u32[]{:S(2)}) collective-permute-start(bf16[1024,256]{1,0:T(8,128)(2,1)} %get-tuple-element.155), channel_id=1, source_target_pairs={{0,1},{1,0},{2,3},{3,2},{4,5},{5,4},{6,7},{7,6},{8,9},{9,8},{10,11... | collective-permute-start | bytes 1572872 | tf_op jit(solution)/shard_map/ppermute | solution.py:458
  134.0 42.9 %collective-permute-start.26 = (bf16[1024,256]{1,0:T(8,128)(2,1)}, bf16[1024,256]{1,0:T(8,128)(2,1)S(1)}, u32[]{:S(2)}, u32[]{:S(2)}) collective-permute-start(bf16[1024,256]{1,0:T(8,128)(2,1)} %get-tuple-element.156), channel_id=1, source_target_pairs={{0,2},{1,3},{2,0},{3,1},{4,6},{5,7},{6,4},{7,5},{8,10},{9,11},{10,... | collective-permute-start | bytes 1572872 | tf_op jit(solution)/shard_map/ppermute | solution.py:458
  135.6 41.3 %collective-permute-start.27 = (bf16[1024,256]{1,0:T(8,128)(2,1)S(1)}, bf16[1024,256]{1,0:T(8,128)(2,1)S(1)}, u32[]{:S(2)}, u32[]{:S(2)}) collective-permute-start(bf16[1024,256]{1,0:T(8,128)(2,1)S(1)} %copy-done.58), channel_id=1, source_target_pairs={{0,3},{1,2},{2,1},{3,0},{4,7},{5,6},{6,5},{7,4},{8,11},{9,10},{10,... | collective-permute-start | bytes 1572872 | tf_op jit(solution)/shard_map/ppermute | solution.py:458
  145.7 31.3 %collective-permute-start.24 = (bf16[640,256]{1,0:T(8,128)(2,1)S(1)}, bf16[640,256]{1,0:T(8,128)(2,1)S(1)}, u32[]{:S(2)}, u32[]{:S(2)}) collective-permute-start(bf16[640,256]{1,0:T(8,128)(2,1)S(1)} %get-tuple-element.264), channel_id=1, source_target_pairs={{0,12},{4,0},{8,4},{12,8},{1,13},{5,1},{9,5},{13,9},{2,14},{6,2},{... | collective-permute-start | bytes 983048 | tf_op jit(solution)/shard_map/ppermute | solution.py:531
  149.3 27.8 %collective-permute-start.23 = (bf16[640,256]{1,0:T(8,128)(2,1)S(1)}, bf16[640,256]{1,0:T(8,128)(2,1)S(1)}, u32[]{:S(2)}, u32[]{:S(2)}) collective-permute-start(bf16[640,256]{1,0:T(8,128)(2,1)S(1)} %get-tuple-element.265), channel_id=1, source_target_pairs={{0,8},{4,12},{8,0},{12,4},{1,9},{5,13},{9,1},{13,5},{2,10},{6,14},... | collective-permute-start | bytes 983048 | tf_op jit(solution)/shard_map/ppermute | solution.py:531
  149.3 27.8 %collective-permute-start.22 = (bf16[640,256]{1,0:T(8,128)(2,1)S(1)}, bf16[640,256]{1,0:T(8,128)(2,1)S(1)}, u32[]{:S(2)}, u32[]{:S(2)}) collective-permute-start(bf16[640,256]{1,0:T(8,128)(2,1)S(1)} %get-tuple-element.266), channel_id=1, source_target_pairs={{0,4},{4,8},{8,12},{12,0},{1,5},{5,9},{9,13},{13,1},{2,6},{6,10},{... | collective-permute-start | bytes 983048 | tf_op jit(solution)/shard_map/ppermute | solution.py:531
  184.5 19.5 %collective-permute-start.35 = (bf16[1024,896]{1,0:T(8,128)(2,1)}, bf16[1024,896]{1,0:T(8,128)(2,1)}, u32[]{:S(2)}, u32[]{:S(2)}) collective-permute-start(bf16[1024,896]{1,0:T(8,128)(2,1)} %weight_gradient.11), channel_id=1, source_target_pairs={{0,16},{16,0},{1,17},{17,1},{2,18},{18,2},{3,19},{19,3},{4,20},{20... | collective-permute-start | bytes 5505032 | tf_op jit(solution)/shard_map/ppermute | solution.py:458
  184.5 14.5 %collective-permute-start.28 = (bf16[2,1024,128]{2,1,0:T(8,128)(2,1)}, bf16[2,1024,128]{2,1,0:T(8,128)(2,1)S(1)}, u32[]{:S(2)}, u32[]{:S(2)}) collective-permute-start(bf16[2,1024,128]{2,1,0:T(8,128)(2,1)} %get-tuple-element.159), channel_id=1, source_target_pairs={{0,1},{1,0},{2,3},{3,2},{4,5},{5,4},{6,7},{7,6},{8,9},{9,8},{10,11... | collective-permute-start | bytes 1572872 | tf_op jit(solution)/shard_map/ppermute | solution.py:458
  185.1 14.3 %collective-permute-start.30 = (bf16[2,1024,128]{2,1,0:T(8,128)(2,1)}, bf16[2,1024,128]{2,1,0:T(8,128)(2,1)}, u32[]{:S(2)}, u32[]{:S(2)}) collective-permute-start(bf16[2,1024,128]{2,1,0:T(8,128)(2,1)} %get-tuple-element.161), channel_id=1, source_target_pairs={{0,2},{1,3},{2,0},{3,1},{4,6},{5,7},{6,4},{7,5},{8,10},{9,11},{10,... | collective-permute-start | bytes 1572872 | tf_op jit(solution)/shard_map/ppermute | solution.py:458
  259.9 28.3 %collective-permute-start.46 = (bf16[640,256]{1,0:T(8,128)(2,1)S(1)}, bf16[640,256]{1,0:T(8,128)(2,1)S(1)}, u32[]{:S(2)}, u32[]{:S(2)}) collective-permute-start(bf16[640,256]{1,0:T(8,128)(2,1)S(1)} %get-tuple-element.260), channel_id=1, source_target_pairs={{0,12},{4,0},{8,4},{12,8},{1,13},{5,1},{9,5},{13,9},{2,14},{6,2},{... | collective-permute-start | bytes 983048 | tf_op jit(solution)/shard_map/ppermute | solution.py:531
  261.4 28.0 %collective-permute-start.45 = (bf16[640,256]{1,0:T(8,128)(2,1)S(1)}, bf16[640,256]{1,0:T(8,128)(2,1)S(1)}, u32[]{:S(2)}, u32[]{:S(2)}) collective-permute-start(bf16[640,256]{1,0:T(8,128)(2,1)S(1)} %get-tuple-element.261), channel_id=1, source_target_pairs={{0,8},{4,12},{8,0},{12,4},{1,9},{5,13},{9,1},{13,5},{2,10},{6,14},... | collective-permute-start | bytes 983048 | tf_op jit(solution)/shard_map/ppermute | solution.py:531
  261.4 28.0 %collective-permute-start.44 = (bf16[640,256]{1,0:T(8,128)(2,1)S(1)}, bf16[640,256]{1,0:T(8,128)(2,1)S(1)}, u32[]{:S(2)}, u32[]{:S(2)}) collective-permute-start(bf16[640,256]{1,0:T(8,128)(2,1)S(1)} %get-tuple-element.262), channel_id=1, source_target_pairs={{0,4},{4,8},{8,12},{12,0},{1,5},{5,9},{9,13},{13,1},{2,6},{6,10},{... | collective-permute-start | bytes 983048 | tf_op jit(solution)/shard_map/ppermute | solution.py:531
  297.5 15.7 %collective-permute-start.47 = (bf16[1024,256]{1,0:T(8,128)(2,1)}, bf16[1024,256]{1,0:T(8,128)(2,1)S(1)}, u32[]{:S(2)}, u32[]{:S(2)}) collective-permute-start(bf16[1024,256]{1,0:T(8,128)(2,1)} %get-tuple-element.198), channel_id=1, source_target_pairs={{0,1},{1,0},{2,3},{3,2},{4,5},{5,4},{6,7},{7,6},{8,9},{9,8},{10,11... | collective-permute-start | bytes 1572872 | tf_op jit(solution)/shard_map/ppermute | solution.py:458
  298.7 24.2 %collective-permute-start.48 = (bf16[1024,256]{1,0:T(8,128)(2,1)}, bf16[1024,256]{1,0:T(8,128)(2,1)}, u32[]{:S(2)}, u32[]{:S(2)}) collective-permute-start(bf16[1024,256]{1,0:T(8,128)(2,1)} %get-tuple-element.199), channel_id=1, source_target_pairs={{0,2},{1,3},{2,0},{3,1},{4,6},{5,7},{6,4},{7,5},{8,10},{9,11},{10,... | collective-permute-start | bytes 1572872 | tf_op jit(solution)/shard_map/ppermute | solution.py:458
  299.7 24.5 %collective-permute-start.49 = (bf16[1024,256]{1,0:T(8,128)(2,1)}, bf16[1024,256]{1,0:T(8,128)(2,1)}, u32[]{:S(2)}, u32[]{:S(2)}) collective-permute-start(bf16[1024,256]{1,0:T(8,128)(2,1)} %get-tuple-element.200), channel_id=1, source_target_pairs={{0,3},{1,2},{2,1},{3,0},{4,7},{5,6},{6,5},{7,4},{8,11},{9,10},{10,... | collective-permute-start | bytes 1572872 | tf_op jit(solution)/shard_map/ppermute | solution.py:458
  309.0 15.2 %collective-permute-start.51 = (bf16[256,896]{1,0:T(8,128)(2,1)}, bf16[256,896]{1,0:T(8,128)(2,1)}, u32[]{:S(2)}, u32[]{:S(2)}) collective-permute-start(bf16[256,896]{1,0:T(8,128)(2,1)} %add_convert_fusion.9), channel_id=1, source_target_pairs={{0,4},{4,8},{8,12},{12,0},{1,5},{5,9},{9,13},{13,1},{2,6},{6,10},{... | collective-permute-start | bytes 1376264 | tf_op jit(solution)/shard_map/ppermute | solution.py:512
  333.4 27.6 %collective-permute-start.63 = (bf16[640,256]{1,0:T(8,128)(2,1)}, bf16[640,256]{1,0:T(8,128)(2,1)}, u32[]{:S(2)}, u32[]{:S(2)}) collective-permute-start(bf16[640,256]{1,0:T(8,128)(2,1)} %broadcast_select_fusion.3), channel_id=1, source_target_pairs={{0,16},{16,0},{1,17},{17,1},{2,18},{18,2},{3,19},{19,3},{4,20},{20... | collective-permute-start | bytes 983048 | tf_op jit(solution)/shard_map/ppermute | solution.py:458
  336.1 22.7 %collective-permute-start.60 = (bf16[256,896]{1,0:T(8,128)(2,1)}, bf16[256,896]{1,0:T(8,128)(2,1)}, u32[]{:S(2)}, u32[]{:S(2)}) collective-permute-start(bf16[256,896]{1,0:T(8,128)(2,1)} %add_convert_fusion.7), channel_id=1, source_target_pairs={{0,4},{4,8},{8,12},{12,0},{1,5},{5,9},{9,13},{13,1},{2,6},{6,10},{... | collective-permute-start | bytes 1376264 | tf_op jit(solution)/shard_map/ppermute | solution.py:512
  338.8 13.5 %collective-permute-start.59 = (f32[17152]{0:T(1024)S(1)}, f32[17152]{0:T(1024)S(1)}, u32[]{:S(2)}, u32[]{:S(2)}) collective-permute-start(f32[17152]{0:T(1024)S(1)} %select_add_fusion), channel_id=1, source_target_pairs={{0,12},{4,0},{8,4},{12,8},{1,13},{5,1},{9,5},{13,9},{2,14},{6,2},{... | collective-permute-start | bytes 205832 | tf_op jit(solution)/shard_map/ppermute | solution.py:521
  340.8 15.9 %collective-permute-start.58 = (f32[17152]{0:T(1024)S(1)}, f32[17152]{0:T(1024)S(1)}, u32[]{:S(2)}, u32[]{:S(2)}) collective-permute-start(f32[17152]{0:T(1024)S(1)} %select_add_fusion), channel_id=1, source_target_pairs={{0,8},{4,12},{8,0},{12,4},{1,9},{5,13},{9,1},{13,5},{2,10},{6,14},... | collective-permute-start | bytes 205832 | tf_op jit(solution)/shard_map/ppermute | solution.py:521
  342.3 14.5 %collective-permute-start.57 = (f32[17152]{0:T(1024)S(1)}, f32[17152]{0:T(1024)S(1)}, u32[]{:S(2)}, u32[]{:S(2)}) collective-permute-start(f32[17152]{0:T(1024)S(1)} %select_add_fusion), channel_id=1, source_target_pairs={{0,4},{4,8},{8,12},{12,0},{1,5},{5,9},{9,13},{13,1},{2,6},{6,10},{... | collective-permute-start | bytes 205832 | tf_op jit(solution)/shard_map/ppermute | solution.py:521
  352.3 25.9 %collective-permute-start.55 = (f32[1024,256]{1,0:T(8,128)}, f32[1024,256]{1,0:T(8,128)}, u32[]{:S(2)}, u32[]{:S(2)}) collective-permute-start(f32[1024,256]{1,0:T(8,128)} %get-tuple-element.259), channel_id=1, source_target_pairs={{0,16},{16,0},{1,17},{17,1},{2,18},{18,2},{3,19},{19,3},{4,20},{20... | collective-permute-start | bytes 3145736 | tf_op jit(solution)/shard_map/ppermute | solution.py:458
  360.3 14.3 %collective-permute-start.61 = (bf16[256,896]{1,0:T(8,128)(2,1)S(1)}, bf16[256,896]{1,0:T(8,128)(2,1)S(1)}, u32[]{:S(2)}, u32[]{:S(2)}) collective-permute-start(bf16[256,896]{1,0:T(8,128)(2,1)S(1)} %add_convert_fusion.5), channel_id=1, source_target_pairs={{0,4},{4,8},{8,12},{12,0},{1,5},{5,9},{9,13},{13,1},{2,6},{6,10},{... | collective-permute-start | bytes 1376264 | tf_op jit(solution)/shard_map/ppermute | solution.py:512
  (92 other events, 874.4 us)
where the time goes:
time: 386 us; the launch traced here: 384 us
  Pallas kernels  147 us (38%)
  waiting for transfers between devices  104 us (27%)
  starting transfers between devices  62.9 us (16%)
  other arithmetic  41 us (11%)
  local copies, waits for them, and re-layouts  25 us (6%)
    ppermute x49, waiting for transfers between devices, swap(): lax.ppermute(value, axis, [(k, k ^ by) for k in range(lax.axis_size(axis))])  60.4 us
    pallas_call x2, Pallas kernels, backward_layer(): pl.pallas_call(functools.partial(backward_kernel, carry is not None, phas...  52.8 us
    pallas_call x8, Pallas kernels, product(): pl.pallas_call(product_kernel, name='weight_gradient', out_shape=jax.Shap...  48 us
    ppermute x49, starting transfers between devices, swap(): lax.ppermute(value, axis, [(k, k ^ by) for k in range(lax.axis_size(axis))])  45.7 us
    pallas_call x2, Pallas kernels, forward_layer(): pl.pallas_call(functools.partial(forward_kernel, carry is not None, phase...  44.5 us
    ppermute x6, waiting for transfers between devices, ring_scatter(): arrived = after(lax.ppermute(total, axis, pairs), *meanwhile)  30.5 us
    ppermute x3, waiting for transfers between devices, dp_total(): lax.ppermute(values, 'dp', [(i, (i + k) % count) for i in range(count)])  12.3 us
  transfers between devices with their start and end apart: 64, of which 25 were waited for; matrix products, arithmetic and copies ran while one was open for 15% of the time, Pallas kernels for 32%

commit v1 on v0

--- a/solution.py
+++ b/solution.py
@@ -459,9 +459,13 @@
 
 
 def gather_pieces(shard, meanwhile=()):
-    half = shard.shape[1] // 2
     from_x, from_y = after((swap(shard, "mp", 1), swap(shard, "mp", 2)), *meanwhile)
-    return shard, from_x, from_y, swap(from_x[:, :half], "mp", 2), swap(from_y[:, half:], "mp", 1)
+    return (shard, from_x, from_y) + last_pieces(from_x, from_y)
+
+
+def last_pieces(from_x, from_y):
+    half = from_x.shape[1] // 2
+    return tuple(lax.optimization_barrier((swap(from_x[:, :half], "mp", 2), swap(from_y[:, half:], "mp", 1))))
 
 
 def after(values, *others):
@@ -509,17 +513,18 @@
     pairs = [(k, (k + 1) % count) for k in range(count)]
     total = block_of((rank + count - 1) % count)
     for step in range(2, count + 1):
-        arrived = after(lax.ppermute(total, axis, pairs), *meanwhile)
+        arrived = lax.ppermute(total, axis, pairs)
+        if step in (2, count):
+            arrived = after(arrived, *meanwhile)
         total = (arrived.astype(F32) + block_of((rank + count - step) % count).astype(F32)).astype(BF16)
         yield arrived, total
 
 
-def dp_total(values):
+def dp_sends(values):
     count = lax.axis_size("dp")
     if count > 8:
-        return lax.psum(values, "dp")
-    sent = [lax.ppermute(values, "dp", [(i, (i + k) % count) for i in range(count)]) for k in range(1, count)]
-    return sum(sent, values)
+        return [lax.psum(values, "dp")]
+    return [values] + [lax.ppermute(values, "dp", [(i, (i + k) % count) for i in range(count)]) for k in range(1, count)]
 
 
 def block_sends(block_of, axis):
@@ -555,7 +560,7 @@
                 num_scalar_prefetch=1, grid=(steps,),
                 in_specs=[pl.BlockSpec((rows, block), left_at), pl.BlockSpec((rows, n), right_at)],
                 out_specs=pl.BlockSpec((block, n), lambda i, which: (i, 0))),
-            compiler_params=params(58),
+            compiler_params=params(20),
             cost_estimate=pl.CostEstimate(flops=2 * rows * m * n, transcendentals=0, bytes_accessed=2 * (rows * (m + n) + m * n)),
         )(which.reshape(1).astype(jnp.int32), left, right)
 
@@ -630,8 +635,7 @@
     hidden = (shard0.astype(F32) + scatter_sum(part0)).astype(BF16)
     pieces1 = gather_pieces(hidden)
     cot_x, cot_y = after((cot_x, cot_y), pieces1[3], pieces1[4])
-    half = shard_width // 2
-    pieces_g = cot, cot_x, cot_y, swap(cot_x[:, :half], "mp", 2), swap(cot_y[:, half:], "mp", 1)
+    pieces_g = (cot, cot_x, cot_y) + last_pieces(cot_x, cot_y)
     part1, all1, _ = forward_layer(metas[1], lens, pieces1, weights1, tables, length, 0, False)
     out_kept, out_sent = direct_sends(part1)
 
@@ -692,9 +696,12 @@
     kept, sent = direct_sends(parts)
     mine0, arrived0 = weight_gradient(saved0[0], dcat0, False, section)
     block0 = in_block(mine0, arrived0)
-    steps0 = list(ring_scatter(block0, "dp", sent))
-    sums = mp_total(after(stats, steps0[0][0]))
-    sent, dmix0, out_blocks0, out_blocks1 = after((sent, dmix0, out_blocks0, out_blocks1), steps0[0][0])
+    meanwhile = list(sent)
+    ring0 = ring_scatter(block0, "dp", meanwhile)
+    steps0 = [next(ring0)]
+    meanwhile.clear()
+    sums = mp_total(after(stats, steps0[0][1]))
+    sent, dmix0, out_blocks0, out_blocks1 = after((sent, dmix0, out_blocks0, out_blocks1), steps0[0][1])
     d_normed = kept + sent[0].astype(F32) + sent[1].astype(F32) + sent[2].astype(F32)
     d_input = norm_backward(g0, d_normed, sums, all0[1:3], weights0[0][0])
     small0 = small_gradients(d_normed, all0[1:3], dmix0, fsum0)
@@ -706,14 +713,18 @@
 
     grads_out = to_owner(sum_blocks(out_blocks0), sum_blocks(out_blocks1), 0)
     small_mine, small_send = both(small0, small1)
-    small_sum = dp_total(small_mine + swap(small_send, "section", 1))
+    small_sum = small_mine + swap(small_send, "section", 1)
+    small_parts = dp_sends(small_sum)
+    keep, send = both(d_input, out)
+    arrived = swap(send, "section", 1)
+    boundary = jnp.where(is_first, jnp.stack([keep, arrived]), jnp.stack([arrived, keep]))
+    meanwhile.append(arrived)
+    steps0 += list(ring0)
+    grads_in = to_owner(steps0[-1][1], red_in1, 1)
+    small_sum = sum(after(small_parts, steps0[-1][0]))
     feat_grad = small_sum[2 * shard_width:2 * shard_width + LANES].reshape(heads, HEAD) / feat_weight[0]
     freq_grad = jnp.einsum("nk,hnm->hkm", table, small_sum[2 * shard_width + LANES:].reshape(heads, HEAD, HEAD),
                            precision=lax.Precision.HIGHEST)
-    keep, send = both(d_input, out)
-    arrived = swap(send, "section", 1)
-    boundary = jnp.where(is_first, jnp.stack([keep, arrived]), jnp.stack([arrived, keep]))
-    grads_in = to_owner(steps0[-1][1], red_in1, 1)
     qkv_grad = jnp.stack([grads_in[:, t * shard_width:(t + 1) * shard_width] for t in range(3)])
     return (
         boundary[None],

time: 386 us -> 374 us (0.969)
  waiting for transfers between devices: 104 us -> 92.6 us
  Pallas kernels: 147 us -> 137 us
  local copies, waits for them, and re-layouts: 25 us -> 32.1 us
  other arithmetic: 41 us -> 36.9 us
    pallas_call x8, Pallas kernels: 48 us -> 27.2 us  [product(): pl.pallas_call(product_kernel, name='weight_gradient', out_shape=jax.Shap...]
    ppermute x9, waiting for transfers between devices: 42.8 us -> 29.4 us  [the longest x6 27.9 us: ring_scatter(): arrived = lax.ppermute(total, axis, pairs)]
    pallas_call x2, Pallas kernels: 1.86 us -> 11.9 us  [join(): pl.pallas_call(join_kernel, name='join', out_shape=jax.ShapeDtypeStruct((...]
    unnamed x121 -> x155, local copies, waits for them, and re-layouts: 5.89 us -> 14.6 us
  transfers between devices with their start and end apart: 64 -> 64, of which waited for: 25 -> 27; matrix products, arithmetic and copies ran while one was open for 15% -> 13% of each run, Pallas kernels for 32% -> 30%
where the time goes in v1:
time: 374 us; the launch traced here: 368 us
  Pallas kernels  137 us (37%)
  waiting for transfers between devices  92.6 us (25%)
  starting transfers between devices  66.7 us (18%)
  other arithmetic  36.9 us (10%)
  local copies, waits for them, and re-layouts  32.1 us (9%)
    ppermute x49, waiting for transfers between devices, swap(): lax.ppermute(value, axis, [(k, k ^ by) for k in range(lax.axis_size(axis))])  62 us
    pallas_call x2, Pallas kernels, backward_layer(): pl.pallas_call(functools.partial(backward_kernel, carry is not None, phas...  52.9 us
    ppermute x49, starting transfers between devices, swap(): lax.ppermute(value, axis, [(k, k ^ by) for k in range(lax.axis_size(axis))])  49.6 us
    pallas_call x2, Pallas kernels, forward_layer(): pl.pallas_call(functools.partial(forward_kernel, carry is not None, phase...  44.6 us
    ppermute x6, waiting for transfers between devices, ring_scatter(): arrived = lax.ppermute(total, axis, pairs)  27.9 us
    pallas_call x8, Pallas kernels, product(): pl.pallas_call(product_kernel, name='weight_gradient', out_shape=jax.Shap...  27.2 us
    unnamed x155, local copies, waits for them, and re-layouts  14.6 us
    pallas_call x2, Pallas kernels, join(): pl.pallas_call(join_kernel, name='join', out_shape=jax.ShapeDtypeStruct((...  11.9 us
  transfers between devices with their start and end apart: 64, of which 27 were waited for; matrix products, arithmetic and copies ran while one was open for 13% of the time, Pallas kernels for 30%

profile of v1, /device:TPU:0, one launch (start us, length us, event | category | flops | bytes accessed | tf_op | source)
XLA Modules:
  0.0 368.4 jit_solution(5016212886600088816)
XLA Ops:
  1.9 3.1 collective-permute-start.2
  11.4 2.8 multiply_select_fusion
  20.7 4.6 %collective-permute-done.3.refs_6_ = bf16[1024,128]{1,0:T(8,128)(2,1)} collective-permute-done((bf16[1024,128]{1,0:T(8,128)(2,1)S(1)}, bf16[1024,128]{1,0:T(8,128)(2,1)}, u32[]{:S(2)}, u32[]{:S(2)}) %collective-permute-start.3) | collective-permute-done | bytes 262176 | tf_op jit(solution)/shard_map/ppermute | solution.py:458
  28.3 4.3 %collective-permute-done.1.refs_5_ = bf16[1024,128]{1,0:T(8,128)(2,1)S(1)} collective-permute-done((bf16[1024,128]{1,0:T(8,128)(2,1)S(1)}, bf16[1024,128]{1,0:T(8,128)(2,1)S(1)}, u32[]{:S(2)}, u32[]{:S(2)}) %collective-permute-start.1) | collective-permute-done | bytes 262176 | tf_op jit(solution)/shard_map/ppermute | solution.py:458
  34.1 22.5 %layer_forward.2 = (bf16[2,1024,128]{2,1,0:T(8,128)(2,1)}, bf16[2,1024,128]{2,1,0:T(8,128)(2,1)}, f32[1024,256]{1,0:T(8,128)}, f32[1024,128]{1,0:T(8,128)}, f32[...) custom-call(s32[2]{0:T(128)} %pad_add_fusion.2.refs_0_.meta, ...), custom_call_target="tpu_custom_call" | custom-call | flops 20480000000 | bytes 25165824 | tf_op jit(solution)/shard_map/layer_forward/pallas_call | solution.py:386
  59.4 8.8 %collective-permute-done.11 = bf16[2,1024,128]{2,1,0:T(8,128)(2,1)S(1)} collective-permute-done((bf16[2,1024,128]{2,1,0:T(8,128)(2,1)}, bf16[2,1024,128]{2,1,0:T(8,128)(2,1)S(1)}, u32[]{:S(2)}, u32[]{:S(2)}) %collective-permute-start.11) | collective-permute-done | bytes 524320 | tf_op jit(solution)/shard_map/ppermute | solution.py:458
  75.7 3.4 collective-permute-done.14
  81.5 7.4 %collective-permute-done.16.refs_4_ = bf16[1024,256]{1,0:T(8,128)(2,1)S(1)} collective-permute-done((bf16[1024,256]{1,0:T(8,128)(2,1)S(1)}, bf16[1024,256]{1,0:T(8,128)(2,1)S(1)}, u32[]{:S(2)}, u32[]{:S(2)}) %collective-permute-start.16) | collective-permute-done | bytes 524320 | tf_op jit(solution)/shard_map/ppermute | solution.py:458
  89.0 2.6 collective-permute-start.18
  97.4 4.4 %collective-permute-done.17.refs_5_ = bf16[1024,128]{1,0:T(8,128)(2,1)} collective-permute-done((bf16[1024,128]{1,0:T(8,128)(2,1)S(1)}, bf16[1024,128]{1,0:T(8,128)(2,1)}, u32[]{:S(2)}, u32[]{:S(2)}) %collective-permute-start.17) | collective-permute-done | bytes 262176 | tf_op jit(solution)/shard_map/ppermute | solution.py:458
  103.2 22.1 %layer_forward.3 = (f32[1024,256]{1,0:T(8,128)}, bf16[1024,256]{1,0:T(8,128)(2,1)}, bf16[1024,256]{1,0:T(8,128)(2,1)}, bf16[1024,256]{1,0:T(8,128)(2,1)}, bf16[1...) custom-call(s32[2]{0:T(128)} %pad_add_fusion.refs_0_.meta, ...), custom_call_target="tpu_custom_call" | custom-call | flops 20480000000 | bytes 25165824 | tf_op jit(solution)/shard_map/layer_forward/pallas_call | solution.py:386
  127.1 3.7 %weight_gradient.9 = bf16[640,1024]{1,0:T(8,128)(2,1)} custom-call(s32[1]{0:T(128)} %bitcast.21.which, bf16[1024,1280]{1,0:T(8,128)(2,1)S(1)} %copy-done.9, bf16[1024,1024]{1,0:T(8,128)(2,1)S(1)} %join.2.right.refs_1_), custom_call_target="tpu_custom_call" | custom-call | flops 1342177280 | bytes 4718592 | tf_op jit(solution)/shard_map/weight_gradient/pallas_call | solution.py:555
  136.0 2.7 weight_gradient.8
  140.5 3.0 collective-permute-start.24
  146.7 26.7 %layer_backward.2 = (bf16[2,1024,128]{2,1,0:T(8,128)(2,1)}, bf16[2,1024,128]{2,1,0:T(8,128)(2,1)}, f32[1024,256]{1,0:T(8,128)}, f32[1024,128]{1,0:T(8,128)}, f32...) custom-call(s32[2]{0:T(128)} %pad_add_fusion.refs_0_.meta, ...), custom_call_target="tpu_custom_call" | custom-call | flops 25600000000 | bytes 25165824 | tf_op jit(solution)/shard_map/layer_backward/pallas_call | solution.py:426
  176.6 4.3 %weight_gradient.11 = bf16[1024,896]{1,0:T(8,128)(2,1)} custom-call(s32[1]{0:T(128)} %bitcast.21.which, bf16[1024,1024]{1,0:T(8,128)(2,1)S(1)} %copy-done.12, bf16[1024,1792]{1,0:T(8,128)(2,1)S(1)} %copy-done.6), custom_call_target="tpu_custom_call" | custom-call | flops 1879048192 | bytes 5767168 | tf_op jit(solution)/shard_map/weight_gradient/pallas_call | solution.py:555
  187.0 3.5 weight_gradient.10
  190.5 5.0 %collective-permute-done.28 = bf16[2,1024,128]{2,1,0:T(8,128)(2,1)} collective-permute-done((bf16[2,1024,128]{2,1,0:T(8,128)(2,1)}, bf16[2,1024,128]{2,1,0:T(8,128)(2,1)}, u32[]{:S(2)}, u32[]{:S(2)}) %collective-permute-start.28) | collective-permute-done | bytes 524320 | tf_op jit(solution)/shard_map/ppermute | solution.py:458
  207.5 7.9 %collective-permute-done.36 = bf16[256,896]{1,0:T(8,128)(2,1)S(1)} collective-permute-done((bf16[256,896]{1,0:T(8,128)(2,1)S(1)}, bf16[256,896]{1,0:T(8,128)(2,1)S(1)}, u32[]{:S(2)}, u32[]{:S(2)}) %collective-permute-start.36) | collective-permute-done | bytes 458784 | tf_op jit(solution)/shard_map/ppermute | solution.py:516
  221.9 6.8 %collective-permute-done.39 = bf16[256,896]{1,0:T(8,128)(2,1)S(1)} collective-permute-done((bf16[256,896]{1,0:T(8,128)(2,1)S(1)}, bf16[256,896]{1,0:T(8,128)(2,1)S(1)}, u32[]{:S(2)}, u32[]{:S(2)}) %collective-permute-start.39) | collective-permute-done | bytes 458784 | tf_op jit(solution)/shard_map/ppermute | solution.py:516
  234.2 4.4 %collective-permute-done.41.p3b = bf16[1024,128]{1,0:T(8,128)(2,1)S(1)} collective-permute-done((bf16[1024,128]{1,0:T(8,128)(2,1)S(1)}, bf16[1024,128]{1,0:T(8,128)(2,1)S(1)}, u32[]{:S(2)}, u32[]{:S(2)}) %collective-permute-start.41) | collective-permute-done | bytes 262176 | tf_op jit(solution)/shard_map/ppermute | solution.py:458
  241.2 10.7 %join.3.right.refs_1_ = bf16[1024,1024]{1,0:T(8,128)(2,1)S(1)} custom-call(s32[2]{0:T(128)S(1)} %copy-done.23, bf16[1024,256]{1,0:T(8,128)(2,1)S(1)} %get-tuple-element.190.p0, bf16[1024,256]{1,0:T(8,128)(2,1)S(1)} %collective-permute-done.37.p1, bf16[1024,256]{1,0:T(8,128)(2,1)S(1)} %collective-permute-done.38.p2, ...), custom_call_target="tpu_custom_call" | custom-call | bytes 4194304 | tf_op jit(solution)/shard_map/join/pallas_call | solution.py:442
  251.9 2.7 weight_gradient.13
  254.7 2.7 weight_gradient.12
  259.1 2.9 collective-permute-start.46
  262.6 26.1 %layer_backward.3 = (f32[1024,256]{1,0:T(8,128)}, bf16[1024,256]{1,0:T(8,128)(2,1)}, bf16[1024,256]{1,0:T(8,128)(2,1)}, bf16[1024,256]{1,0:T(8,128)(2,1)}, f32[8...) custom-call(s32[2]{0:T(128)} %pad_add_fusion.2.refs_0_.meta, ...), custom_call_target="tpu_custom_call" | custom-call | flops 25600000000 | bytes 25165824 | tf_op jit(solution)/shard_map/layer_backward/pallas_call | solution.py:426
  292.1 4.2 %weight_gradient.15 = bf16[1024,896]{1,0:T(8,128)(2,1)} custom-call(s32[1]{0:T(128)} %bitcast.21.which, bf16[1024,1024]{1,0:T(8,128)(2,1)S(1)} %copy-done.11, bf16[1024,1792]{1,0:T(8,128)(2,1)S(1)} %copy-done.4), custom_call_target="tpu_custom_call" | custom-call | flops 1879048192 | bytes 5767168 | tf_op jit(solution)/shard_map/weight_gradient/pallas_call | solution.py:555
  303.3 3.5 weight_gradient.14
  314.4 9.3 %collective-permute-done.48 = bf16[1024,256]{1,0:T(8,128)(2,1)} collective-permute-done((bf16[1024,256]{1,0:T(8,128)(2,1)}, bf16[1024,256]{1,0:T(8,128)(2,1)}, u32[]{:S(2)}, u32[]{:S(2)}) %collective-permute-start.48) | collective-permute-done | bytes 524320 | tf_op jit(solution)/shard_map/ppermute | solution.py:458
  340.4 3.6 collective-permute-done.60
  348.5 8.3 %collective-permute-done.61 = bf16[256,896]{1,0:T(8,128)(2,1)S(1)} collective-permute-done((bf16[256,896]{1,0:T(8,128)(2,1)S(1)}, bf16[256,896]{1,0:T(8,128)(2,1)S(1)}, u32[]{:S(2)}, u32[]{:S(2)}) %collective-permute-start.61) | collective-permute-done | bytes 458784 | tf_op jit(solution)/shard_map/ppermute | solution.py:516
  362.2 3.1 maximum_select_fusion
  (359 shorter events, 135.0 us)
Async XLA Ops:
  1.9 15.0 %collective-permute-start.2 = (bf16[1024,256]{1,0:T(8,128)(2,1)S(1)}, bf16[1024,256]{1,0:T(8,128)(2,1)S(1)}, u32[]{:S(2)}, u32[]{:S(2)}) collective-permute-start(bf16[1024,256]{1,0:T(8,128)(2,1)S(1)} %dynamic-slice_bitcast_fusion.refs_2_), channel_id=1, source_target_pairs={{0,2},{1,3},{2,0},{3,1},{4,6},{5,7},{6,4},{7,5},{8,10},{9,11},{10,... | collective-permute-start | bytes 1572872 | tf_op jit(solution)/shard_map/ppermute | solution.py:458
  4.9 14.4 %collective-permute-start = (bf16[1024,256]{1,0:T(8,128)(2,1)S(1)}, bf16[1024,256]{1,0:T(8,128)(2,1)}, u32[]{:S(2)}, u32[]{:S(2)}) collective-permute-start(bf16[1024,256]{1,0:T(8,128)(2,1)S(1)} %dynamic-slice_bitcast_fusion.refs_2_), channel_id=1, source_target_pairs={{0,1},{1,0},{2,3},{3,2},{4,5},{5,4},{6,7},{7,6},{8,9},{9,8},{10,11... | collective-permute-start | bytes 1572872 | tf_op jit(solution)/shard_map/ppermute | solution.py:458
  8.9 25.2 %collective-permute-start.6 = (bf16[1,1024,1024]{2,1,0:T(8,128)(2,1)}, bf16[1,1024,1024]{2,1,0:T(8,128)(2,1)}, u32[]{:S(2)}, u32[]{:S(2)}) collective-permute-start(bf16[1,1024,1024]{2,1,0:T(8,128)(2,1)} %refs_19_.3), channel_id=1, source_target_pairs={{0,16},{16,0},{1,17},{17,1},{2,18},{18,2},{3,19},{19,3},{4,20},{20... | collective-permute-start | bytes 6291464 | tf_op jit(solution)/shard_map/ppermute | solution.py:458
  9.4 24.7 %collective-permute-start.8 = (bf16[1,1024,1024]{2,1,0:T(8,128)(2,1)}, bf16[1,1024,1024]{2,1,0:T(8,128)(2,1)}, u32[]{:S(2)}, u32[]{:S(2)}) collective-permute-start(bf16[1,1024,1024]{2,1,0:T(8,128)(2,1)} %refs_21_.3), channel_id=1, source_target_pairs={{0,16},{16,0},{1,17},{17,1},{2,18},{18,2},{3,19},{19,3},{4,20},{20... | collective-permute-start | bytes 6291464 | tf_op jit(solution)/shard_map/ppermute | solution.py:458
  15.6 18.4 %collective-permute-start.5 = (bf16[1,3,1024,256]{3,2,1,0:T(8,128)(2,1)}, bf16[1,3,1024,256]{3,2,1,0:T(8,128)(2,1)}, u32[]{:S(2)}, u32[]{:S(2)}) collective-permute-start(bf16[1,3,1024,256]{3,2,1,0:T(8,128)(2,1)} %refs_18_.3), channel_id=1, source_target_pairs={{0,16},{16,0},{1,17},{17,1},{2,18},{18,2},{3,19},{19,3},{4,20},{20... | collective-permute-start | bytes 4718600 | tf_op jit(solution)/shard_map/ppermute | solution.py:458
  19.3 13.6 %collective-permute-start.7 = (bf16[1,256,1024]{2,1,0:T(8,128)(2,1)}, bf16[1,256,1024]{2,1,0:T(8,128)(2,1)}, u32[]{:S(2)}, u32[]{:S(2)}) collective-permute-start(bf16[1,256,1024]{2,1,0:T(8,128)(2,1)} %refs_20_.3), channel_id=1, source_target_pairs={{0,16},{16,0},{1,17},{17,1},{2,18},{18,2},{3,19},{19,3},{4,20},{20... | collective-permute-start | bytes 1572872 | tf_op jit(solution)/shard_map/ppermute | solution.py:458
  32.6 23.9 %collective-permute-start.10 = (bf16[1024,256]{1,0:T(8,128)(2,1)S(1)}, bf16[1024,256]{1,0:T(8,128)(2,1)S(1)}, u32[]{:S(2)}, u32[]{:S(2)}) collective-permute-start(bf16[1024,256]{1,0:T(8,128)(2,1)S(1)} %dynamic-slice_bitcast_fusion.1.p0), channel_id=1, source_target_pairs={{0,2},{1,3},{2,0},{3,1},{4,6},{5,7},{6,4},{7,5},{8,10},{9,11},{10,... | collective-permute-start | bytes 1572872 | tf_op jit(solution)/shard_map/ppermute | solution.py:458
  32.9 23.7 %collective-permute-start.9 = (bf16[1024,256]{1,0:T(8,128)(2,1)S(1)}, bf16[1024,256]{1,0:T(8,128)(2,1)S(1)}, u32[]{:S(2)}, u32[]{:S(2)}) collective-permute-start(bf16[1024,256]{1,0:T(8,128)(2,1)S(1)} %dynamic-slice_bitcast_fusion.1.p0), channel_id=1, source_target_pairs={{0,1},{1,0},{2,3},{3,2},{4,5},{5,4},{6,7},{7,6},{8,9},{9,8},{10,11... | collective-permute-start | bytes 1572872 | tf_op jit(solution)/shard_map/ppermute | solution.py:458
  57.6 13.0 %collective-permute-start.13 = (bf16[2,1024,128]{2,1,0:T(8,128)(2,1)}, bf16[2,1024,128]{2,1,0:T(8,128)(2,1)S(1)}, u32[]{:S(2)}, u32[]{:S(2)}) collective-permute-start(bf16[2,1024,128]{2,1,0:T(8,128)(2,1)} %get-tuple-element.141), channel_id=1, source_target_pairs={{0,2},{1,3},{2,0},{3,1},{4,6},{5,7},{6,4},{7,5},{8,10},{9,11},{10,... | collective-permute-start | bytes 1572872 | tf_op jit(solution)/shard_map/ppermute | solution.py:458
  101.9 23.4 %collective-permute-start.20 = (bf16[1024,128]{1,0:T(8,128)(2,1)S(1)}, bf16[1024,128]{1,0:T(8,128)(2,1)S(1)}, u32[]{:S(2)}, u32[]{:S(2)}) collective-permute-start(bf16[1024,128]{1,0:T(8,128)(2,1)S(1)} %slice.192), channel_id=1, source_target_pairs={{0,1},{1,0},{2,3},{3,2},{4,5},{5,4},{6,7},{7,6},{8,9},{9,8},{10,11... | collective-permute-start | bytes 786440 | tf_op jit(solution)/shard_map/ppermute | solution.py:458
  102.3 23.0 %collective-permute-start.19 = (bf16[1024,128]{1,0:T(8,128)(2,1)S(1)}, bf16[1024,128]{1,0:T(8,128)(2,1)S(1)}, u32[]{:S(2)}, u32[]{:S(2)}) collective-permute-start(bf16[1024,128]{1,0:T(8,128)(2,1)S(1)} %slice.191), channel_id=1, source_target_pairs={{0,2},{1,3},{2,0},{3,1},{4,6},{5,7},{6,4},{7,5},{8,10},{9,11},{10,... | collective-permute-start | bytes 786440 | tf_op jit(solution)/shard_map/ppermute | solution.py:458
  130.8 15.0 %collective-permute-start.25 = (bf16[1024,256]{1,0:T(8,128)(2,1)}, bf16[1024,256]{1,0:T(8,128)(2,1)S(1)}, u32[]{:S(2)}, u32[]{:S(2)}) collective-permute-start(bf16[1024,256]{1,0:T(8,128)(2,1)} %get-tuple-element.172), channel_id=1, source_target_pairs={{0,1},{1,0},{2,3},{3,2},{4,5},{5,4},{6,7},{7,6},{8,9},{9,8},{10,11... | collective-permute-start | bytes 1572872 | tf_op jit(solution)/shard_map/ppermute | solution.py:458
  131.9 41.6 %collective-permute-start.26 = (bf16[1024,256]{1,0:T(8,128)(2,1)}, bf16[1024,256]{1,0:T(8,128)(2,1)S(1)}, u32[]{:S(2)}, u32[]{:S(2)}) collective-permute-start(bf16[1024,256]{1,0:T(8,128)(2,1)} %get-tuple-element.173), channel_id=1, source_target_pairs={{0,2},{1,3},{2,0},{3,1},{4,6},{5,7},{6,4},{7,5},{8,10},{9,11},{10,... | collective-permute-start | bytes 1572872 | tf_op jit(solution)/shard_map/ppermute | solution.py:458
  133.7 39.8 %collective-permute-start.27 = (bf16[1024,256]{1,0:T(8,128)(2,1)}, bf16[1024,256]{1,0:T(8,128)(2,1)S(1)}, u32[]{:S(2)}, u32[]{:S(2)}) collective-permute-start(bf16[1024,256]{1,0:T(8,128)(2,1)} %get-tuple-element.174), channel_id=1, source_target_pairs={{0,3},{1,2},{2,1},{3,0},{4,7},{5,6},{6,5},{7,4},{8,11},{9,10},{10,... | collective-permute-start | bytes 1572872 | tf_op jit(solution)/shard_map/ppermute | solution.py:458
  140.5 33.0 %collective-permute-start.24 = (bf16[640,256]{1,0:T(8,128)(2,1)S(1)}, bf16[640,256]{1,0:T(8,128)(2,1)S(1)}, u32[]{:S(2)}, u32[]{:S(2)}) collective-permute-start(bf16[640,256]{1,0:T(8,128)(2,1)S(1)} %get-tuple-element.286), channel_id=1, source_target_pairs={{0,12},{4,0},{8,4},{12,8},{1,13},{5,1},{9,5},{13,9},{2,14},{6,2},{... | collective-permute-start | bytes 983048 | tf_op jit(solution)/shard_map/ppermute | solution.py:536
  143.5 30.0 %collective-permute-start.23 = (bf16[640,256]{1,0:T(8,128)(2,1)S(1)}, bf16[640,256]{1,0:T(8,128)(2,1)S(1)}, u32[]{:S(2)}, u32[]{:S(2)}) collective-permute-start(bf16[640,256]{1,0:T(8,128)(2,1)S(1)} %get-tuple-element.287), channel_id=1, source_target_pairs={{0,8},{4,12},{8,0},{12,4},{1,9},{5,13},{9,1},{13,5},{2,10},{6,14},... | collective-permute-start | bytes 983048 | tf_op jit(solution)/shard_map/ppermute | solution.py:536
  145.8 27.8 %collective-permute-start.22 = (bf16[640,256]{1,0:T(8,128)(2,1)S(1)}, bf16[640,256]{1,0:T(8,128)(2,1)S(1)}, u32[]{:S(2)}, u32[]{:S(2)}) collective-permute-start(bf16[640,256]{1,0:T(8,128)(2,1)S(1)} %get-tuple-element.288), channel_id=1, source_target_pairs={{0,4},{4,8},{8,12},{12,0},{1,5},{5,9},{9,13},{13,1},{2,6},{6,10},{... | collective-permute-start | bytes 983048 | tf_op jit(solution)/shard_map/ppermute | solution.py:536
  180.9 20.5 %collective-permute-start.35 = (bf16[1024,896]{1,0:T(8,128)(2,1)}, bf16[1024,896]{1,0:T(8,128)(2,1)}, u32[]{:S(2)}, u32[]{:S(2)}) collective-permute-start(bf16[1024,896]{1,0:T(8,128)(2,1)} %weight_gradient.11), channel_id=1, source_target_pairs={{0,16},{16,0},{1,17},{17,1},{2,18},{18,2},{3,19},{19,3},{4,20},{20... | collective-permute-start | bytes 5505032 | tf_op jit(solution)/shard_map/ppermute | solution.py:458
  180.9 14.7 %collective-permute-start.28 = (bf16[2,1024,128]{2,1,0:T(8,128)(2,1)}, bf16[2,1024,128]{2,1,0:T(8,128)(2,1)}, u32[]{:S(2)}, u32[]{:S(2)}) collective-permute-start(bf16[2,1024,128]{2,1,0:T(8,128)(2,1)} %get-tuple-element.176), channel_id=1, source_target_pairs={{0,1},{1,0},{2,3},{3,2},{4,5},{5,4},{6,7},{7,6},{8,9},{9,8},{10,11... | collective-permute-start | bytes 1572872 | tf_op jit(solution)/shard_map/ppermute | solution.py:458
  182.4 14.4 %collective-permute-start.30 = (bf16[2,1024,128]{2,1,0:T(8,128)(2,1)}, bf16[2,1024,128]{2,1,0:T(8,128)(2,1)}, u32[]{:S(2)}, u32[]{:S(2)}) collective-permute-start(bf16[2,1024,128]{2,1,0:T(8,128)(2,1)} %get-tuple-element.178), channel_id=1, source_target_pairs={{0,2},{1,3},{2,0},{3,1},{4,6},{5,7},{6,4},{7,5},{8,10},{9,11},{10,... | collective-permute-start | bytes 1572872 | tf_op jit(solution)/shard_map/ppermute | solution.py:458
  259.1 29.6 %collective-permute-start.46 = (bf16[640,256]{1,0:T(8,128)(2,1)S(1)}, bf16[640,256]{1,0:T(8,128)(2,1)S(1)}, u32[]{:S(2)}, u32[]{:S(2)}) collective-permute-start(bf16[640,256]{1,0:T(8,128)(2,1)S(1)} %get-tuple-element.282), channel_id=1, source_target_pairs={{0,12},{4,0},{8,4},{12,8},{1,13},{5,1},{9,5},{13,9},{2,14},{6,2},{... | collective-permute-start | bytes 983048 | tf_op jit(solution)/shard_map/ppermute | solution.py:536
  262.0 27.8 %collective-permute-start.45 = (bf16[640,256]{1,0:T(8,128)(2,1)S(1)}, bf16[640,256]{1,0:T(8,128)(2,1)S(1)}, u32[]{:S(2)}, u32[]{:S(2)}) collective-permute-start(bf16[640,256]{1,0:T(8,128)(2,1)S(1)} %get-tuple-element.283), channel_id=1, source_target_pairs={{0,8},{4,12},{8,0},{12,4},{1,9},{5,13},{9,1},{13,5},{2,10},{6,14},... | collective-permute-start | bytes 983048 | tf_op jit(solution)/shard_map/ppermute | solution.py:536
  262.0 27.8 %collective-permute-start.44 = (bf16[640,256]{1,0:T(8,128)(2,1)S(1)}, bf16[640,256]{1,0:T(8,128)(2,1)S(1)}, u32[]{:S(2)}, u32[]{:S(2)}) collective-permute-start(bf16[640,256]{1,0:T(8,128)(2,1)S(1)} %get-tuple-element.284), channel_id=1, source_target_pairs={{0,4},{4,8},{8,12},{12,0},{1,5},{5,9},{9,13},{13,1},{2,6},{6,10},{... | collective-permute-start | bytes 983048 | tf_op jit(solution)/shard_map/ppermute | solution.py:536
  297.8 16.5 %collective-permute-start.47 = (bf16[1024,256]{1,0:T(8,128)(2,1)}, bf16[1024,256]{1,0:T(8,128)(2,1)S(1)}, u32[]{:S(2)}, u32[]{:S(2)}) collective-permute-start(bf16[1024,256]{1,0:T(8,128)(2,1)} %get-tuple-element.217), channel_id=1, source_target_pairs={{0,1},{1,0},{2,3},{3,2},{4,5},{5,4},{6,7},{7,6},{8,9},{9,8},{10,11... | collective-permute-start | bytes 1572872 | tf_op jit(solution)/shard_map/ppermute | solution.py:458
  298.1 25.6 %collective-permute-start.48 = (bf16[1024,256]{1,0:T(8,128)(2,1)}, bf16[1024,256]{1,0:T(8,128)(2,1)}, u32[]{:S(2)}, u32[]{:S(2)}) collective-permute-start(bf16[1024,256]{1,0:T(8,128)(2,1)} %get-tuple-element.218), channel_id=1, source_target_pairs={{0,2},{1,3},{2,0},{3,1},{4,6},{5,7},{6,4},{7,5},{8,10},{9,11},{10,... | collective-permute-start | bytes 1572872 | tf_op jit(solution)/shard_map/ppermute | solution.py:458
  299.2 24.4 %collective-permute-start.49 = (bf16[1024,256]{1,0:T(8,128)(2,1)}, bf16[1024,256]{1,0:T(8,128)(2,1)}, u32[]{:S(2)}, u32[]{:S(2)}) collective-permute-start(bf16[1024,256]{1,0:T(8,128)(2,1)} %get-tuple-element.219), channel_id=1, source_target_pairs={{0,3},{1,2},{2,1},{3,0},{4,7},{5,6},{6,5},{7,4},{8,11},{9,10},{10,... | collective-permute-start | bytes 1572872 | tf_op jit(solution)/shard_map/ppermute | solution.py:458
  309.9 14.1 %collective-permute-start.51 = (bf16[256,896]{1,0:T(8,128)(2,1)}, bf16[256,896]{1,0:T(8,128)(2,1)}, u32[]{:S(2)}, u32[]{:S(2)}) collective-permute-start(bf16[256,896]{1,0:T(8,128)(2,1)} %add_convert_fusion.9), channel_id=1, source_target_pairs={{0,4},{4,8},{8,12},{12,0},{1,5},{5,9},{9,13},{13,1},{2,6},{6,10},{... | collective-permute-start | bytes 1376264 | tf_op jit(solution)/shard_map/ppermute | solution.py:516
  329.8 14.2 %collective-permute-start.60 = (bf16[256,896]{1,0:T(8,128)(2,1)}, bf16[256,896]{1,0:T(8,128)(2,1)}, u32[]{:S(2)}, u32[]{:S(2)}) collective-permute-start(bf16[256,896]{1,0:T(8,128)(2,1)} %add_convert_fusion.7), channel_id=1, source_target_pairs={{0,4},{4,8},{8,12},{12,0},{1,5},{5,9},{9,13},{13,1},{2,6},{6,10},{... | collective-permute-start | bytes 1376264 | tf_op jit(solution)/shard_map/ppermute | solution.py:516
  337.0 19.8 %collective-permute-start.55 = (f32[1024,256]{1,0:T(8,128)S(1)}, f32[1024,256]{1,0:T(8,128)}, u32[]{:S(2)}, u32[]{:S(2)}) collective-permute-start(f32[1024,256]{1,0:T(8,128)S(1)} %get-tuple-element.281), channel_id=1, source_target_pairs={{0,16},{16,0},{1,17},{17,1},{2,18},{18,2},{3,19},{19,3},{4,20},{20... | collective-permute-start | bytes 3145736 | tf_op jit(solution)/shard_map/ppermute | solution.py:458
  337.0 19.7 %collective-permute-start.59 = (f32[17152]{0:T(1024)S(1)}, f32[17152]{0:T(1024)S(1)}, u32[]{:S(2)}, u32[]{:S(2)}) collective-permute-start(f32[17152]{0:T(1024)S(1)} %select_add_fusion), channel_id=1, source_target_pairs={{0,12},{4,0},{8,4},{12,8},{1,13},{5,1},{9,5},{13,9},{2,14},{6,2},{... | collective-permute-start | bytes 205832 | tf_op jit(solution)/shard_map/ppermute | solution.py:527
  339.4 18.9 %collective-permute-start.58 = (f32[17152]{0:T(1024)S(1)}, f32[17152]{0:T(1024)S(1)}, u32[]{:S(2)}, u32[]{:S(2)}) collective-permute-start(f32[17152]{0:T(1024)S(1)} %select_add_fusion), channel_id=1, source_target_pairs={{0,8},{4,12},{8,0},{12,4},{1,9},{5,13},{9,1},{13,5},{2,10},{6,14},... | collective-permute-start | bytes 205832 | tf_op jit(solution)/shard_map/ppermute | solution.py:527
  340.2 18.2 %collective-permute-start.57 = (f32[17152]{0:T(1024)S(1)}, f32[17152]{0:T(1024)S(1)}, u32[]{:S(2)}, u32[]{:S(2)}) collective-permute-start(f32[17152]{0:T(1024)S(1)} %select_add_fusion), channel_id=1, source_target_pairs={{0,4},{4,8},{8,12},{12,0},{1,5},{5,9},{9,13},{13,1},{2,6},{6,10},{... | collective-permute-start | bytes 205832 | tf_op jit(solution)/shard_map/ppermute | solution.py:527
  (109 other events, 1041.2 us)

commit v2 on v1

--- a/solution.py
+++ b/solution.py
@@ -176,12 +176,16 @@
     hcat[:, 0:LANES] = attended.astype(BF16)
 
     wait_weights(tile, mine, w_in, w_out, sems, (3,))
-    for c in range(4):
-        cols = slice(c * LANES, (c + 1) * LANES)
-        up = dot_nn(tokens, w_in[:, (3 + c) * LANES:(4 + c) * LANES])
+
+    def hidden_units(c, _):
+        at = lambda k: pl.ds(pl.multiple_of((2 * c + k) * LANES, LANES), 2 * LANES)
+        up = dot_nn(tokens, w_in[:, at(3)])
         cdf = 0.5 * (1.0 + lax.erf(up * RSQRT2))
-        hcat[:, (1 + c) * LANES:(2 + c) * LANES] = (up * cdf).astype(BF16)
-        dgelu[:, cols] = (cdf + up * (RSQRT2PI * jnp.exp(-0.5 * up * up))).astype(BF16)
+        hcat[:, at(1)] = (up * cdf).astype(BF16)
+        dgelu[:, at(0)] = (cdf + up * (RSQRT2PI * jnp.exp(-0.5 * up * up))).astype(BF16)
+        return _
+
+    lax.fori_loop(0, 2, hidden_units, 0)
 
     wait_weights(tile, mine, w_in, w_out, sems, (4, 5))
     hidden = hcat[...]
@@ -214,14 +218,15 @@
     refs = list(refs)
     take = lambda n: [refs.pop(0) for _ in range(n)]
     meta, = take(1)
-    grad, normed, rq, rk, qf_i, kf_i, v_i, att_i, dgelu, invz, prior_s, prior_k, gain, bias, mix_hi, cos_t, sin_t = take(17)
+    pieces = take(5)
+    normed, rq, rk, qf_i, kf_i, v_i, att_i, dgelu, invz, prior_s, prior_k, gain, bias, mix_hi, cos_t, sin_t = take(16)
     mine, other = take(4), take(4)
     if carried:
         state_in, gsum_in, dmix_in, fsum_in = take(4)
         take(2)
     parts = take(5 if phased else 4)
     stats, dcat, state, gsum, dmix, fsum = take(6)
-    w_in, w_out, sems = take(3)
+    w_in, w_out, sems, grad = take(4)
     step = pl.program_id(0)
     rank = meta[0]
 
@@ -240,6 +245,7 @@
             fsum[...] = jnp.zeros_like(fsum)
 
     wait_weights(step, mine, w_in, w_out, sems, (4, 5))
+    assemble(rank, pieces, grad)
     g = grad[...]
     d_att = dot_nt(g, w_out[0:LANES, :]).astype(BF16).astype(F32)
     square = (TILE, TILE)
@@ -292,10 +298,14 @@
         dr = dot_nt(dl, mix_hi[...])
         dcat[:, c * LANES:(c + 1) * LANES] = (dr * cosine - partner(dr) * sine).astype(BF16)
     dcat[:, 2 * LANES:3 * LANES] = d_v.astype(BF16)
-    for c in range(4):
-        cols = slice(c * LANES, (c + 1) * LANES)
-        d_act = dot_nt(g, w_out[(1 + c) * LANES:(2 + c) * LANES, :])
-        dcat[:, (3 + c) * LANES:(4 + c) * LANES] = (d_act * dgelu[:, cols].astype(F32)).astype(BF16)
+
+    def hidden_units(c, _):
+        at = lambda k: pl.ds(pl.multiple_of((c + k) * LANES, LANES), LANES)
+        d_act = dot_nt(g, w_out[at(1), :])
+        dcat[:, at(3)] = (d_act * dgelu[:, at(0)].astype(F32)).astype(BF16)
+        return _
+
+    lax.fori_loop(0, 4, hidden_units, 0)
     wait_weights(step, mine, w_in, w_out, sems, (0, 1, 2, 3))
     wide = dcat[...]
     row = iota((8, LANES), 0)
@@ -313,17 +323,25 @@
     stats[...] = totals[0] + totals[1] + totals[2] + totals[3]
 
 
+def assemble(rank, pieces, whole):
+    half = LANES // 2
+    for r in range(3):
+        whole[:, pl.ds(pl.multiple_of((rank ^ r) * LANES, LANES), LANES)] = pieces[r][...]
+    at = pl.multiple_of((rank ^ 3) * LANES, LANES)
+    whole[:, pl.ds(at, half)] = pieces[3][...]
+    whole[:, pl.ds(pl.multiple_of(at + half, half), half)] = pieces[4][...]
+
+
 def product_kernel(which, left, right, out):
     out[...] = dot_tn(left[...], right[...]).astype(BF16)
 
 
-def join_kernel(meta, p0, p1, p2, p3a, p3b, whole):
-    half = LANES // 2
-    for r, piece in enumerate((p0, p1, p2)):
-        whole[:, pl.ds(pl.multiple_of((meta[0] ^ r) * LANES, LANES), LANES)] = piece[...]
-    at = pl.multiple_of((meta[0] ^ 3) * LANES, LANES)
-    whole[:, pl.ds(at, half)] = p3a[...]
-    whole[:, pl.ds(pl.multiple_of(at + half, half), half)] = p3b[...]
+def product_pieces_kernel(which, left, p0, p1, p2, p3a, p3b, out, right):
+    @pl.when(pl.program_id(0) == 0)
+    def _():
+        assemble(which[1], (p0, p1, p2, p3a, p3b), right)
+
+    out[...] = dot_tn(left[...], right[...]).astype(BF16)
 
 
 def partial_outs(rows, phased, row_of):
@@ -397,8 +415,8 @@
     return outs[:count], outs[count:count + SAVED], outs[count + SAVED:]
 
 
-def backward_layer(meta, grad, saved, weights, tables, length, first_row, phased, carry=None):
-    rows = grad.shape[0]
+def backward_layer(meta, pieces, saved, weights, tables, length, first_row, phased, carry=None):
+    rows = pieces[0].shape[0]
     tiles, before = rows // TILE, first_row // TILE
     half, width = LANES // 2, 4 * LANES
     local = lambda t, *_: tiles - 1 - t
@@ -412,9 +430,9 @@
     states = [(LANES, LANES), (8, LANES)] * 2
     shapes += [jax.ShapeDtypeStruct(s, F32) for s in states]
     specs += [fixed(s) for s in states]
-    operands = [meta, grad, normed, rq, rk, qf, kf, value, attended, dgelu, invz, prior_s, prior_k, gain, bias, mix_hi, *tables,
+    operands = [meta, *pieces, normed, rq, rk, qf, kf, value, attended, dgelu, invz, prior_s, prior_k, gain, bias, mix_hi, *tables,
                 *mine, *other]
-    in_specs = [by_row(width, local), by_row(width)] + [by_row(LANES)] * 6 + [by_row(width), by_row(LANES)] + [
+    in_specs = [by_row(p.shape[1], local) for p in pieces] + [by_row(width)] + [by_row(LANES)] * 6 + [by_row(width), by_row(LANES)] + [
         pl.BlockSpec((1, n, LANES), lambda *i: (there(*i), 0, 0)) for n in (LANES, 8)] + [
         fixed(w.shape) for w in (gain, bias, mix_hi)] + [by_row(half)] * 2 + outside(8)
     aliases = {}
@@ -428,30 +446,14 @@
         name="layer_backward",
         out_shape=shapes,
         grid_spec=pltpu.PrefetchScalarGridSpec(
-            num_scalar_prefetch=1, grid=(tiles,), in_specs=in_specs, out_specs=specs, scratch_shapes=weight_scratch(width)),
+            num_scalar_prefetch=1, grid=(tiles,), in_specs=in_specs, out_specs=specs,
+            scratch_shapes=weight_scratch(width) + [pltpu.VMEM((TILE, width), BF16)]),
         input_output_aliases=aliases,
         compiler_params=params(56),
         cost_estimate=pl.CostEstimate(flops=rows * 25_000_000, transcendentals=0, bytes_accessed=24 << 20),
     )(*operands)
     count = 5 if phased else 4
     return outs[:count], outs[count:count + 2], outs[count + 2:]
-
-
-def join(meta, pieces):
-    rows, block = pieces[0].shape[0], 2 * TILE
-    return pl.pallas_call(
-        join_kernel,
-        name="join",
-        out_shape=jax.ShapeDtypeStruct((rows, 4 * LANES), BF16),
-        grid_spec=pltpu.PrefetchScalarGridSpec(
-            num_scalar_prefetch=1,
-            grid=(rows // block,),
-            in_specs=[pl.BlockSpec((block, p.shape[1]), lambda i, *_: (i, 0)) for p in pieces],
-            out_specs=pl.BlockSpec((block, 4 * LANES), lambda i, *_: (i, 0)),
-        ),
-        compiler_params=params(8),
-        cost_estimate=pl.CostEstimate(flops=0, transcendentals=0, bytes_accessed=rows * 16 * LANES),
-    )(meta, *pieces)
 
 
 def swap(value, axis, by):
@@ -543,26 +545,32 @@
     return total.astype(BF16)
 
 
-def weight_gradient(left, right, cut_left, section):
-    rows = left.shape[0]
-    m, n = left.shape[1] // (2 if cut_left else 1), right.shape[1] // (1 if cut_left else 2)
-    block = 128 if cut_left else 256
+def weight_gradient(left, rights, section, place):
+    rows, block = left.shape[0], 128
+    whole = len(rights) == 1
+    m = left.shape[1] // (1 if whole else 2)
+    n = rights[0].shape[1] // 2 if whole else 4 * LANES
     steps = m // block
-    left_at = (lambda i, which: (0, which[0] * steps + i)) if cut_left else (lambda i, which: (0, i))
-    right_at = (lambda i, which: (0, 0)) if cut_left else (lambda i, which: (0, which[0]))
+    if whole:
+        left_at = lambda i, which: (0, i)
+        right_specs = [pl.BlockSpec((rows, n), lambda i, which: (0, which[0]))]
+    else:
+        left_at = lambda i, which: (0, which[0] * steps + i)
+        right_specs = [fixed(p.shape) for p in rights]
 
     def product(which):
         return pl.pallas_call(
-            product_kernel,
+            product_kernel if whole else product_pieces_kernel,
             name="weight_gradient",
             out_shape=jax.ShapeDtypeStruct((m, n), BF16),
             grid_spec=pltpu.PrefetchScalarGridSpec(
                 num_scalar_prefetch=1, grid=(steps,),
-                in_specs=[pl.BlockSpec((rows, block), left_at), pl.BlockSpec((rows, n), right_at)],
-                out_specs=pl.BlockSpec((block, n), lambda i, which: (i, 0))),
+                in_specs=[pl.BlockSpec((rows, block), left_at)] + right_specs,
+                out_specs=pl.BlockSpec((block, n), lambda i, which: (i, 0)),
+                scratch_shapes=[] if whole else [pltpu.VMEM((rows, n), BF16)]),
             compiler_params=params(20),
             cost_estimate=pl.CostEstimate(flops=2 * rows * m * n, transcendentals=0, bytes_accessed=2 * (rows * (m + n) + m * n)),
-        )(which.reshape(1).astype(jnp.int32), left, right)
+        )(jnp.stack([which, place]).astype(jnp.int32), left, *rights)
 
     arrived = swap(product(1 - section), "section", 1)
     return product(section), arrived
@@ -670,14 +678,13 @@
         return jnp.concatenate([gain_part, bias_part, fsum[0], diagonal.reshape(-1)])
 
     saved1, saved0 = saved_of(all1), saved_of(all0)
-    grad1 = join(metas[1], pieces_g)
-    out_blocks1 = block_sends(out_block(*weight_gradient(saved1[6], grad1, True, section)), "dp")
-    grad1_b = after(grad1, out_blocks1[0])
+    out_blocks1 = block_sends(out_block(*weight_gradient(saved1[6], pieces_g, section, place)), "dp")
+    grad1_b = after(pieces_g, out_blocks1[0])
     parts, stats, dcat1, dmix1, fsum1 = run_backward(metas[1], grad1_b, saved1, weights1, True)
     parts, stats, dcat1, dmix1, fsum1 = after((parts, stats, dcat1, dmix1, fsum1), *out_blocks1, *out_sent)
     arrived = scatter_start(parts)
     turn = scatter_turn(parts, arrived)
-    steps1 = list(ring_scatter(in_block(*weight_gradient(saved1[0], dcat1, False, section)), "dp"))
+    steps1 = list(ring_scatter(in_block(*weight_gradient(saved1[0], (dcat1,), section, place)), "dp"))
     arrivals1, red_in1 = [arrival for arrival, _ in steps1], steps1[-1][1]
     d_normed = scatter_end(parts, arrived, *turn)
     sums = mp_total(after(stats, *turn))
@@ -687,14 +694,13 @@
     pieces_g0 = after(pieces_g0, *arrivals1[2:3])
     out = hidden.astype(F32) + out_kept + out_sent[0].astype(F32) + out_sent[1].astype(F32) + out_sent[2].astype(F32)
 
-    grad0 = join(metas[0], pieces_g0)
-    out_blocks0 = block_sends(out_block(*weight_gradient(saved0[6], grad0, True, section)), "dp")
-    grad0_b = after(grad0, out_blocks0[0])
+    out_blocks0 = block_sends(out_block(*weight_gradient(saved0[6], pieces_g0, section, place)), "dp")
+    grad0_b = after(pieces_g0, out_blocks0[0])
     parts, stats, dcat0, dmix0, fsum0 = run_backward(metas[0], grad0_b, saved0, weights0, False)
     parts, stats, dcat0, dmix0, fsum0 = after((parts, stats, dcat0, dmix0, fsum0), *out_blocks0)
     out_blocks1 = after(out_blocks1, dcat0)
     kept, sent = direct_sends(parts)
-    mine0, arrived0 = weight_gradient(saved0[0], dcat0, False, section)
+    mine0, arrived0 = weight_gradient(saved0[0], (dcat0,), section, place)
     block0 = in_block(mine0, arrived0)
     meanwhile = list(sent)
     ring0 = ring_scatter(block0, "dp", meanwhile)

time: 374 us -> 375 us (level); the launches traced: 368 us -> 373 us
  Pallas kernels: 137 us -> 147 us
  waiting for transfers between devices: 92.6 us -> 87.3 us
    pallas_call x2, Pallas kernels: 52.9 us -> 60.7 us  [backward_layer(): pl.pallas_call(functools.partial(backward_kernel, carry is not None, phas...]
    ppermute x49, waiting for transfers between devices: 62 us -> 56.3 us  [swap(): lax.ppermute(value, axis, [(k, k ^ by) for k in range(lax.axis_size(axis))])]
    unnamed x155 -> x157, local copies, waits for them, and re-layouts: 14.6 us -> 15.1 us
    pallas_call x10 -> x8, Pallas kernels: 39.1 us -> 39.4 us  [product(): pl.pallas_call(product_kernel if whole else product_pieces_kernel, name='...]
  transfers between devices with their start and end apart: 64 -> 64, of which waited for: 27 -> 23; matrix products, arithmetic and copies ran while one was open for 13% -> 13% of each run, Pallas kernels for 30% -> 34%
where the time goes in v2:
time: 375 us; the launch traced here: 373 us
  Pallas kernels  147 us (39%)
  waiting for transfers between devices  87.3 us (23%)
  starting transfers between devices  65.2 us (17%)
  other arithmetic  37.2 us (10%)
  local copies, waits for them, and re-layouts  33.5 us (9%)
    pallas_call x2, Pallas kernels, backward_layer(): pl.pallas_call(functools.partial(backward_kernel, carry is not None, phas...  60.7 us
    ppermute x49, waiting for transfers between devices, swap(): lax.ppermute(value, axis, [(k, k ^ by) for k in range(lax.axis_size(axis))])  56.3 us
    ppermute x49, starting transfers between devices, swap(): lax.ppermute(value, axis, [(k, k ^ by) for k in range(lax.axis_size(axis))])  47 us
    pallas_call x2, Pallas kernels, forward_layer(): pl.pallas_call(functools.partial(forward_kernel, carry is not None, phase...  46.4 us
    pallas_call x8, Pallas kernels, product(): pl.pallas_call(product_kernel if whole else product_pieces_kernel, name='...  39.4 us
    ppermute x6, waiting for transfers between devices, ring_scatter(): arrived = lax.ppermute(total, axis, pairs)  29.5 us
    unnamed x157, local copies, waits for them, and re-layouts  15.1 us
  transfers between devices with their start and end apart: 64, of which 23 were waited for; matrix products, arithmetic and copies ran while one was open for 13% of the time, Pallas kernels for 34%

profile of v2, /device:TPU:0, one launch (start us, length us, event | category | flops | bytes accessed | tf_op | source)
XLA Modules:
  0.0 373.2 jit_solution(15722338275162833974)
XLA Ops:
  1.9 3.1 collective-permute-start.2
  11.4 2.8 multiply_select_fusion
  20.7 4.4 %collective-permute-done.3.refs_6_ = bf16[1024,128]{1,0:T(8,128)(2,1)S(1)} collective-permute-done((bf16[1024,128]{1,0:T(8,128)(2,1)S(1)}, bf16[1024,128]{1,0:T(8,128)(2,1)S(1)}, u32[]{:S(2)}, u32[]{:S(2)}) %collective-permute-start.3) | collective-permute-done | bytes 262176 | tf_op jit(solution)/shard_map/ppermute | solution.py:460
  28.2 4.3 %collective-permute-done.1.refs_5_ = bf16[1024,128]{1,0:T(8,128)(2,1)} collective-permute-done((bf16[1024,128]{1,0:T(8,128)(2,1)S(1)}, bf16[1024,128]{1,0:T(8,128)(2,1)}, u32[]{:S(2)}, u32[]{:S(2)}) %collective-permute-start.1) | collective-permute-done | bytes 262176 | tf_op jit(solution)/shard_map/ppermute | solution.py:460
  34.1 23.4 %layer_forward.2 = (bf16[2,1024,128]{2,1,0:T(8,128)(2,1)}, bf16[2,1024,128]{2,1,0:T(8,128)(2,1)}, f32[1024,256]{1,0:T(8,128)}, f32[1024,128]{1,0:T(8,128)}, f32[...) custom-call(s32[2]{0:T(128)} %pad_add_fusion.2.refs_0_, ...), custom_call_target="tpu_custom_call" | custom-call | flops 20480000000 | bytes 25165824 | tf_op jit(solution)/shard_map/layer_forward/pallas_call | solution.py:404
  60.2 8.8 %collective-permute-done.11 = bf16[2,1024,128]{2,1,0:T(8,128)(2,1)S(1)} collective-permute-done((bf16[2,1024,128]{2,1,0:T(8,128)(2,1)}, bf16[2,1024,128]{2,1,0:T(8,128)(2,1)S(1)}, u32[]{:S(2)}, u32[]{:S(2)}) %collective-permute-start.11) | collective-permute-done | bytes 524320 | tf_op jit(solution)/shard_map/ppermute | solution.py:460
  76.6 4.0 %collective-permute-done.14 = bf16[1024,128]{1,0:T(8,128)(2,1)S(1)} collective-permute-done((bf16[1024,128]{1,0:T(8,128)(2,1)S(1)}, bf16[1024,128]{1,0:T(8,128)(2,1)S(1)}, u32[]{:S(2)}, u32[]{:S(2)}) %collective-permute-start.14) | collective-permute-done | bytes 262176 | tf_op jit(solution)/shard_map/ppermute | solution.py:460
  82.5 8.2 %collective-permute-done.16.refs_4_ = bf16[1024,256]{1,0:T(8,128)(2,1)} collective-permute-done((bf16[1024,256]{1,0:T(8,128)(2,1)S(1)}, bf16[1024,256]{1,0:T(8,128)(2,1)}, u32[]{:S(2)}, u32[]{:S(2)}) %collective-permute-start.16) | collective-permute-done | bytes 524320 | tf_op jit(solution)/shard_map/ppermute | solution.py:460
  100.3 2.4 collective-permute-done.17.refs_5_
  104.1 23.0 %layer_forward.3 = (f32[1024,256]{1,0:T(8,128)}, bf16[1024,256]{1,0:T(8,128)(2,1)}, bf16[1024,256]{1,0:T(8,128)(2,1)}, bf16[1024,256]{1,0:T(8,128)(2,1)}, bf16[1...) custom-call(s32[2]{0:T(128)} %pad_add_fusion.refs_0_, ...), custom_call_target="tpu_custom_call" | custom-call | flops 20480000000 | bytes 25165824 | tf_op jit(solution)/shard_map/layer_forward/pallas_call | solution.py:404
  129.0 4.6 %weight_gradient.9 = bf16[640,1024]{1,0:T(8,128)(2,1)} custom-call(s32[2]{0:T(128)S(1)} %pad_add_fusion.4.which, bf16[1024,1280]{1,0:T(8,128)(2,1)S(1)} %copy-done.7, bf16[1024,256]{1,0:T(8,128)(2,1)S(1)} %dynamic-slice_bitcast_fusion.1.p0.refs_1_, bf16[1024,256]{1,0:T(8,128)(2,1)S(1)} %copy-done.20, bf16[1024,256]{1,0:T(8,128)(2,1)S(1)} %copy-done.17, ...), custom_call_target="tpu_custom_call" | custom-call | flops 1342177280 | bytes 4718592 | tf_op jit(solution)/shard_map/weight_gradient/pallas_call | solution.py:562
  140.3 3.6 weight_gradient.8
  145.8 3.4 collective-permute-start.24
  150.2 30.6 %layer_backward.2 = (bf16[2,1024,128]{2,1,0:T(8,128)(2,1)}, bf16[2,1024,128]{2,1,0:T(8,128)(2,1)}, f32[1024,256]{1,0:T(8,128)}, f32[1024,128]{1,0:T(8,128)}, f32...) custom-call(s32[2]{0:T(128)} %pad_add_fusion.refs_0_, ...), custom_call_target="tpu_custom_call" | custom-call | flops 25600000000 | bytes 25165824 | tf_op jit(solution)/shard_map/layer_backward/pallas_call | solution.py:444
  180.9 2.7 copy-done.4
  183.6 6.2 %weight_gradient.11 = bf16[1024,896]{1,0:T(8,128)(2,1)} custom-call(s32[2]{0:T(128)S(1)} %pad_add_fusion.4.which, bf16[1024,1024]{1,0:T(8,128)(2,1)S(1)} %copy-done.14, bf16[1024,1792]{1,0:T(8,128)(2,1)S(1)} %copy-done.4), custom_call_target="tpu_custom_call" | custom-call | flops 1879048192 | bytes 5767168 | tf_op jit(solution)/shard_map/weight_gradient/pallas_call | solution.py:562
  195.6 5.2 %weight_gradient.10 = bf16[1024,896]{1,0:T(8,128)(2,1)S(1)} custom-call(s32[2]{0:T(128)S(1)} %pad_add_fusion.3.which, bf16[1024,1024]{1,0:T(8,128)(2,1)S(1)} %copy-done.14, bf16[1024,1792]{1,0:T(8,128)(2,1)S(1)} %copy-done.5), custom_call_target="tpu_custom_call" | custom-call | flops 1879048192 | bytes 5767168 | tf_op jit(solution)/shard_map/weight_gradient/pallas_call | solution.py:562
  200.8 3.8 %collective-permute-done.28 = bf16[2,1024,128]{2,1,0:T(8,128)(2,1)} collective-permute-done((bf16[2,1024,128]{2,1,0:T(8,128)(2,1)}, bf16[2,1024,128]{2,1,0:T(8,128)(2,1)}, u32[]{:S(2)}, u32[]{:S(2)}) %collective-permute-start.28) | collective-permute-done | bytes 524320 | tf_op jit(solution)/shard_map/ppermute | solution.py:460
  211.3 2.5 collective-permute-start.36
  216.9 7.4 %collective-permute-done.36 = bf16[256,896]{1,0:T(8,128)(2,1)S(1)} collective-permute-done((bf16[256,896]{1,0:T(8,128)(2,1)S(1)}, bf16[256,896]{1,0:T(8,128)(2,1)S(1)}, u32[]{:S(2)}, u32[]{:S(2)}) %collective-permute-start.36) | collective-permute-done | bytes 458784 | tf_op jit(solution)/shard_map/ppermute | solution.py:518
  230.9 6.8 %collective-permute-done.39 = bf16[256,896]{1,0:T(8,128)(2,1)S(1)} collective-permute-done((bf16[256,896]{1,0:T(8,128)(2,1)S(1)}, bf16[256,896]{1,0:T(8,128)(2,1)S(1)}, u32[]{:S(2)}, u32[]{:S(2)}) %collective-permute-start.39) | collective-permute-done | bytes 458784 | tf_op jit(solution)/shard_map/ppermute | solution.py:518
  243.2 4.9 %collective-permute-done.41.p3b.refs_5_ = bf16[1024,128]{1,0:T(8,128)(2,1)S(1)} collective-permute-done((bf16[1024,128]{1,0:T(8,128)(2,1)S(1)}, bf16[1024,128]{1,0:T(8,128)(2,1)S(1)}, u32[]{:S(2)}, u32[]{:S(2)}) %collective-permute-start.41) | collective-permute-done | bytes 262176 | tf_op jit(solution)/shard_map/ppermute | solution.py:460
  250.2 3.6 weight_gradient.13
  254.0 3.6 weight_gradient.12
  261.4 30.1 %layer_backward.3 = (f32[1024,256]{1,0:T(8,128)}, bf16[1024,256]{1,0:T(8,128)(2,1)}, bf16[1024,256]{1,0:T(8,128)(2,1)}, bf16[1024,256]{1,0:T(8,128)(2,1)}, f32[8...) custom-call(s32[2]{0:T(128)} %pad_add_fusion.2.refs_0_, ...), custom_call_target="tpu_custom_call" | custom-call | flops 25600000000 | bytes 25165824 | tf_op jit(solution)/shard_map/layer_backward/pallas_call | solution.py:444
  293.9 6.2 %weight_gradient.15 = bf16[1024,896]{1,0:T(8,128)(2,1)} custom-call(s32[2]{0:T(128)S(1)} %pad_add_fusion.4.which, bf16[1024,1024]{1,0:T(8,128)(2,1)S(1)} %copy-done.13, bf16[1024,1792]{1,0:T(8,128)(2,1)S(1)} %copy-done.2), custom_call_target="tpu_custom_call" | custom-call | flops 1879048192 | bytes 5767168 | tf_op jit(solution)/shard_map/weight_gradient/pallas_call | solution.py:562
  307.1 6.3 %weight_gradient.14 = bf16[1024,896]{1,0:T(8,128)(2,1)} custom-call(s32[2]{0:T(128)S(1)} %pad_add_fusion.3.which, bf16[1024,1024]{1,0:T(8,128)(2,1)S(1)} %copy-done.13, bf16[1024,1792]{1,0:T(8,128)(2,1)S(1)} %copy-done.3), custom_call_target="tpu_custom_call" | custom-call | flops 1879048192 | bytes 5767168 | tf_op jit(solution)/shard_map/weight_gradient/pallas_call | solution.py:562
  315.4 2.9 collective-permute-start.51
  320.8 7.0 %collective-permute-done.48 = bf16[1024,256]{1,0:T(8,128)(2,1)} collective-permute-done((bf16[1024,256]{1,0:T(8,128)(2,1)}, bf16[1024,256]{1,0:T(8,128)(2,1)}, u32[]{:S(2)}, u32[]{:S(2)}) %collective-permute-start.48) | collective-permute-done | bytes 524320 | tf_op jit(solution)/shard_map/ppermute | solution.py:460
  342.4 2.8 collective-permute-start.59
  346.0 3.0 collective-permute-done.60
  352.3 9.7 %collective-permute-done.61 = bf16[256,896]{1,0:T(8,128)(2,1)S(1)} collective-permute-done((bf16[256,896]{1,0:T(8,128)(2,1)S(1)}, bf16[256,896]{1,0:T(8,128)(2,1)S(1)}, u32[]{:S(2)}, u32[]{:S(2)}) %collective-permute-start.61) | collective-permute-done | bytes 458784 | tf_op jit(solution)/shard_map/ppermute | solution.py:518
  (361 shorter events, 129.7 us)
Async XLA Ops:
  1.9 15.0 %collective-permute-start.2 = (bf16[1024,256]{1,0:T(8,128)(2,1)S(1)}, bf16[1024,256]{1,0:T(8,128)(2,1)S(1)}, u32[]{:S(2)}, u32[]{:S(2)}) collective-permute-start(bf16[1024,256]{1,0:T(8,128)(2,1)S(1)} %dynamic-slice_bitcast_fusion.refs_2_), channel_id=1, source_target_pairs={{0,2},{1,3},{2,0},{3,1},{4,6},{5,7},{6,4},{7,5},{8,10},{9,11},{10,... | collective-permute-start | bytes 1572872 | tf_op jit(solution)/shard_map/ppermute | solution.py:460
  4.9 14.4 %collective-permute-start = (bf16[1024,256]{1,0:T(8,128)(2,1)S(1)}, bf16[1024,256]{1,0:T(8,128)(2,1)}, u32[]{:S(2)}, u32[]{:S(2)}) collective-permute-start(bf16[1024,256]{1,0:T(8,128)(2,1)S(1)} %dynamic-slice_bitcast_fusion.refs_2_), channel_id=1, source_target_pairs={{0,1},{1,0},{2,3},{3,2},{4,5},{5,4},{6,7},{7,6},{8,9},{9,8},{10,11... | collective-permute-start | bytes 1572872 | tf_op jit(solution)/shard_map/ppermute | solution.py:460
  8.9 25.1 %collective-permute-start.6 = (bf16[1,1024,1024]{2,1,0:T(8,128)(2,1)}, bf16[1,1024,1024]{2,1,0:T(8,128)(2,1)}, u32[]{:S(2)}, u32[]{:S(2)}) collective-permute-start(bf16[1,1024,1024]{2,1,0:T(8,128)(2,1)} %refs_23_.3), channel_id=1, source_target_pairs={{0,16},{16,0},{1,17},{17,1},{2,18},{18,2},{3,19},{19,3},{4,20},{20... | collective-permute-start | bytes 6291464 | tf_op jit(solution)/shard_map/ppermute | solution.py:460
  9.4 24.6 %collective-permute-start.8 = (bf16[1,1024,1024]{2,1,0:T(8,128)(2,1)}, bf16[1,1024,1024]{2,1,0:T(8,128)(2,1)}, u32[]{:S(2)}, u32[]{:S(2)}) collective-permute-start(bf16[1,1024,1024]{2,1,0:T(8,128)(2,1)} %refs_25_.3), channel_id=1, source_target_pairs={{0,16},{16,0},{1,17},{17,1},{2,18},{18,2},{3,19},{19,3},{4,20},{20... | collective-permute-start | bytes 6291464 | tf_op jit(solution)/shard_map/ppermute | solution.py:460
  15.6 18.5 %collective-permute-start.5 = (bf16[1,3,1024,256]{3,2,1,0:T(8,128)(2,1)}, bf16[1,3,1024,256]{3,2,1,0:T(8,128)(2,1)}, u32[]{:S(2)}, u32[]{:S(2)}) collective-permute-start(bf16[1,3,1024,256]{3,2,1,0:T(8,128)(2,1)} %refs_22_.3), channel_id=1, source_target_pairs={{0,16},{16,0},{1,17},{17,1},{2,18},{18,2},{3,19},{19,3},{4,20},{20... | collective-permute-start | bytes 4718600 | tf_op jit(solution)/shard_map/ppermute | solution.py:460
  19.4 13.5 %collective-permute-start.7 = (bf16[1,256,1024]{2,1,0:T(8,128)(2,1)}, bf16[1,256,1024]{2,1,0:T(8,128)(2,1)S(1)}, u32[]{:S(2)}, u32[]{:S(2)}) collective-permute-start(bf16[1,256,1024]{2,1,0:T(8,128)(2,1)} %refs_24_.3), channel_id=1, source_target_pairs={{0,16},{16,0},{1,17},{17,1},{2,18},{18,2},{3,19},{19,3},{4,20},{20... | collective-permute-start | bytes 1572872 | tf_op jit(solution)/shard_map/ppermute | solution.py:460
  32.5 25.0 %collective-permute-start.10 = (bf16[1024,256]{1,0:T(8,128)(2,1)S(1)}, bf16[1024,256]{1,0:T(8,128)(2,1)S(1)}, u32[]{:S(2)}, u32[]{:S(2)}) collective-permute-start(bf16[1024,256]{1,0:T(8,128)(2,1)S(1)} %dynamic-slice_bitcast_fusion.1.p0.refs_1_), channel_id=1, source_target_pairs={{0,2},{1,3},{2,0},{3,1},{4,6},{5,7},{6,4},{7,5},{8,10},{9,11},{10,... | collective-permute-start | bytes 1572872 | tf_op jit(solution)/shard_map/ppermute | solution.py:460
  32.8 24.7 %collective-permute-start.9 = (bf16[1024,256]{1,0:T(8,128)(2,1)S(1)}, bf16[1024,256]{1,0:T(8,128)(2,1)S(1)}, u32[]{:S(2)}, u32[]{:S(2)}) collective-permute-start(bf16[1024,256]{1,0:T(8,128)(2,1)S(1)} %dynamic-slice_bitcast_fusion.1.p0.refs_1_), channel_id=1, source_target_pairs={{0,1},{1,0},{2,3},{3,2},{4,5},{5,4},{6,7},{7,6},{8,9},{9,8},{10,11... | collective-permute-start | bytes 1572872 | tf_op jit(solution)/shard_map/ppermute | solution.py:460
  58.5 13.6 %collective-permute-start.13 = (bf16[2,1024,128]{2,1,0:T(8,128)(2,1)}, bf16[2,1024,128]{2,1,0:T(8,128)(2,1)S(1)}, u32[]{:S(2)}, u32[]{:S(2)}) collective-permute-start(bf16[2,1024,128]{2,1,0:T(8,128)(2,1)} %get-tuple-element.149), channel_id=1, source_target_pairs={{0,2},{1,3},{2,0},{3,1},{4,6},{5,7},{6,4},{7,5},{8,10},{9,11},{10,... | collective-permute-start | bytes 1572872 | tf_op jit(solution)/shard_map/ppermute | solution.py:460
  102.8 24.3 %collective-permute-start.20 = (bf16[1024,128]{1,0:T(8,128)(2,1)S(1)}, bf16[1024,128]{1,0:T(8,128)(2,1)S(1)}, u32[]{:S(2)}, u32[]{:S(2)}) collective-permute-start(bf16[1024,128]{1,0:T(8,128)(2,1)S(1)} %slice.192), channel_id=1, source_target_pairs={{0,1},{1,0},{2,3},{3,2},{4,5},{5,4},{6,7},{7,6},{8,9},{9,8},{10,11... | collective-permute-start | bytes 786440 | tf_op jit(solution)/shard_map/ppermute | solution.py:460
  103.8 23.3 %collective-permute-start.19 = (bf16[1024,128]{1,0:T(8,128)(2,1)S(1)}, bf16[1024,128]{1,0:T(8,128)(2,1)S(1)}, u32[]{:S(2)}, u32[]{:S(2)}) collective-permute-start(bf16[1024,128]{1,0:T(8,128)(2,1)S(1)} %slice.191), channel_id=1, source_target_pairs={{0,2},{1,3},{2,0},{3,1},{4,6},{5,7},{6,4},{7,5},{8,10},{9,11},{10,... | collective-permute-start | bytes 786440 | tf_op jit(solution)/shard_map/ppermute | solution.py:460
  133.7 15.4 %collective-permute-start.25 = (bf16[1024,256]{1,0:T(8,128)(2,1)}, bf16[1024,256]{1,0:T(8,128)(2,1)}, u32[]{:S(2)}, u32[]{:S(2)}) collective-permute-start(bf16[1024,256]{1,0:T(8,128)(2,1)} %get-tuple-element.184), channel_id=1, source_target_pairs={{0,1},{1,0},{2,3},{3,2},{4,5},{5,4},{6,7},{7,6},{8,9},{9,8},{10,11... | collective-permute-start | bytes 1572872 | tf_op jit(solution)/shard_map/ppermute | solution.py:460
  134.8 46.1 %collective-permute-start.26 = (bf16[1024,256]{1,0:T(8,128)(2,1)}, bf16[1024,256]{1,0:T(8,128)(2,1)S(1)}, u32[]{:S(2)}, u32[]{:S(2)}) collective-permute-start(bf16[1024,256]{1,0:T(8,128)(2,1)} %get-tuple-element.185), channel_id=1, source_target_pairs={{0,2},{1,3},{2,0},{3,1},{4,6},{5,7},{6,4},{7,5},{8,10},{9,11},{10,... | collective-permute-start | bytes 1572872 | tf_op jit(solution)/shard_map/ppermute | solution.py:460
  136.5 44.3 %collective-permute-start.27 = (bf16[1024,256]{1,0:T(8,128)(2,1)}, bf16[1024,256]{1,0:T(8,128)(2,1)S(1)}, u32[]{:S(2)}, u32[]{:S(2)}) collective-permute-start(bf16[1024,256]{1,0:T(8,128)(2,1)} %get-tuple-element.186), channel_id=1, source_target_pairs={{0,3},{1,2},{2,1},{3,0},{4,7},{5,6},{6,5},{7,4},{8,11},{9,10},{10,... | collective-permute-start | bytes 1572872 | tf_op jit(solution)/shard_map/ppermute | solution.py:460
  145.8 35.1 %collective-permute-start.24 = (bf16[640,256]{1,0:T(8,128)(2,1)S(1)}, bf16[640,256]{1,0:T(8,128)(2,1)S(1)}, u32[]{:S(2)}, u32[]{:S(2)}) collective-permute-start(bf16[640,256]{1,0:T(8,128)(2,1)S(1)} %get-tuple-element.302), channel_id=1, source_target_pairs={{0,12},{4,0},{8,4},{12,8},{1,13},{5,1},{9,5},{13,9},{2,14},{6,2},{... | collective-permute-start | bytes 983048 | tf_op jit(solution)/shard_map/ppermute | solution.py:538
  149.1 31.8 %collective-permute-start.23 = (bf16[640,256]{1,0:T(8,128)(2,1)S(1)}, bf16[640,256]{1,0:T(8,128)(2,1)S(1)}, u32[]{:S(2)}, u32[]{:S(2)}) collective-permute-start(bf16[640,256]{1,0:T(8,128)(2,1)S(1)} %get-tuple-element.303), channel_id=1, source_target_pairs={{0,8},{4,12},{8,0},{12,4},{1,9},{5,13},{9,1},{13,5},{2,10},{6,14},... | collective-permute-start | bytes 983048 | tf_op jit(solution)/shard_map/ppermute | solution.py:538
  149.1 31.8 %collective-permute-start.22 = (bf16[640,256]{1,0:T(8,128)(2,1)S(1)}, bf16[640,256]{1,0:T(8,128)(2,1)S(1)}, u32[]{:S(2)}, u32[]{:S(2)}) collective-permute-start(bf16[640,256]{1,0:T(8,128)(2,1)S(1)} %get-tuple-element.304), channel_id=1, source_target_pairs={{0,4},{4,8},{8,12},{12,0},{1,5},{5,9},{9,13},{13,1},{2,6},{6,10},{... | collective-permute-start | bytes 983048 | tf_op jit(solution)/shard_map/ppermute | solution.py:538
  189.9 20.3 %collective-permute-start.35 = (bf16[1024,896]{1,0:T(8,128)(2,1)}, bf16[1024,896]{1,0:T(8,128)(2,1)}, u32[]{:S(2)}, u32[]{:S(2)}) collective-permute-start(bf16[1024,896]{1,0:T(8,128)(2,1)} %weight_gradient.11), channel_id=1, source_target_pairs={{0,16},{16,0},{1,17},{17,1},{2,18},{18,2},{3,19},{19,3},{4,20},{20... | collective-permute-start | bytes 5505032 | tf_op jit(solution)/shard_map/ppermute | solution.py:460
  189.9 14.6 %collective-permute-start.28 = (bf16[2,1024,128]{2,1,0:T(8,128)(2,1)}, bf16[2,1024,128]{2,1,0:T(8,128)(2,1)}, u32[]{:S(2)}, u32[]{:S(2)}) collective-permute-start(bf16[2,1024,128]{2,1,0:T(8,128)(2,1)} %get-tuple-element.188), channel_id=1, source_target_pairs={{0,1},{1,0},{2,3},{3,2},{4,5},{5,4},{6,7},{7,6},{8,9},{9,8},{10,11... | collective-permute-start | bytes 1572872 | tf_op jit(solution)/shard_map/ppermute | solution.py:460
  191.0 14.6 %collective-permute-start.30 = (bf16[2,1024,128]{2,1,0:T(8,128)(2,1)}, bf16[2,1024,128]{2,1,0:T(8,128)(2,1)}, u32[]{:S(2)}, u32[]{:S(2)}) collective-permute-start(bf16[2,1024,128]{2,1,0:T(8,128)(2,1)} %get-tuple-element.190), channel_id=1, source_target_pairs={{0,2},{1,3},{2,0},{3,1},{4,6},{5,7},{6,4},{7,5},{8,10},{9,11},{10,... | collective-permute-start | bytes 1572872 | tf_op jit(solution)/shard_map/ppermute | solution.py:460
  258.4 33.2 %collective-permute-start.46 = (bf16[640,256]{1,0:T(8,128)(2,1)S(1)}, bf16[640,256]{1,0:T(8,128)(2,1)S(1)}, u32[]{:S(2)}, u32[]{:S(2)}) collective-permute-start(bf16[640,256]{1,0:T(8,128)(2,1)S(1)} %get-tuple-element.298), channel_id=1, source_target_pairs={{0,12},{4,0},{8,4},{12,8},{1,13},{5,1},{9,5},{13,9},{2,14},{6,2},{... | collective-permute-start | bytes 983048 | tf_op jit(solution)/shard_map/ppermute | solution.py:538
  260.8 30.8 %collective-permute-start.45 = (bf16[640,256]{1,0:T(8,128)(2,1)S(1)}, bf16[640,256]{1,0:T(8,128)(2,1)S(1)}, u32[]{:S(2)}, u32[]{:S(2)}) collective-permute-start(bf16[640,256]{1,0:T(8,128)(2,1)S(1)} %get-tuple-element.299), channel_id=1, source_target_pairs={{0,8},{4,12},{8,0},{12,4},{1,9},{5,13},{9,1},{13,5},{2,10},{6,14},... | collective-permute-start | bytes 983048 | tf_op jit(solution)/shard_map/ppermute | solution.py:538
  260.8 30.8 %collective-permute-start.44 = (bf16[640,256]{1,0:T(8,128)(2,1)S(1)}, bf16[640,256]{1,0:T(8,128)(2,1)S(1)}, u32[]{:S(2)}, u32[]{:S(2)}) collective-permute-start(bf16[640,256]{1,0:T(8,128)(2,1)S(1)} %get-tuple-element.300), channel_id=1, source_target_pairs={{0,4},{4,8},{8,12},{12,0},{1,5},{5,9},{9,13},{13,1},{2,6},{6,10},{... | collective-permute-start | bytes 983048 | tf_op jit(solution)/shard_map/ppermute | solution.py:538
  301.6 19.3 %collective-permute-start.47 = (bf16[1024,256]{1,0:T(8,128)(2,1)}, bf16[1024,256]{1,0:T(8,128)(2,1)S(1)}, u32[]{:S(2)}, u32[]{:S(2)}) collective-permute-start(bf16[1024,256]{1,0:T(8,128)(2,1)} %get-tuple-element.233), channel_id=1, source_target_pairs={{0,1},{1,0},{2,3},{3,2},{4,5},{5,4},{6,7},{7,6},{8,9},{9,8},{10,11... | collective-permute-start | bytes 1572872 | tf_op jit(solution)/shard_map/ppermute | solution.py:460
  302.3 25.6 %collective-permute-start.48 = (bf16[1024,256]{1,0:T(8,128)(2,1)}, bf16[1024,256]{1,0:T(8,128)(2,1)}, u32[]{:S(2)}, u32[]{:S(2)}) collective-permute-start(bf16[1024,256]{1,0:T(8,128)(2,1)} %get-tuple-element.234), channel_id=1, source_target_pairs={{0,2},{1,3},{2,0},{3,1},{4,6},{5,7},{6,4},{7,5},{8,10},{9,11},{10,... | collective-permute-start | bytes 1572872 | tf_op jit(solution)/shard_map/ppermute | solution.py:460
  303.4 24.5 %collective-permute-start.49 = (bf16[1024,256]{1,0:T(8,128)(2,1)}, bf16[1024,256]{1,0:T(8,128)(2,1)}, u32[]{:S(2)}, u32[]{:S(2)}) collective-permute-start(bf16[1024,256]{1,0:T(8,128)(2,1)} %get-tuple-element.235), channel_id=1, source_target_pairs={{0,3},{1,2},{2,1},{3,0},{4,7},{5,6},{6,5},{7,4},{8,11},{9,10},{10,... | collective-permute-start | bytes 1572872 | tf_op jit(solution)/shard_map/ppermute | solution.py:460
  315.4 14.2 %collective-permute-start.51 = (bf16[256,896]{1,0:T(8,128)(2,1)}, bf16[256,896]{1,0:T(8,128)(2,1)}, u32[]{:S(2)}, u32[]{:S(2)}) collective-permute-start(bf16[256,896]{1,0:T(8,128)(2,1)} %add_convert_fusion.9), channel_id=1, source_target_pairs={{0,4},{4,8},{8,12},{12,0},{1,5},{5,9},{9,13},{13,1},{2,6},{6,10},{... | collective-permute-start | bytes 1376264 | tf_op jit(solution)/shard_map/ppermute | solution.py:518
  335.3 13.7 %collective-permute-start.60 = (bf16[256,896]{1,0:T(8,128)(2,1)}, bf16[256,896]{1,0:T(8,128)(2,1)}, u32[]{:S(2)}, u32[]{:S(2)}) collective-permute-start(bf16[256,896]{1,0:T(8,128)(2,1)} %add_convert_fusion.7), channel_id=1, source_target_pairs={{0,4},{4,8},{8,12},{12,0},{1,5},{5,9},{9,13},{13,1},{2,6},{6,10},{... | collective-permute-start | bytes 1376264 | tf_op jit(solution)/shard_map/ppermute | solution.py:518
  342.2 19.8 %collective-permute-start.55 = (f32[1024,256]{1,0:T(8,128)S(1)}, f32[1024,256]{1,0:T(8,128)S(1)}, u32[]{:S(2)}, u32[]{:S(2)}) collective-permute-start(f32[1024,256]{1,0:T(8,128)S(1)} %get-tuple-element.297), channel_id=1, source_target_pairs={{0,16},{16,0},{1,17},{17,1},{2,18},{18,2},{3,19},{19,3},{4,20},{20... | collective-permute-start | bytes 3145736 | tf_op jit(solution)/shard_map/ppermute | solution.py:460
  342.4 19.7 %collective-permute-start.59 = (f32[17152]{0:T(1024)S(1)}, f32[17152]{0:T(1024)S(1)}, u32[]{:S(2)}, u32[]{:S(2)}) collective-permute-start(f32[17152]{0:T(1024)S(1)} %select_add_fusion), channel_id=1, source_target_pairs={{0,12},{4,0},{8,4},{12,8},{1,13},{5,1},{9,5},{13,9},{2,14},{6,2},{... | collective-permute-start | bytes 205832 | tf_op jit(solution)/shard_map/ppermute | solution.py:529
  345.2 18.3 %collective-permute-start.58 = (f32[17152]{0:T(1024)S(1)}, f32[17152]{0:T(1024)S(1)}, u32[]{:S(2)}, u32[]{:S(2)}) collective-permute-start(f32[17152]{0:T(1024)S(1)} %select_add_fusion), channel_id=1, source_target_pairs={{0,8},{4,12},{8,0},{12,4},{1,9},{5,13},{9,1},{13,5},{2,10},{6,14},... | collective-permute-start | bytes 205832 | tf_op jit(solution)/shard_map/ppermute | solution.py:529
  345.2 18.3 %collective-permute-start.57 = (f32[17152]{0:T(1024)S(1)}, f32[17152]{0:T(1024)S(1)}, u32[]{:S(2)}, u32[]{:S(2)}) collective-permute-start(f32[17152]{0:T(1024)S(1)} %select_add_fusion), channel_id=1, source_target_pairs={{0,4},{4,8},{8,12},{12,0},{1,5},{5,9},{9,13},{13,1},{2,6},{6,10},{... | collective-permute-start | bytes 205832 | tf_op jit(solution)/shard_map/ppermute | solution.py:529
  (110 other events, 1161.3 us)

commit v3 on v2

--- a/solution.py
+++ b/solution.py
@@ -176,16 +176,12 @@
     hcat[:, 0:LANES] = attended.astype(BF16)
 
     wait_weights(tile, mine, w_in, w_out, sems, (3,))
-
-    def hidden_units(c, _):
-        at = lambda k: pl.ds(pl.multiple_of((2 * c + k) * LANES, LANES), 2 * LANES)
-        up = dot_nn(tokens, w_in[:, at(3)])
+    for c in range(4):
+        cols = slice(c * LANES, (c + 1) * LANES)
+        up = dot_nn(tokens, w_in[:, (3 + c) * LANES:(4 + c) * LANES])
         cdf = 0.5 * (1.0 + lax.erf(up * RSQRT2))
-        hcat[:, at(1)] = (up * cdf).astype(BF16)
-        dgelu[:, at(0)] = (cdf + up * (RSQRT2PI * jnp.exp(-0.5 * up * up))).astype(BF16)
-        return _
-
-    lax.fori_loop(0, 2, hidden_units, 0)
+        hcat[:, (1 + c) * LANES:(2 + c) * LANES] = (up * cdf).astype(BF16)
+        dgelu[:, cols] = (cdf + up * (RSQRT2PI * jnp.exp(-0.5 * up * up))).astype(BF16)
 
     wait_weights(tile, mine, w_in, w_out, sems, (4, 5))
     hidden = hcat[...]
@@ -298,14 +294,10 @@
         dr = dot_nt(dl, mix_hi[...])
         dcat[:, c * LANES:(c + 1) * LANES] = (dr * cosine - partner(dr) * sine).astype(BF16)
     dcat[:, 2 * LANES:3 * LANES] = d_v.astype(BF16)
-
-    def hidden_units(c, _):
-        at = lambda k: pl.ds(pl.multiple_of((c + k) * LANES, LANES), LANES)
-        d_act = dot_nt(g, w_out[at(1), :])
-        dcat[:, at(3)] = (d_act * dgelu[:, at(0)].astype(F32)).astype(BF16)
-        return _
-
-    lax.fori_loop(0, 4, hidden_units, 0)
+    for c in range(4):
+        cols = slice(c * LANES, (c + 1) * LANES)
+        d_act = dot_nt(g, w_out[(1 + c) * LANES:(2 + c) * LANES, :])
+        dcat[:, (3 + c) * LANES:(4 + c) * LANES] = (d_act * dgelu[:, cols].astype(F32)).astype(BF16)
     wait_weights(step, mine, w_in, w_out, sems, (0, 1, 2, 3))
     wide = dcat[...]
     row = iota((8, LANES), 0)
@@ -332,16 +324,27 @@
     whole[:, pl.ds(pl.multiple_of(at + half, half), half)] = pieces[4][...]
 
 
-def product_kernel(which, left, right, out):
-    out[...] = dot_tn(left[...], right[...]).astype(BF16)
-
-
-def product_pieces_kernel(which, left, p0, p1, p2, p3a, p3b, out, right):
-    @pl.when(pl.program_id(0) == 0)
+def product_kernel(steps, meta, left, *refs):
+    *rights, out_other, out_own = refs[:-1] if len(refs) > 3 else refs
+    step = pl.program_id(0)
+    if len(rights) == 1:
+        right = rights[0]
+    else:
+        right = refs[-1]
+
+        @pl.when(step == 0)
+        def _():
+            assemble(meta[1], rights, right)
+
+    product = dot_tn(left[...], right[...]).astype(BF16)
+
+    @pl.when(step < steps)
     def _():
-        assemble(which[1], (p0, p1, p2, p3a, p3b), right)
-
-    out[...] = dot_tn(left[...], right[...]).astype(BF16)
+        out_other[...] = product
+
+    @pl.when(step >= steps)
+    def _():
+        out_own[...] = product
 
 
 def partial_outs(rows, phased, row_of):
@@ -546,34 +549,33 @@
 
 
 def weight_gradient(left, rights, section, place):
-    rows, block = left.shape[0], 128
+    rows = left.shape[0]
     whole = len(rights) == 1
+    block = 256 if whole else 128
     m = left.shape[1] // (1 if whole else 2)
     n = rights[0].shape[1] // 2 if whole else 4 * LANES
     steps = m // block
+    half_at = lambda i, meta: jnp.where(i < steps, 1 - meta[0], meta[0])
     if whole:
-        left_at = lambda i, which: (0, i)
-        right_specs = [pl.BlockSpec((rows, n), lambda i, which: (0, which[0]))]
+        left_at = lambda i, meta: (0, i % steps)
+        right_specs = [pl.BlockSpec((rows, n), lambda i, meta: (0, half_at(i, meta)))]
     else:
-        left_at = lambda i, which: (0, which[0] * steps + i)
+        left_at = lambda i, meta: (0, half_at(i, meta) * steps + i % steps)
         right_specs = [fixed(p.shape) for p in rights]
-
-    def product(which):
-        return pl.pallas_call(
-            product_kernel if whole else product_pieces_kernel,
-            name="weight_gradient",
-            out_shape=jax.ShapeDtypeStruct((m, n), BF16),
-            grid_spec=pltpu.PrefetchScalarGridSpec(
-                num_scalar_prefetch=1, grid=(steps,),
-                in_specs=[pl.BlockSpec((rows, block), left_at)] + right_specs,
-                out_specs=pl.BlockSpec((block, n), lambda i, which: (i, 0)),
-                scratch_shapes=[] if whole else [pltpu.VMEM((rows, n), BF16)]),
-            compiler_params=params(20),
-            cost_estimate=pl.CostEstimate(flops=2 * rows * m * n, transcendentals=0, bytes_accessed=2 * (rows * (m + n) + m * n)),
-        )(jnp.stack([which, place]).astype(jnp.int32), left, *rights)
-
-    arrived = swap(product(1 - section), "section", 1)
-    return product(section), arrived
+    other, own = pl.pallas_call(
+        functools.partial(product_kernel, steps),
+        name="weight_gradient",
+        out_shape=[jax.ShapeDtypeStruct((m, n), BF16)] * 2,
+        grid_spec=pltpu.PrefetchScalarGridSpec(
+            num_scalar_prefetch=1, grid=(2 * steps,),
+            in_specs=[pl.BlockSpec((rows, block), left_at)] + right_specs,
+            out_specs=[pl.BlockSpec((block, n), lambda i, meta: (jnp.minimum(i, steps - 1), 0)),
+                       pl.BlockSpec((block, n), lambda i, meta: (jnp.maximum(i - steps, 0), 0))],
+            scratch_shapes=[] if whole else [pltpu.VMEM((rows, n), BF16)]),
+        compiler_params=params(20),
+        cost_estimate=pl.CostEstimate(flops=4 * rows * m * n, transcendentals=0, bytes_accessed=4 * (rows * (m + n) + m * n)),
+    )(jnp.stack([section, place]).astype(jnp.int32), left, *rights)
+    return own, swap(other, "section", 1)
 
 
 def dct_table(order):
@@ -682,12 +684,12 @@
     grad1_b = after(pieces_g, out_blocks1[0])
     parts, stats, dcat1, dmix1, fsum1 = run_backward(metas[1], grad1_b, saved1, weights1, True)
     parts, stats, dcat1, dmix1, fsum1 = after((parts, stats, dcat1, dmix1, fsum1), *out_blocks1, *out_sent)
-    arrived = scatter_start(parts)
+    sums = mp_total(stats)
+    arrived = after(scatter_start(parts), sums)
     turn = scatter_turn(parts, arrived)
     steps1 = list(ring_scatter(in_block(*weight_gradient(saved1[0], (dcat1,), section, place)), "dp"))
     arrivals1, red_in1 = [arrival for arrival, _ in steps1], steps1[-1][1]
     d_normed = scatter_end(parts, arrived, *turn)
-    sums = mp_total(after(stats, *turn))
     g0 = norm_backward(cot, d_normed, sums, all1[1:3], weights1[0][0]).astype(BF16)
     small1 = small_gradients(d_normed, all1[1:3], dmix1, fsum1)
     pieces_g0 = gather_pieces(after(g0, arrivals1[0]), arrivals1[1:2])
@@ -702,11 +704,11 @@
     kept, sent = direct_sends(parts)
     mine0, arrived0 = weight_gradient(saved0[0], (dcat0,), section, place)
     block0 = in_block(mine0, arrived0)
-    meanwhile = list(sent)
+    sums = mp_total(after(stats, arrived0))
+    meanwhile = list(sent) + [sums]
     ring0 = ring_scatter(block0, "dp", meanwhile)
     steps0 = [next(ring0)]
     meanwhile.clear()
-    sums = mp_total(after(stats, steps0[0][1]))
     sent, dmix0, out_blocks0, out_blocks1 = after((sent, dmix0, out_blocks0, out_blocks1), steps0[0][1])
     d_normed = kept + sent[0].astype(F32) + sent[1].astype(F32) + sent[2].astype(F32)
     d_input = norm_backward(g0, d_normed, sums, all0[1:3], weights0[0][0])

time: 375 us -> 392 us (1.045)
  waiting for transfers between devices: 87.3 us -> 127 us
  Pallas kernels: 147 us -> 130 us
    ppermute x49, waiting for transfers between devices: 56.3 us -> 86.3 us  [swap(): lax.ppermute(value, axis, [(k, k ^ by) for k in range(lax.axis_size(axis))])]
    ppermute x6, waiting for transfers between devices: 29.5 us -> 39 us  [ring_scatter(): arrived = lax.ppermute(total, axis, pairs)]
    pallas_call x8 -> x4, Pallas kernels: 39.4 us -> 32 us  [weight_gradient(): pl.pallas_call(functools.partial(product_kernel, steps), name='weight_gra...]
    pallas_call x2, Pallas kernels: 60.7 us -> 53.9 us  [backward_layer(): pl.pallas_call(functools.partial(backward_kernel, carry is not None, phas...]
    unnamed x157 -> x147, local copies, waits for them, and re-layouts: 15.1 us -> 12 us
  transfers between devices with their start and end apart: 64 -> 64, of which waited for: 23 -> 26; matrix products, arithmetic and copies ran while one was open for 13% -> 12% of each run, Pallas kernels for 34% -> 25%
where the time goes in v3:
time: 392 us; the launch traced here: 391 us
  Pallas kernels  130 us (33%)
  waiting for transfers between devices  127 us (32%)
  starting transfers between devices  62.1 us (16%)
  other arithmetic  36.6 us (9%)
  local copies, waits for them, and re-layouts  31.1 us (8%)
    ppermute x49, waiting for transfers between devices, swap(): lax.ppermute(value, axis, [(k, k ^ by) for k in range(lax.axis_size(axis))])  86.3 us
    pallas_call x2, Pallas kernels, backward_layer(): pl.pallas_call(functools.partial(backward_kernel, carry is not None, phas...  53.9 us
    ppermute x49, starting transfers between devices, swap(): lax.ppermute(value, axis, [(k, k ^ by) for k in range(lax.axis_size(axis))])  44.6 us
    pallas_call x2, Pallas kernels, forward_layer(): pl.pallas_call(functools.partial(forward_kernel, carry is not None, phase...  44.6 us
    ppermute x6, waiting for transfers between devices, ring_scatter(): arrived = lax.ppermute(total, axis, pairs)  39 us
    pallas_call x4, Pallas kernels, weight_gradient(): pl.pallas_call(functools.partial(product_kernel, steps), name='weight_gra...  32 us
    unnamed x147, local copies, waits for them, and re-layouts  12 us
    ppermute x6, starting transfers between devices, block_sends(): lax.ppermute(block_of((rank + k) % count), axis, [(i, (i + k) % count) fo...  8.74 us
  transfers between devices with their start and end apart: 64, of which 26 were waited for; matrix products, arithmetic and copies ran while one was open for 12% of the time, Pallas kernels for 25%

profile of v3, /device:TPU:0, one launch (start us, length us, event | category | flops | bytes accessed | tf_op | source)
XLA Modules:
  0.0 390.6 jit_solution(10890817140122854148)
XLA Ops:
  1.9 3.1 collective-permute-start.2
  11.4 2.9 multiply_select_fusion
  21.4 4.0 %collective-permute-done.3.refs_6_ = bf16[1024,128]{1,0:T(8,128)(2,1)} collective-permute-done((bf16[1024,128]{1,0:T(8,128)(2,1)S(1)}, bf16[1024,128]{1,0:T(8,128)(2,1)}, u32[]{:S(2)}, u32[]{:S(2)}) %collective-permute-start.3) | collective-permute-done | bytes 262176 | tf_op jit(solution)/shard_map/ppermute | solution.py:463
  28.2 4.5 %collective-permute-done.1.refs_5_ = bf16[1024,128]{1,0:T(8,128)(2,1)S(1)} collective-permute-done((bf16[1024,128]{1,0:T(8,128)(2,1)S(1)}, bf16[1024,128]{1,0:T(8,128)(2,1)S(1)}, u32[]{:S(2)}, u32[]{:S(2)}) %collective-permute-start.1) | collective-permute-done | bytes 262176 | tf_op jit(solution)/shard_map/ppermute | solution.py:463
  34.3 22.5 %layer_forward.2 = (bf16[2,1024,128]{2,1,0:T(8,128)(2,1)}, bf16[2,1024,128]{2,1,0:T(8,128)(2,1)}, f32[1024,256]{1,0:T(8,128)}, f32[1024,128]{1,0:T(8,128)}, f32[...) custom-call(s32[2]{0:T(128)} %pad_add_fusion.2.refs_0_, ...), custom_call_target="tpu_custom_call" | custom-call | flops 20480000000 | bytes 25165824 | tf_op jit(solution)/shard_map/layer_forward/pallas_call | solution.py:407
  59.5 9.0 %collective-permute-done.11 = bf16[2,1024,128]{2,1,0:T(8,128)(2,1)S(1)} collective-permute-done((bf16[2,1024,128]{2,1,0:T(8,128)(2,1)}, bf16[2,1024,128]{2,1,0:T(8,128)(2,1)S(1)}, u32[]{:S(2)}, u32[]{:S(2)}) %collective-permute-start.11) | collective-permute-done | bytes 524320 | tf_op jit(solution)/shard_map/ppermute | solution.py:463
  76.1 3.8 collective-permute-done.14
  82.3 7.3 %collective-permute-done.16.refs_4_ = bf16[1024,256]{1,0:T(8,128)(2,1)} collective-permute-done((bf16[1024,256]{1,0:T(8,128)(2,1)S(1)}, bf16[1024,256]{1,0:T(8,128)(2,1)}, u32[]{:S(2)}, u32[]{:S(2)}) %collective-permute-start.16) | collective-permute-done | bytes 524320 | tf_op jit(solution)/shard_map/ppermute | solution.py:463
  98.2 4.0 %collective-permute-done.17.refs_5_ = bf16[1024,128]{1,0:T(8,128)(2,1)} collective-permute-done((bf16[1024,128]{1,0:T(8,128)(2,1)}, bf16[1024,128]{1,0:T(8,128)(2,1)}, u32[]{:S(2)}, u32[]{:S(2)}) %collective-permute-start.17) | collective-permute-done | bytes 262176 | tf_op jit(solution)/shard_map/ppermute | solution.py:463
  104.2 22.1 %layer_forward.3 = (f32[1024,256]{1,0:T(8,128)}, bf16[1024,256]{1,0:T(8,128)(2,1)}, bf16[1024,256]{1,0:T(8,128)(2,1)}, bf16[1024,256]{1,0:T(8,128)(2,1)}, bf16[1...) custom-call(s32[2]{0:T(128)} %pad_add_fusion.refs_0_, ...), custom_call_target="tpu_custom_call" | custom-call | flops 20480000000 | bytes 25165824 | tf_op jit(solution)/shard_map/layer_forward/pallas_call | solution.py:407
  128.3 7.8 %weight_gradient.4 = (bf16[640,1024]{1,0:T(8,128)(2,1)}, bf16[640,1024]{1,0:T(8,128)(2,1)S(1)}) custom-call(s32[2]{0:T(128)S(1)} %pad_add_fusion.3.meta, bf16[1024,1280]{1,0:T(8,128)(2,1)S(1)} %copy-done.18, bf16[1024,256]{1,0:T(8,128)(2,1)S(1)} %dynamic-slice_bitcast_fusion.1.refs_0_.refs_1_, bf16[1024,256]{1,0:T(8,128)(2,1)S(1)} %copy-done.10, ...), custom_call_target="tpu_custom_call" | custom-call | flops 2684354560 | bytes 9437184 | tf_op jit(solution)/shard_map/weight_gradient/pallas_call | solution.py:565
  141.2 3.3 collective-permute-start.24
  144.5 6.7 %collective-permute-done.25 = bf16[1024,256]{1,0:T(8,128)(2,1)S(1)} collective-permute-done((bf16[1024,256]{1,0:T(8,128)(2,1)}, bf16[1024,256]{1,0:T(8,128)(2,1)S(1)}, u32[]{:S(2)}, u32[]{:S(2)}) %collective-permute-start.25) | collective-permute-done | bytes 524320 | tf_op jit(solution)/shard_map/ppermute | solution.py:463
  152.6 27.1 %layer_backward.2 = (bf16[2,1024,128]{2,1,0:T(8,128)(2,1)}, bf16[2,1024,128]{2,1,0:T(8,128)(2,1)}, f32[1024,256]{1,0:T(8,128)}, f32[1024,128]{1,0:T(8,128)}, f32...) custom-call(s32[2]{0:T(128)} %pad_add_fusion.refs_0_, ...), custom_call_target="tpu_custom_call" | custom-call | flops 25600000000 | bytes 25165824 | tf_op jit(solution)/shard_map/layer_backward/pallas_call | solution.py:447
  182.9 8.7 %weight_gradient.5 = (bf16[1024,896]{1,0:T(8,128)(2,1)}, bf16[1024,896]{1,0:T(8,128)(2,1)S(1)}) custom-call(s32[2]{0:T(128)S(1)} %pad_add_fusion.3.meta, bf16[1024,1024]{1,0:T(8,128)(2,1)S(1)} %copy-done.22, bf16[1024,1792]{1,0:T(8,128)(2,1)S(1)} %copy-done.19), custom_call_target="tpu_custom_call" | custom-call | flops 3758096384 | bytes 11534336 | tf_op jit(solution)/shard_map/weight_gradient/pallas_call | solution.py:565
  196.8 10.5 %collective-permute-done.32 = f32[8,1024]{1,0:T(8,128)S(1)} collective-permute-done((f32[8,1024]{1,0:T(8,128)S(1)}, f32[8,1024]{1,0:T(8,128)S(1)}, u32[]{:S(2)}, u32[]{:S(2)}) %collective-permute-start.32) | collective-permute-done | bytes 32800 | tf_op jit(solution)/shard_map/ppermute | solution.py:463
  208.7 2.5 collective-permute-done.30
  218.1 8.7 %collective-permute-done.36 = bf16[256,896]{1,0:T(8,128)(2,1)S(1)} collective-permute-done((bf16[256,896]{1,0:T(8,128)(2,1)S(1)}, bf16[256,896]{1,0:T(8,128)(2,1)S(1)}, u32[]{:S(2)}, u32[]{:S(2)}) %collective-permute-start.36) | collective-permute-done | bytes 458784 | tf_op jit(solution)/shard_map/ppermute | solution.py:521
  232.2 7.1 %collective-permute-done.39 = bf16[256,896]{1,0:T(8,128)(2,1)S(1)} collective-permute-done((bf16[256,896]{1,0:T(8,128)(2,1)S(1)}, bf16[256,896]{1,0:T(8,128)(2,1)S(1)}, u32[]{:S(2)}, u32[]{:S(2)}) %collective-permute-start.39) | collective-permute-done | bytes 458784 | tf_op jit(solution)/shard_map/ppermute | solution.py:521
  244.9 4.5 %collective-permute-done.41.refs_4_.refs_5_ = bf16[1024,128]{1,0:T(8,128)(2,1)S(1)} collective-permute-done((bf16[1024,128]{1,0:T(8,128)(2,1)S(1)}, bf16[1024,128]{1,0:T(8,128)(2,1)S(1)}, u32[]{:S(2)}, u32[]{:S(2)}) %collective-permute-start.41) | collective-permute-done | bytes 262176 | tf_op jit(solution)/shard_map/ppermute | solution.py:463
  250.9 6.7 %weight_gradient.6 = (bf16[640,1024]{1,0:T(8,128)(2,1)S(1)}, bf16[640,1024]{1,0:T(8,128)(2,1)S(1)}) custom-call(s32[2]{0:T(128)S(1)} %pad_add_fusion.3.meta, bf16[1024,1280]{1,0:T(8,128)(2,1)S(1)} %copy-done.17, bf16[1024,256]{1,0:T(8,128)(2,1)S(1)} %get-tuple-element.224.refs_0_.refs_1_, bf16[1024,256]{1,0:T(8,128)(2,1)S(1)} %collective-permute-done.37.refs_1_.refs_2_, ...), custom_call_target="tpu_custom_call" | custom-call | flops 2684354560 | bytes 9437184 | tf_op jit(solution)/shard_map/weight_gradient/pallas_call | solution.py:565
  257.7 3.0 collective-permute-done.43
  261.4 3.4 collective-permute-start.46
  265.5 26.7 %layer_backward.3 = (f32[1024,256]{1,0:T(8,128)}, bf16[1024,256]{1,0:T(8,128)(2,1)}, bf16[1024,256]{1,0:T(8,128)(2,1)}, bf16[1024,256]{1,0:T(8,128)(2,1)}, f32[8...) custom-call(s32[2]{0:T(128)} %pad_add_fusion.2.refs_0_, ...), custom_call_target="tpu_custom_call" | custom-call | flops 25600000000 | bytes 25165824 | tf_op jit(solution)/shard_map/layer_backward/pallas_call | solution.py:447
  295.5 8.7 %weight_gradient.7 = (bf16[1024,896]{1,0:T(8,128)(2,1)}, bf16[1024,896]{1,0:T(8,128)(2,1)S(1)}) custom-call(s32[2]{0:T(128)S(1)} %pad_add_fusion.3.meta, bf16[1024,1024]{1,0:T(8,128)(2,1)S(1)} %copy-done.21, bf16[1024,1792]{1,0:T(8,128)(2,1)S(1)} %copy-done.20), custom_call_target="tpu_custom_call" | custom-call | flops 3758096384 | bytes 11534336 | tf_op jit(solution)/shard_map/weight_gradient/pallas_call | solution.py:565
  315.0 18.9 %collective-permute-done.54 = f32[8,1024]{1,0:T(8,128)S(1)} collective-permute-done((f32[8,1024]{1,0:T(8,128)S(1)}, f32[8,1024]{1,0:T(8,128)S(1)}, u32[]{:S(2)}, u32[]{:S(2)}) %collective-permute-start.54) | collective-permute-done | bytes 32800 | tf_op jit(solution)/shard_map/ppermute | solution.py:463
  335.3 2.5 collective-permute-start.51
  340.0 9.3 %collective-permute-done.51 = bf16[256,896]{1,0:T(8,128)(2,1)} collective-permute-done((bf16[256,896]{1,0:T(8,128)(2,1)}, bf16[256,896]{1,0:T(8,128)(2,1)}, u32[]{:S(2)}, u32[]{:S(2)}) %collective-permute-start.51) | collective-permute-done | bytes 458784 | tf_op jit(solution)/shard_map/ppermute | solution.py:521
  357.9 3.1 collective-permute-start.59
  361.9 4.5 %collective-permute-done.60 = bf16[256,896]{1,0:T(8,128)(2,1)} collective-permute-done((bf16[256,896]{1,0:T(8,128)(2,1)}, bf16[256,896]{1,0:T(8,128)(2,1)}, u32[]{:S(2)}, u32[]{:S(2)}) %collective-permute-start.60) | collective-permute-done | bytes 458784 | tf_op jit(solution)/shard_map/ppermute | solution.py:521
  369.7 9.2 %collective-permute-done.61 = bf16[256,896]{1,0:T(8,128)(2,1)} collective-permute-done((bf16[256,896]{1,0:T(8,128)(2,1)S(1)}, bf16[256,896]{1,0:T(8,128)(2,1)}, u32[]{:S(2)}, u32[]{:S(2)}) %collective-permute-start.61) | collective-permute-done | bytes 458784 | tf_op jit(solution)/shard_map/ppermute | solution.py:521
  384.5 3.2 maximum_select_fusion
  (346 shorter events, 119.4 us)
Async XLA Ops:
  1.9 15.0 %collective-permute-start.2 = (bf16[1024,256]{1,0:T(8,128)(2,1)S(1)}, bf16[1024,256]{1,0:T(8,128)(2,1)S(1)}, u32[]{:S(2)}, u32[]{:S(2)}) collective-permute-start(bf16[1024,256]{1,0:T(8,128)(2,1)S(1)} %dynamic-slice_bitcast_fusion.refs_2_), channel_id=1, source_target_pairs={{0,2},{1,3},{2,0},{3,1},{4,6},{5,7},{6,4},{7,5},{8,10},{9,11},{10,... | collective-permute-start | bytes 1572872 | tf_op jit(solution)/shard_map/ppermute | solution.py:463
  4.9 14.4 %collective-permute-start = (bf16[1024,256]{1,0:T(8,128)(2,1)S(1)}, bf16[1024,256]{1,0:T(8,128)(2,1)S(1)}, u32[]{:S(2)}, u32[]{:S(2)}) collective-permute-start(bf16[1024,256]{1,0:T(8,128)(2,1)S(1)} %dynamic-slice_bitcast_fusion.refs_2_), channel_id=1, source_target_pairs={{0,1},{1,0},{2,3},{3,2},{4,5},{5,4},{6,7},{7,6},{8,9},{9,8},{10,11... | collective-permute-start | bytes 1572872 | tf_op jit(solution)/shard_map/ppermute | solution.py:463
  8.9 25.4 %collective-permute-start.6 = (bf16[1,1024,1024]{2,1,0:T(8,128)(2,1)}, bf16[1,1024,1024]{2,1,0:T(8,128)(2,1)}, u32[]{:S(2)}, u32[]{:S(2)}) collective-permute-start(bf16[1,1024,1024]{2,1,0:T(8,128)(2,1)} %refs_23_.3), channel_id=1, source_target_pairs={{0,16},{16,0},{1,17},{17,1},{2,18},{18,2},{3,19},{19,3},{4,20},{20... | collective-permute-start | bytes 6291464 | tf_op jit(solution)/shard_map/ppermute | solution.py:463
  9.4 24.9 %collective-permute-start.8 = (bf16[1,1024,1024]{2,1,0:T(8,128)(2,1)}, bf16[1,1024,1024]{2,1,0:T(8,128)(2,1)}, u32[]{:S(2)}, u32[]{:S(2)}) collective-permute-start(bf16[1,1024,1024]{2,1,0:T(8,128)(2,1)} %refs_25_.3), channel_id=1, source_target_pairs={{0,16},{16,0},{1,17},{17,1},{2,18},{18,2},{3,19},{19,3},{4,20},{20... | collective-permute-start | bytes 6291464 | tf_op jit(solution)/shard_map/ppermute | solution.py:463
  15.7 18.6 %collective-permute-start.5 = (bf16[1,3,1024,256]{3,2,1,0:T(8,128)(2,1)}, bf16[1,3,1024,256]{3,2,1,0:T(8,128)(2,1)}, u32[]{:S(2)}, u32[]{:S(2)}) collective-permute-start(bf16[1,3,1024,256]{3,2,1,0:T(8,128)(2,1)} %refs_22_.3), channel_id=1, source_target_pairs={{0,16},{16,0},{1,17},{17,1},{2,18},{18,2},{3,19},{19,3},{4,20},{20... | collective-permute-start | bytes 4718600 | tf_op jit(solution)/shard_map/ppermute | solution.py:463
  32.8 24.1 %collective-permute-start.10 = (bf16[1024,256]{1,0:T(8,128)(2,1)S(1)}, bf16[1024,256]{1,0:T(8,128)(2,1)S(1)}, u32[]{:S(2)}, u32[]{:S(2)}) collective-permute-start(bf16[1024,256]{1,0:T(8,128)(2,1)S(1)} %dynamic-slice_bitcast_fusion.1.refs_0_.refs_1_), channel_id=1, source_target_pairs={{0,2},{1,3},{2,0},{3,1},{4,6},{5,7},{6,4},{7,5},{8,10},{9,11},{10,... | collective-permute-start | bytes 1572872 | tf_op jit(solution)/shard_map/ppermute | solution.py:463
  33.0 23.8 %collective-permute-start.9 = (bf16[1024,256]{1,0:T(8,128)(2,1)S(1)}, bf16[1024,256]{1,0:T(8,128)(2,1)S(1)}, u32[]{:S(2)}, u32[]{:S(2)}) collective-permute-start(bf16[1024,256]{1,0:T(8,128)(2,1)S(1)} %dynamic-slice_bitcast_fusion.1.refs_0_.refs_1_), channel_id=1, source_target_pairs={{0,1},{1,0},{2,3},{3,2},{4,5},{5,4},{6,7},{7,6},{8,9},{9,8},{10,11... | collective-permute-start | bytes 1572872 | tf_op jit(solution)/shard_map/ppermute | solution.py:463
  102.2 24.2 %collective-permute-start.20 = (bf16[1024,128]{1,0:T(8,128)(2,1)S(1)}, bf16[1024,128]{1,0:T(8,128)(2,1)S(1)}, u32[]{:S(2)}, u32[]{:S(2)}) collective-permute-start(bf16[1024,128]{1,0:T(8,128)(2,1)S(1)} %slice.192), channel_id=1, source_target_pairs={{0,1},{1,0},{2,3},{3,2},{4,5},{5,4},{6,7},{7,6},{8,9},{9,8},{10,11... | collective-permute-start | bytes 786440 | tf_op jit(solution)/shard_map/ppermute | solution.py:463
  103.5 22.9 %collective-permute-start.19 = (bf16[1024,128]{1,0:T(8,128)(2,1)S(1)}, bf16[1024,128]{1,0:T(8,128)(2,1)S(1)}, u32[]{:S(2)}, u32[]{:S(2)}) collective-permute-start(bf16[1024,128]{1,0:T(8,128)(2,1)S(1)} %slice.191), channel_id=1, source_target_pairs={{0,2},{1,3},{2,0},{3,1},{4,6},{5,7},{6,4},{7,5},{8,10},{9,11},{10,... | collective-permute-start | bytes 786440 | tf_op jit(solution)/shard_map/ppermute | solution.py:463
  136.1 15.1 %collective-permute-start.25 = (bf16[1024,256]{1,0:T(8,128)(2,1)}, bf16[1024,256]{1,0:T(8,128)(2,1)S(1)}, u32[]{:S(2)}, u32[]{:S(2)}) collective-permute-start(bf16[1024,256]{1,0:T(8,128)(2,1)} %get-tuple-element.195), channel_id=1, source_target_pairs={{0,1},{1,0},{2,3},{3,2},{4,5},{5,4},{6,7},{7,6},{8,9},{9,8},{10,11... | collective-permute-start | bytes 1572872 | tf_op jit(solution)/shard_map/ppermute | solution.py:463
  136.9 42.8 %collective-permute-start.26 = (bf16[1024,256]{1,0:T(8,128)(2,1)}, bf16[1024,256]{1,0:T(8,128)(2,1)S(1)}, u32[]{:S(2)}, u32[]{:S(2)}) collective-permute-start(bf16[1024,256]{1,0:T(8,128)(2,1)} %get-tuple-element.196), channel_id=1, source_target_pairs={{0,2},{1,3},{2,0},{3,1},{4,6},{5,7},{6,4},{7,5},{8,10},{9,11},{10,... | collective-permute-start | bytes 1572872 | tf_op jit(solution)/shard_map/ppermute | solution.py:463
  138.3 41.5 %collective-permute-start.27 = (bf16[1024,256]{1,0:T(8,128)(2,1)}, bf16[1024,256]{1,0:T(8,128)(2,1)S(1)}, u32[]{:S(2)}, u32[]{:S(2)}) collective-permute-start(bf16[1024,256]{1,0:T(8,128)(2,1)} %get-tuple-element.197), channel_id=1, source_target_pairs={{0,3},{1,2},{2,1},{3,0},{4,7},{5,6},{6,5},{7,4},{8,11},{9,10},{10,... | collective-permute-start | bytes 1572872 | tf_op jit(solution)/shard_map/ppermute | solution.py:463
  141.2 38.6 %collective-permute-start.24 = (bf16[640,256]{1,0:T(8,128)(2,1)S(1)}, bf16[640,256]{1,0:T(8,128)(2,1)S(1)}, u32[]{:S(2)}, u32[]{:S(2)}) collective-permute-start(bf16[640,256]{1,0:T(8,128)(2,1)S(1)} %get-tuple-element.320), channel_id=1, source_target_pairs={{0,12},{4,0},{8,4},{12,8},{1,13},{5,1},{9,5},{13,9},{2,14},{6,2},{... | collective-permute-start | bytes 983048 | tf_op jit(solution)/shard_map/ppermute | solution.py:541
  144.5 35.3 %collective-permute-start.23 = (bf16[640,256]{1,0:T(8,128)(2,1)S(1)}, bf16[640,256]{1,0:T(8,128)(2,1)S(1)}, u32[]{:S(2)}, u32[]{:S(2)}) collective-permute-start(bf16[640,256]{1,0:T(8,128)(2,1)S(1)} %get-tuple-element.321), channel_id=1, source_target_pairs={{0,8},{4,12},{8,0},{12,4},{1,9},{5,13},{9,1},{13,5},{2,10},{6,14},... | collective-permute-start | bytes 983048 | tf_op jit(solution)/shard_map/ppermute | solution.py:541
  151.2 28.6 %collective-permute-start.22 = (bf16[640,256]{1,0:T(8,128)(2,1)S(1)}, bf16[640,256]{1,0:T(8,128)(2,1)S(1)}, u32[]{:S(2)}, u32[]{:S(2)}) collective-permute-start(bf16[640,256]{1,0:T(8,128)(2,1)S(1)} %get-tuple-element.322), channel_id=1, source_target_pairs={{0,4},{4,8},{8,12},{12,0},{1,5},{5,9},{9,13},{13,1},{2,6},{6,10},{... | collective-permute-start | bytes 983048 | tf_op jit(solution)/shard_map/ppermute | solution.py:541
  191.7 21.9 %collective-permute-start.35 = (bf16[1024,896]{1,0:T(8,128)(2,1)}, bf16[1024,896]{1,0:T(8,128)(2,1)}, u32[]{:S(2)}, u32[]{:S(2)}) collective-permute-start(bf16[1024,896]{1,0:T(8,128)(2,1)} %get-tuple-element.210), channel_id=1, source_target_pairs={{0,16},{16,0},{1,17},{17,1},{2,18},{18,2},{3,19},{19,3},{4,20},{20... | collective-permute-start | bytes 5505032 | tf_op jit(solution)/shard_map/ppermute | solution.py:463
  191.7 19.5 %collective-permute-start.28 = (bf16[2,1024,128]{2,1,0:T(8,128)(2,1)}, bf16[2,1024,128]{2,1,0:T(8,128)(2,1)}, u32[]{:S(2)}, u32[]{:S(2)}) collective-permute-start(bf16[2,1024,128]{2,1,0:T(8,128)(2,1)} %get-tuple-element.199), channel_id=1, source_target_pairs={{0,1},{1,0},{2,3},{3,2},{4,5},{5,4},{6,7},{7,6},{8,9},{9,8},{10,11... | collective-permute-start | bytes 1572872 | tf_op jit(solution)/shard_map/ppermute | solution.py:463
  192.4 18.8 %collective-permute-start.29 = (bf16[2,1024,128]{2,1,0:T(8,128)(2,1)}, bf16[2,1024,128]{2,1,0:T(8,128)(2,1)}, u32[]{:S(2)}, u32[]{:S(2)}) collective-permute-start(bf16[2,1024,128]{2,1,0:T(8,128)(2,1)} %get-tuple-element.200), channel_id=1, source_target_pairs={{0,2},{1,3},{2,0},{3,1},{4,6},{5,7},{6,4},{7,5},{8,10},{9,11},{10,... | collective-permute-start | bytes 1572872 | tf_op jit(solution)/shard_map/ppermute | solution.py:463
  212.2 15.9 %collective-permute-start.33 = (bf16[1024,128]{1,0:T(8,128)(2,1)S(1)}, bf16[1024,128]{1,0:T(8,128)(2,1)S(1)}, u32[]{:S(2)}, u32[]{:S(2)}) collective-permute-start(bf16[1024,128]{1,0:T(8,128)(2,1)S(1)} %fusion.6), channel_id=1, source_target_pairs={{0,2},{1,3},{2,0},{3,1},{4,6},{5,7},{6,4},{7,5},{8,10},{9,11},{10,... | collective-permute-start | bytes 786440 | tf_op jit(solution)/shard_map/ppermute | solution.py:463
  261.4 30.8 %collective-permute-start.46 = (bf16[640,256]{1,0:T(8,128)(2,1)S(1)}, bf16[640,256]{1,0:T(8,128)(2,1)S(1)}, u32[]{:S(2)}, u32[]{:S(2)}) collective-permute-start(bf16[640,256]{1,0:T(8,128)(2,1)S(1)} %get-tuple-element.316), channel_id=1, source_target_pairs={{0,12},{4,0},{8,4},{12,8},{1,13},{5,1},{9,5},{13,9},{2,14},{6,2},{... | collective-permute-start | bytes 983048 | tf_op jit(solution)/shard_map/ppermute | solution.py:541
  264.8 27.8 %collective-permute-start.45 = (bf16[640,256]{1,0:T(8,128)(2,1)S(1)}, bf16[640,256]{1,0:T(8,128)(2,1)S(1)}, u32[]{:S(2)}, u32[]{:S(2)}) collective-permute-start(bf16[640,256]{1,0:T(8,128)(2,1)S(1)} %get-tuple-element.317), channel_id=1, source_target_pairs={{0,8},{4,12},{8,0},{12,4},{1,9},{5,13},{9,1},{13,5},{2,10},{6,14},... | collective-permute-start | bytes 983048 | tf_op jit(solution)/shard_map/ppermute | solution.py:541
  264.8 27.8 %collective-permute-start.44 = (bf16[640,256]{1,0:T(8,128)(2,1)S(1)}, bf16[640,256]{1,0:T(8,128)(2,1)S(1)}, u32[]{:S(2)}, u32[]{:S(2)}) collective-permute-start(bf16[640,256]{1,0:T(8,128)(2,1)S(1)} %get-tuple-element.318), channel_id=1, source_target_pairs={{0,4},{4,8},{8,12},{12,0},{1,5},{5,9},{9,13},{13,1},{2,6},{6,10},{... | collective-permute-start | bytes 983048 | tf_op jit(solution)/shard_map/ppermute | solution.py:541
  307.1 32.8 %collective-permute-start.47 = (bf16[1024,256]{1,0:T(8,128)(2,1)}, bf16[1024,256]{1,0:T(8,128)(2,1)}, u32[]{:S(2)}, u32[]{:S(2)}) collective-permute-start(bf16[1024,256]{1,0:T(8,128)(2,1)} %get-tuple-element.249), channel_id=1, source_target_pairs={{0,1},{1,0},{2,3},{3,2},{4,5},{5,4},{6,7},{7,6},{8,9},{9,8},{10,11... | collective-permute-start | bytes 1572872 | tf_op jit(solution)/shard_map/ppermute | solution.py:463
  308.0 32.0 %collective-permute-start.48 = (bf16[1024,256]{1,0:T(8,128)(2,1)}, bf16[1024,256]{1,0:T(8,128)(2,1)}, u32[]{:S(2)}, u32[]{:S(2)}) collective-permute-start(bf16[1024,256]{1,0:T(8,128)(2,1)} %get-tuple-element.250), channel_id=1, source_target_pairs={{0,2},{1,3},{2,0},{3,1},{4,6},{5,7},{6,4},{7,5},{8,10},{9,11},{10,... | collective-permute-start | bytes 1572872 | tf_op jit(solution)/shard_map/ppermute | solution.py:463
  309.3 30.7 %collective-permute-start.49 = (bf16[1024,256]{1,0:T(8,128)(2,1)}, bf16[1024,256]{1,0:T(8,128)(2,1)}, u32[]{:S(2)}, u32[]{:S(2)}) collective-permute-start(bf16[1024,256]{1,0:T(8,128)(2,1)} %get-tuple-element.251), channel_id=1, source_target_pairs={{0,3},{1,2},{2,1},{3,0},{4,7},{5,6},{6,5},{7,4},{8,11},{9,10},{10,... | collective-permute-start | bytes 1572872 | tf_op jit(solution)/shard_map/ppermute | solution.py:463
  310.7 23.2 %collective-permute-start.54 = (f32[8,1024]{1,0:T(8,128)S(1)}, f32[8,1024]{1,0:T(8,128)S(1)}, u32[]{:S(2)}, u32[]{:S(2)}) collective-permute-start(f32[8,1024]{1,0:T(8,128)S(1)} %copy-done.60), channel_id=1, source_target_pairs={{0,3},{1,2},{2,1},{3,0},{4,7},{5,6},{6,5},{7,4},{8,11},{9,10},{10,... | collective-permute-start | bytes 98312 | tf_op jit(solution)/shard_map/ppermute | solution.py:463
  312.2 23.1 %collective-permute-start.53 = (f32[8,1024]{1,0:T(8,128)S(1)}, f32[8,1024]{1,0:T(8,128)S(1)}, u32[]{:S(2)}, u32[]{:S(2)}) collective-permute-start(f32[8,1024]{1,0:T(8,128)S(1)} %copy-done.60), channel_id=1, source_target_pairs={{0,2},{1,3},{2,0},{3,1},{4,6},{5,7},{6,4},{7,5},{8,10},{9,11},{10,... | collective-permute-start | bytes 98312 | tf_op jit(solution)/shard_map/ppermute | solution.py:463
  351.5 14.9 %collective-permute-start.60 = (bf16[256,896]{1,0:T(8,128)(2,1)}, bf16[256,896]{1,0:T(8,128)(2,1)}, u32[]{:S(2)}, u32[]{:S(2)}) collective-permute-start(bf16[256,896]{1,0:T(8,128)(2,1)} %add_convert_fusion.7), channel_id=1, source_target_pairs={{0,4},{4,8},{8,12},{12,0},{1,5},{5,9},{9,13},{13,1},{2,6},{6,10},{... | collective-permute-start | bytes 1376264 | tf_op jit(solution)/shard_map/ppermute | solution.py:521
  357.8 21.1 %collective-permute-start.55 = (f32[1024,256]{1,0:T(8,128)S(1)}, f32[1024,256]{1,0:T(8,128)}, u32[]{:S(2)}, u32[]{:S(2)}) collective-permute-start(f32[1024,256]{1,0:T(8,128)S(1)} %get-tuple-element.315), channel_id=1, source_target_pairs={{0,16},{16,0},{1,17},{17,1},{2,18},{18,2},{3,19},{19,3},{4,20},{20... | collective-permute-start | bytes 3145736 | tf_op jit(solution)/shard_map/ppermute | solution.py:463
  357.9 21.0 %collective-permute-start.59 = (f32[17152]{0:T(1024)S(1)}, f32[17152]{0:T(1024)S(1)}, u32[]{:S(2)}, u32[]{:S(2)}) collective-permute-start(f32[17152]{0:T(1024)S(1)} %select_add_fusion), channel_id=1, source_target_pairs={{0,12},{4,0},{8,4},{12,8},{1,13},{5,1},{9,5},{13,9},{2,14},{6,2},{... | collective-permute-start | bytes 205832 | tf_op jit(solution)/shard_map/ppermute | solution.py:532
  361.0 19.3 %collective-permute-start.58 = (f32[17152]{0:T(1024)S(1)}, f32[17152]{0:T(1024)S(1)}, u32[]{:S(2)}, u32[]{:S(2)}) collective-permute-start(f32[17152]{0:T(1024)S(1)} %select_add_fusion), channel_id=1, source_target_pairs={{0,8},{4,12},{8,0},{12,4},{1,9},{5,13},{9,1},{13,5},{2,10},{6,14},... | collective-permute-start | bytes 205832 | tf_op jit(solution)/shard_map/ppermute | solution.py:532
  361.0 19.2 %collective-permute-start.57 = (f32[17152]{0:T(1024)S(1)}, f32[17152]{0:T(1024)S(1)}, u32[]{:S(2)}, u32[]{:S(2)}) collective-permute-start(f32[17152]{0:T(1024)S(1)} %select_add_fusion), channel_id=1, source_target_pairs={{0,4},{4,8},{8,12},{12,0},{1,5},{5,9},{9,13},{13,1},{2,6},{6,10},{... | collective-permute-start | bytes 205832 | tf_op jit(solution)/shard_map/ppermute | solution.py:532
  (105 other events, 1139.5 us)

commit v4 on v3

--- a/solution.py
+++ b/solution.py
@@ -611,12 +611,12 @@
         return lax.dynamic_index_in_dim(values, section, 0, keepdims=False)
 
     shard0 = own(block_input)
-    pieces0 = gather_pieces(shard0)
 
     small = jnp.concatenate([ln_gain[0], ln_bias[0], feat_weight.reshape(-1), freq_table.astype(F32).reshape(-1)])
     small_other = swap(small, "section", 1)
     mine = (w_qkv, w_up, w_out, w_down)
     other = tuple(swap(w, "section", 1) for w in mine)
+    pieces0 = gather_pieces(shard0, [small_other, other[2]])
 
     def both(mine, other):
         return jnp.where(is_first, mine, other), jnp.where(is_first, other, mine)
@@ -683,13 +683,13 @@
     out_blocks1 = block_sends(out_block(*weight_gradient(saved1[6], pieces_g, section, place)), "dp")
     grad1_b = after(pieces_g, out_blocks1[0])
     parts, stats, dcat1, dmix1, fsum1 = run_backward(metas[1], grad1_b, saved1, weights1, True)
-    parts, stats, dcat1, dmix1, fsum1 = after((parts, stats, dcat1, dmix1, fsum1), *out_blocks1, *out_sent)
-    sums = mp_total(stats)
-    arrived = after(scatter_start(parts), sums)
+    parts, stats, dcat1, dmix1, fsum1 = after((parts, stats, dcat1, dmix1, fsum1), *out_blocks1, *out_sent[:2])
+    arrived = scatter_start(parts)
     turn = scatter_turn(parts, arrived)
     steps1 = list(ring_scatter(in_block(*weight_gradient(saved1[0], (dcat1,), section, place)), "dp"))
     arrivals1, red_in1 = [arrival for arrival, _ in steps1], steps1[-1][1]
     d_normed = scatter_end(parts, arrived, *turn)
+    sums = mp_total(after(stats, *turn))
     g0 = norm_backward(cot, d_normed, sums, all1[1:3], weights1[0][0]).astype(BF16)
     small1 = small_gradients(d_normed, all1[1:3], dmix1, fsum1)
     pieces_g0 = gather_pieces(after(g0, arrivals1[0]), arrivals1[1:2])
@@ -699,16 +699,16 @@
     out_blocks0 = block_sends(out_block(*weight_gradient(saved0[6], pieces_g0, section, place)), "dp")
     grad0_b = after(pieces_g0, out_blocks0[0])
     parts, stats, dcat0, dmix0, fsum0 = run_backward(metas[0], grad0_b, saved0, weights0, False)
-    parts, stats, dcat0, dmix0, fsum0 = after((parts, stats, dcat0, dmix0, fsum0), *out_blocks0)
+    parts, stats, dcat0, dmix0, fsum0 = after((parts, stats, dcat0, dmix0, fsum0), *out_blocks0, out_sent[2])
     out_blocks1 = after(out_blocks1, dcat0)
     kept, sent = direct_sends(parts)
     mine0, arrived0 = weight_gradient(saved0[0], (dcat0,), section, place)
     block0 = in_block(mine0, arrived0)
-    sums = mp_total(after(stats, arrived0))
-    meanwhile = list(sent) + [sums]
+    meanwhile = list(sent)
     ring0 = ring_scatter(block0, "dp", meanwhile)
     steps0 = [next(ring0)]
     meanwhile.clear()
+    sums = mp_total(after(stats, steps0[0][1]))
     sent, dmix0, out_blocks0, out_blocks1 = after((sent, dmix0, out_blocks0, out_blocks1), steps0[0][1])
     d_normed = kept + sent[0].astype(F32) + sent[1].astype(F32) + sent[2].astype(F32)
     d_input = norm_backward(g0, d_normed, sums, all0[1:3], weights0[0][0])

time: 392 us -> 371 us (0.946)
  waiting for transfers between devices: 127 us -> 106 us
    ppermute x49, waiting for transfers between devices: 86.3 us -> 74.7 us  [swap(): lax.ppermute(value, axis, [(k, k ^ by) for k in range(lax.axis_size(axis))])]
    ppermute x6, waiting for transfers between devices: 39 us -> 30.2 us  [ring_scatter(): arrived = lax.ppermute(total, axis, pairs)]
    ppermute x6, starting transfers between devices: 5.03 us -> 9.52 us  [ring_scatter(): arrived = lax.ppermute(total, axis, pairs)]
    unnamed x147 -> x143, local copies, waits for them, and re-layouts: 12 us -> 10.1 us
  transfers between devices with their start and end apart: 64 -> 64, of which waited for: 26 -> 26; matrix products, arithmetic and copies ran while one was open for 12% -> 14% of each run, Pallas kernels for 25% -> 26%
where the time goes in v4:
time: 371 us; the launch traced here: 370 us
  Pallas kernels  130 us (35%)
  waiting for transfers between devices  106 us (29%)
  starting transfers between devices  61.2 us (16%)
  other arithmetic  39 us (11%)
  local copies, waits for them, and re-layouts  30.3 us (8%)
    ppermute x49, waiting for transfers between devices, swap(): lax.ppermute(value, axis, [(k, k ^ by) for k in range(lax.axis_size(axis))])  74.7 us
    pallas_call x2, Pallas kernels, backward_layer(): pl.pallas_call(functools.partial(backward_kernel, carry is not None, phas...  53.6 us
    pallas_call x2, Pallas kernels, forward_layer(): pl.pallas_call(functools.partial(forward_kernel, carry is not None, phase...  44.4 us
    ppermute x49, starting transfers between devices, swap(): lax.ppermute(value, axis, [(k, k ^ by) for k in range(lax.axis_size(axis))])  41.9 us
    pallas_call x4, Pallas kernels, weight_gradient(): pl.pallas_call(functools.partial(product_kernel, steps), name='weight_gra...  32 us
    ppermute x6, waiting for transfers between devices, ring_scatter(): arrived = lax.ppermute(total, axis, pairs)  30.2 us
    unnamed x143, local copies, waits for them, and re-layouts  10.1 us
    ppermute x6, starting transfers between devices, ring_scatter(): arrived = lax.ppermute(total, axis, pairs)  9.52 us
  transfers between devices with their start and end apart: 64, of which 26 were waited for; matrix products, arithmetic and copies ran while one was open for 14% of the time, Pallas kernels for 26%

profile of v4, /device:TPU:0, one launch (start us, length us, event | category | flops | bytes accessed | tf_op | source)
XLA Modules:
  0.0 370.1 jit_solution(16236175805019483361)
XLA Ops:
  1.9 3.1 collective-permute-start.1
  11.4 2.9 multiply_select_fusion
  25.7 4.2 %collective-permute-done.5.refs_6_ = bf16[1024,128]{1,0:T(8,128)(2,1)S(1)} collective-permute-done((bf16[1024,128]{1,0:T(8,128)(2,1)S(1)}, bf16[1024,128]{1,0:T(8,128)(2,1)S(1)}, u32[]{:S(2)}, u32[]{:S(2)}) %collective-permute-start.5) | collective-permute-done | bytes 262176 | tf_op jit(solution)/shard_map/ppermute | solution.py:463
  32.5 22.5 %layer_forward.2 = (bf16[2,1024,128]{2,1,0:T(8,128)(2,1)}, bf16[2,1024,128]{2,1,0:T(8,128)(2,1)}, f32[1024,256]{1,0:T(8,128)}, f32[1024,128]{1,0:T(8,128)}, f32[...) custom-call(s32[2]{0:T(128)} %pad_add_fusion.2.refs_0_, ...), custom_call_target="tpu_custom_call" | custom-call | flops 20480000000 | bytes 25165824 | tf_op jit(solution)/shard_map/layer_forward/pallas_call | solution.py:407
  57.3 10.6 %collective-permute-done.11 = bf16[2,1024,128]{2,1,0:T(8,128)(2,1)S(1)} collective-permute-done((bf16[2,1024,128]{2,1,0:T(8,128)(2,1)}, bf16[2,1024,128]{2,1,0:T(8,128)(2,1)S(1)}, u32[]{:S(2)}, u32[]{:S(2)}) %collective-permute-start.11) | collective-permute-done | bytes 524320 | tf_op jit(solution)/shard_map/ppermute | solution.py:463
  72.8 2.7 collective-permute-done.12
  75.5 2.3 collective-permute-done.14
  80.5 8.3 %collective-permute-done.16.refs_4_ = bf16[1024,256]{1,0:T(8,128)(2,1)} collective-permute-done((bf16[1024,256]{1,0:T(8,128)(2,1)S(1)}, bf16[1024,256]{1,0:T(8,128)(2,1)}, u32[]{:S(2)}, u32[]{:S(2)}) %collective-permute-start.16) | collective-permute-done | bytes 524320 | tf_op jit(solution)/shard_map/ppermute | solution.py:463
  96.4 5.6 %collective-permute-done.17.refs_5_ = bf16[1024,128]{1,0:T(8,128)(2,1)} collective-permute-done((bf16[1024,128]{1,0:T(8,128)(2,1)}, bf16[1024,128]{1,0:T(8,128)(2,1)}, u32[]{:S(2)}, u32[]{:S(2)}) %collective-permute-start.17) | collective-permute-done | bytes 262176 | tf_op jit(solution)/shard_map/ppermute | solution.py:463
  102.1 2.5 collective-permute-start.19
  104.6 21.9 %layer_forward.3 = (f32[1024,256]{1,0:T(8,128)}, bf16[1024,256]{1,0:T(8,128)(2,1)}, bf16[1024,256]{1,0:T(8,128)(2,1)}, bf16[1024,256]{1,0:T(8,128)(2,1)}, bf16[1...) custom-call(s32[2]{0:T(128)} %pad_add_fusion.refs_0_, ...), custom_call_target="tpu_custom_call" | custom-call | flops 20480000000 | bytes 25165824 | tf_op jit(solution)/shard_map/layer_forward/pallas_call | solution.py:407
  128.5 7.8 %weight_gradient.4 = (bf16[640,1024]{1,0:T(8,128)(2,1)}, bf16[640,1024]{1,0:T(8,128)(2,1)S(1)}) custom-call(s32[2]{0:T(128)S(1)} %pad_add_fusion.3.meta, bf16[1024,1280]{1,0:T(8,128)(2,1)S(1)} %copy-done.16, bf16[1024,256]{1,0:T(8,128)(2,1)S(1)} %dynamic-slice_bitcast_fusion.1.refs_0_.refs_1_, bf16[1024,256]{1,0:T(8,128)(2,1)S(1)} %collective-permute-done.9.refs_1_.refs_2_, ...), custom_call_target="tpu_custom_call" | custom-call | flops 2684354560 | bytes 9437184 | tf_op jit(solution)/shard_map/weight_gradient/pallas_call | solution.py:565
  139.7 2.5 add_convert_fusion.21
  142.3 3.7 collective-permute-start.24
  146.9 27.0 %layer_backward.2 = (bf16[2,1024,128]{2,1,0:T(8,128)(2,1)}, bf16[2,1024,128]{2,1,0:T(8,128)(2,1)}, f32[1024,256]{1,0:T(8,128)}, f32[1024,128]{1,0:T(8,128)}, f32...) custom-call(s32[2]{0:T(128)} %pad_add_fusion.refs_0_, ...), custom_call_target="tpu_custom_call" | custom-call | flops 25600000000 | bytes 25165824 | tf_op jit(solution)/shard_map/layer_backward/pallas_call | solution.py:447
  174.1 2.7 copy-done.18
  176.7 8.7 %weight_gradient.5 = (bf16[1024,896]{1,0:T(8,128)(2,1)}, bf16[1024,896]{1,0:T(8,128)(2,1)S(1)}) custom-call(s32[2]{0:T(128)S(1)} %pad_add_fusion.3.meta, bf16[1024,1024]{1,0:T(8,128)(2,1)S(1)} %copy-done.20, bf16[1024,1792]{1,0:T(8,128)(2,1)S(1)} %copy-done.18), custom_call_target="tpu_custom_call" | custom-call | flops 3758096384 | bytes 11534336 | tf_op jit(solution)/shard_map/weight_gradient/pallas_call | solution.py:565
  187.9 12.3 %collective-permute-done.27 = bf16[2,1024,128]{2,1,0:T(8,128)(2,1)S(1)} collective-permute-done((bf16[2,1024,128]{2,1,0:T(8,128)(2,1)}, bf16[2,1024,128]{2,1,0:T(8,128)(2,1)S(1)}, u32[]{:S(2)}, u32[]{:S(2)}) %collective-permute-start.27) | collective-permute-done | bytes 524320 | tf_op jit(solution)/shard_map/ppermute | solution.py:463
  207.3 2.5 collective-permute-start.35
  211.7 8.7 %collective-permute-done.35 = bf16[256,896]{1,0:T(8,128)(2,1)S(1)} collective-permute-done((bf16[256,896]{1,0:T(8,128)(2,1)S(1)}, bf16[256,896]{1,0:T(8,128)(2,1)S(1)}, u32[]{:S(2)}, u32[]{:S(2)}) %collective-permute-start.35) | collective-permute-done | bytes 458784 | tf_op jit(solution)/shard_map/ppermute | solution.py:521
  225.5 8.2 %collective-permute-done.38 = bf16[256,896]{1,0:T(8,128)(2,1)S(1)} collective-permute-done((bf16[256,896]{1,0:T(8,128)(2,1)S(1)}, bf16[256,896]{1,0:T(8,128)(2,1)S(1)}, u32[]{:S(2)}, u32[]{:S(2)}) %collective-permute-start.38) | collective-permute-done | bytes 458784 | tf_op jit(solution)/shard_map/ppermute | solution.py:521
  238.6 4.2 %collective-permute-done.40.refs_4_.refs_5_ = bf16[1024,128]{1,0:T(8,128)(2,1)S(1)} collective-permute-done((bf16[1024,128]{1,0:T(8,128)(2,1)S(1)}, bf16[1024,128]{1,0:T(8,128)(2,1)S(1)}, u32[]{:S(2)}, u32[]{:S(2)}) %collective-permute-start.40) | collective-permute-done | bytes 262176 | tf_op jit(solution)/shard_map/ppermute | solution.py:463
  246.2 6.7 %weight_gradient.6 = (bf16[640,1024]{1,0:T(8,128)(2,1)S(1)}, bf16[640,1024]{1,0:T(8,128)(2,1)S(1)}) custom-call(s32[2]{0:T(128)S(1)} %pad_add_fusion.3.meta, bf16[1024,1280]{1,0:T(8,128)(2,1)S(1)} %copy-done.15, bf16[1024,256]{1,0:T(8,128)(2,1)S(1)} %get-tuple-element.225.refs_0_.refs_1_, bf16[1024,256]{1,0:T(8,128)(2,1)S(1)} %collective-permute-done.36.refs_1_.refs_2_, ...), custom_call_target="tpu_custom_call" | custom-call | flops 2684354560 | bytes 9437184 | tf_op jit(solution)/shard_map/weight_gradient/pallas_call | solution.py:565
  258.8 26.6 %layer_backward.3 = (f32[1024,256]{1,0:T(8,128)}, bf16[1024,256]{1,0:T(8,128)(2,1)}, bf16[1024,256]{1,0:T(8,128)(2,1)}, bf16[1024,256]{1,0:T(8,128)(2,1)}, f32[8...) custom-call(s32[2]{0:T(128)} %pad_add_fusion.2.refs_0_, ...), custom_call_target="tpu_custom_call" | custom-call | flops 25600000000 | bytes 25165824 | tf_op jit(solution)/shard_map/layer_backward/pallas_call | solution.py:447
  285.6 2.5 copy-done.17
  288.1 8.7 %weight_gradient.7 = (bf16[1024,896]{1,0:T(8,128)(2,1)}, bf16[1024,896]{1,0:T(8,128)(2,1)S(1)}) custom-call(s32[2]{0:T(128)S(1)} %pad_add_fusion.3.meta, bf16[1024,1024]{1,0:T(8,128)(2,1)S(1)} %copy-done.19, bf16[1024,1792]{1,0:T(8,128)(2,1)S(1)} %copy-done.17), custom_call_target="tpu_custom_call" | custom-call | flops 3758096384 | bytes 11534336 | tf_op jit(solution)/shard_map/weight_gradient/pallas_call | solution.py:565
  305.0 2.4 collective-permute-start.51
  310.9 3.7 collective-permute-done.47
  314.6 10.1 %collective-permute-done.48 = bf16[1024,256]{1,0:T(8,128)(2,1)} collective-permute-done((bf16[1024,256]{1,0:T(8,128)(2,1)}, bf16[1024,256]{1,0:T(8,128)(2,1)}, u32[]{:S(2)}, u32[]{:S(2)}) %collective-permute-start.48) | collective-permute-done | bytes 524320 | tf_op jit(solution)/shard_map/ppermute | solution.py:463
  331.2 2.8 collective-permute-start.60
  349.2 9.9 %collective-permute-done.61 = bf16[256,896]{1,0:T(8,128)(2,1)S(1)} collective-permute-done((bf16[256,896]{1,0:T(8,128)(2,1)S(1)}, bf16[256,896]{1,0:T(8,128)(2,1)S(1)}, u32[]{:S(2)}, u32[]{:S(2)}) %collective-permute-start.61) | collective-permute-done | bytes 458784 | tf_op jit(solution)/shard_map/ppermute | solution.py:521
  364.1 3.1 maximum_select_fusion
  (342 shorter events, 116.8 us)
Async XLA Ops:
  1.9 15.0 %collective-permute-start.1 = (bf16[1024,256]{1,0:T(8,128)(2,1)S(1)}, bf16[1024,256]{1,0:T(8,128)(2,1)S(1)}, u32[]{:S(2)}, u32[]{:S(2)}) collective-permute-start(bf16[1024,256]{1,0:T(8,128)(2,1)S(1)} %dynamic-slice_bitcast_fusion.refs_2_), channel_id=1, source_target_pairs={{0,2},{1,3},{2,0},{3,1},{4,6},{5,7},{6,4},{7,5},{8,10},{9,11},{10,... | collective-permute-start | bytes 1572872 | tf_op jit(solution)/shard_map/ppermute | solution.py:463
  4.9 13.5 %collective-permute-start = (bf16[1024,256]{1,0:T(8,128)(2,1)S(1)}, bf16[1024,256]{1,0:T(8,128)(2,1)}, u32[]{:S(2)}, u32[]{:S(2)}) collective-permute-start(bf16[1024,256]{1,0:T(8,128)(2,1)S(1)} %dynamic-slice_bitcast_fusion.refs_2_), channel_id=1, source_target_pairs={{0,1},{1,0},{2,3},{3,2},{4,5},{5,4},{6,7},{7,6},{8,9},{9,8},{10,11... | collective-permute-start | bytes 1572872 | tf_op jit(solution)/shard_map/ppermute | solution.py:463
  8.9 23.6 %collective-permute-start.7 = (bf16[1,1024,1024]{2,1,0:T(8,128)(2,1)}, bf16[1,1024,1024]{2,1,0:T(8,128)(2,1)}, u32[]{:S(2)}, u32[]{:S(2)}) collective-permute-start(bf16[1,1024,1024]{2,1,0:T(8,128)(2,1)} %refs_23_.3), channel_id=1, source_target_pairs={{0,16},{16,0},{1,17},{17,1},{2,18},{18,2},{3,19},{19,3},{4,20},{20... | collective-permute-start | bytes 6291464 | tf_op jit(solution)/shard_map/ppermute | solution.py:463
  9.4 23.1 %collective-permute-start.8 = (bf16[1,1024,1024]{2,1,0:T(8,128)(2,1)}, bf16[1,1024,1024]{2,1,0:T(8,128)(2,1)}, u32[]{:S(2)}, u32[]{:S(2)}) collective-permute-start(bf16[1,1024,1024]{2,1,0:T(8,128)(2,1)} %refs_25_.3), channel_id=1, source_target_pairs={{0,16},{16,0},{1,17},{17,1},{2,18},{18,2},{3,19},{19,3},{4,20},{20... | collective-permute-start | bytes 6291464 | tf_op jit(solution)/shard_map/ppermute | solution.py:463
  15.6 16.8 %collective-permute-start.6 = (bf16[1,3,1024,256]{3,2,1,0:T(8,128)(2,1)}, bf16[1,3,1024,256]{3,2,1,0:T(8,128)(2,1)}, u32[]{:S(2)}, u32[]{:S(2)}) collective-permute-start(bf16[1,3,1024,256]{3,2,1,0:T(8,128)(2,1)} %refs_22_.3), channel_id=1, source_target_pairs={{0,16},{16,0},{1,17},{17,1},{2,18},{18,2},{3,19},{19,3},{4,20},{20... | collective-permute-start | bytes 4718600 | tf_op jit(solution)/shard_map/ppermute | solution.py:463
  30.6 24.4 %collective-permute-start.10 = (bf16[1024,256]{1,0:T(8,128)(2,1)S(1)}, bf16[1024,256]{1,0:T(8,128)(2,1)S(1)}, u32[]{:S(2)}, u32[]{:S(2)}) collective-permute-start(bf16[1024,256]{1,0:T(8,128)(2,1)S(1)} %dynamic-slice_bitcast_fusion.1.refs_0_.refs_1_), channel_id=1, source_target_pairs={{0,2},{1,3},{2,0},{3,1},{4,6},{5,7},{6,4},{7,5},{8,10},{9,11},{10,... | collective-permute-start | bytes 1572872 | tf_op jit(solution)/shard_map/ppermute | solution.py:463
  31.6 23.4 %collective-permute-start.9 = (bf16[1024,256]{1,0:T(8,128)(2,1)S(1)}, bf16[1024,256]{1,0:T(8,128)(2,1)S(1)}, u32[]{:S(2)}, u32[]{:S(2)}) collective-permute-start(bf16[1024,256]{1,0:T(8,128)(2,1)S(1)} %dynamic-slice_bitcast_fusion.1.refs_0_.refs_1_), channel_id=1, source_target_pairs={{0,1},{1,0},{2,3},{3,2},{4,5},{5,4},{6,7},{7,6},{8,9},{9,8},{10,11... | collective-permute-start | bytes 1572872 | tf_op jit(solution)/shard_map/ppermute | solution.py:463
  56.3 14.0 %collective-permute-start.13 = (bf16[2,1024,128]{2,1,0:T(8,128)(2,1)}, bf16[2,1024,128]{2,1,0:T(8,128)(2,1)S(1)}, u32[]{:S(2)}, u32[]{:S(2)}) collective-permute-start(bf16[2,1024,128]{2,1,0:T(8,128)(2,1)} %get-tuple-element.161), channel_id=1, source_target_pairs={{0,2},{1,3},{2,0},{3,1},{4,6},{5,7},{6,4},{7,5},{8,10},{9,11},{10,... | collective-permute-start | bytes 1572872 | tf_op jit(solution)/shard_map/ppermute | solution.py:463
  102.0 24.5 %collective-permute-start.20 = (bf16[1024,128]{1,0:T(8,128)(2,1)S(1)}, bf16[1024,128]{1,0:T(8,128)(2,1)S(1)}, u32[]{:S(2)}, u32[]{:S(2)}) collective-permute-start(bf16[1024,128]{1,0:T(8,128)(2,1)S(1)} %slice.192), channel_id=1, source_target_pairs={{0,1},{1,0},{2,3},{3,2},{4,5},{5,4},{6,7},{7,6},{8,9},{9,8},{10,11... | collective-permute-start | bytes 786440 | tf_op jit(solution)/shard_map/ppermute | solution.py:463
  102.1 24.5 %collective-permute-start.19 = (bf16[1024,128]{1,0:T(8,128)(2,1)S(1)}, bf16[1024,128]{1,0:T(8,128)(2,1)S(1)}, u32[]{:S(2)}, u32[]{:S(2)}) collective-permute-start(bf16[1024,128]{1,0:T(8,128)(2,1)S(1)} %slice.191), channel_id=1, source_target_pairs={{0,2},{1,3},{2,0},{3,1},{4,6},{5,7},{6,4},{7,5},{8,10},{9,11},{10,... | collective-permute-start | bytes 786440 | tf_op jit(solution)/shard_map/ppermute | solution.py:463
  136.4 37.5 %collective-permute-start.25 = (bf16[1024,256]{1,0:T(8,128)(2,1)}, bf16[1024,256]{1,0:T(8,128)(2,1)S(1)}, u32[]{:S(2)}, u32[]{:S(2)}) collective-permute-start(bf16[1024,256]{1,0:T(8,128)(2,1)} %get-tuple-element.198), channel_id=1, source_target_pairs={{0,1},{1,0},{2,3},{3,2},{4,5},{5,4},{6,7},{7,6},{8,9},{9,8},{10,11... | collective-permute-start | bytes 1572872 | tf_op jit(solution)/shard_map/ppermute | solution.py:463
  136.6 37.4 %collective-permute-start.26 = (bf16[1024,256]{1,0:T(8,128)(2,1)}, bf16[1024,256]{1,0:T(8,128)(2,1)S(1)}, u32[]{:S(2)}, u32[]{:S(2)}) collective-permute-start(bf16[1024,256]{1,0:T(8,128)(2,1)} %get-tuple-element.199), channel_id=1, source_target_pairs={{0,2},{1,3},{2,0},{3,1},{4,6},{5,7},{6,4},{7,5},{8,10},{9,11},{10,... | collective-permute-start | bytes 1572872 | tf_op jit(solution)/shard_map/ppermute | solution.py:463
  142.3 31.7 %collective-permute-start.24 = (bf16[640,256]{1,0:T(8,128)(2,1)S(1)}, bf16[640,256]{1,0:T(8,128)(2,1)S(1)}, u32[]{:S(2)}, u32[]{:S(2)}) collective-permute-start(bf16[640,256]{1,0:T(8,128)(2,1)S(1)} %get-tuple-element.322), channel_id=1, source_target_pairs={{0,12},{4,0},{8,4},{12,8},{1,13},{5,1},{9,5},{13,9},{2,14},{6,2},{... | collective-permute-start | bytes 983048 | tf_op jit(solution)/shard_map/ppermute | solution.py:541
  145.9 28.1 %collective-permute-start.23 = (bf16[640,256]{1,0:T(8,128)(2,1)S(1)}, bf16[640,256]{1,0:T(8,128)(2,1)S(1)}, u32[]{:S(2)}, u32[]{:S(2)}) collective-permute-start(bf16[640,256]{1,0:T(8,128)(2,1)S(1)} %get-tuple-element.323), channel_id=1, source_target_pairs={{0,8},{4,12},{8,0},{12,4},{1,9},{5,13},{9,1},{13,5},{2,10},{6,14},... | collective-permute-start | bytes 983048 | tf_op jit(solution)/shard_map/ppermute | solution.py:541
  145.9 28.1 %collective-permute-start.22 = (bf16[640,256]{1,0:T(8,128)(2,1)S(1)}, bf16[640,256]{1,0:T(8,128)(2,1)S(1)}, u32[]{:S(2)}, u32[]{:S(2)}) collective-permute-start(bf16[640,256]{1,0:T(8,128)(2,1)S(1)} %get-tuple-element.324), channel_id=1, source_target_pairs={{0,4},{4,8},{8,12},{12,0},{1,5},{5,9},{9,13},{13,1},{2,6},{6,10},{... | collective-permute-start | bytes 983048 | tf_op jit(solution)/shard_map/ppermute | solution.py:541
  185.5 20.6 %collective-permute-start.34 = (bf16[1024,896]{1,0:T(8,128)(2,1)}, bf16[1024,896]{1,0:T(8,128)(2,1)}, u32[]{:S(2)}, u32[]{:S(2)}) collective-permute-start(bf16[1024,896]{1,0:T(8,128)(2,1)} %get-tuple-element.211), channel_id=1, source_target_pairs={{0,16},{16,0},{1,17},{17,1},{2,18},{18,2},{3,19},{19,3},{4,20},{20... | collective-permute-start | bytes 5505032 | tf_op jit(solution)/shard_map/ppermute | solution.py:463
  185.6 14.5 %collective-permute-start.27 = (bf16[2,1024,128]{2,1,0:T(8,128)(2,1)}, bf16[2,1024,128]{2,1,0:T(8,128)(2,1)S(1)}, u32[]{:S(2)}, u32[]{:S(2)}) collective-permute-start(bf16[2,1024,128]{2,1,0:T(8,128)(2,1)} %get-tuple-element.201), channel_id=1, source_target_pairs={{0,1},{1,0},{2,3},{3,2},{4,5},{5,4},{6,7},{7,6},{8,9},{9,8},{10,11... | collective-permute-start | bytes 1572872 | tf_op jit(solution)/shard_map/ppermute | solution.py:463
  185.7 15.5 %collective-permute-start.29 = (bf16[2,1024,128]{2,1,0:T(8,128)(2,1)}, bf16[2,1024,128]{2,1,0:T(8,128)(2,1)S(1)}, u32[]{:S(2)}, u32[]{:S(2)}) collective-permute-start(bf16[2,1024,128]{2,1,0:T(8,128)(2,1)} %get-tuple-element.203), channel_id=1, source_target_pairs={{0,2},{1,3},{2,0},{3,1},{4,6},{5,7},{6,4},{7,5},{8,10},{9,11},{10,... | collective-permute-start | bytes 1572872 | tf_op jit(solution)/shard_map/ppermute | solution.py:463
  207.3 13.0 %collective-permute-start.35 = (bf16[256,896]{1,0:T(8,128)(2,1)S(1)}, bf16[256,896]{1,0:T(8,128)(2,1)S(1)}, u32[]{:S(2)}, u32[]{:S(2)}) collective-permute-start(bf16[256,896]{1,0:T(8,128)(2,1)S(1)} %add_convert_fusion.14), channel_id=1, source_target_pairs={{0,4},{4,8},{8,12},{12,0},{1,5},{5,9},{9,13},{13,1},{2,6},{6,10},{... | collective-permute-start | bytes 1376264 | tf_op jit(solution)/shard_map/ppermute | solution.py:521
  253.0 32.5 %collective-permute-start.46 = (bf16[1024,256]{1,0:T(8,128)(2,1)S(1)}, bf16[1024,256]{1,0:T(8,128)(2,1)S(1)}, u32[]{:S(2)}, u32[]{:S(2)}) collective-permute-start(bf16[1024,256]{1,0:T(8,128)(2,1)S(1)} %copy-done.69), channel_id=1, source_target_pairs={{0,3},{1,2},{2,1},{3,0},{4,7},{5,6},{6,5},{7,4},{8,11},{9,10},{10,... | collective-permute-start | bytes 1572872 | tf_op jit(solution)/shard_map/ppermute | solution.py:463
  256.8 28.8 %collective-permute-start.45 = (bf16[640,256]{1,0:T(8,128)(2,1)S(1)}, bf16[640,256]{1,0:T(8,128)(2,1)S(1)}, u32[]{:S(2)}, u32[]{:S(2)}) collective-permute-start(bf16[640,256]{1,0:T(8,128)(2,1)S(1)} %get-tuple-element.318), channel_id=1, source_target_pairs={{0,12},{4,0},{8,4},{12,8},{1,13},{5,1},{9,5},{13,9},{2,14},{6,2},{... | collective-permute-start | bytes 983048 | tf_op jit(solution)/shard_map/ppermute | solution.py:541
  257.7 27.8 %collective-permute-start.44 = (bf16[640,256]{1,0:T(8,128)(2,1)S(1)}, bf16[640,256]{1,0:T(8,128)(2,1)S(1)}, u32[]{:S(2)}, u32[]{:S(2)}) collective-permute-start(bf16[640,256]{1,0:T(8,128)(2,1)S(1)} %get-tuple-element.319), channel_id=1, source_target_pairs={{0,8},{4,12},{8,0},{12,4},{1,9},{5,13},{9,1},{13,5},{2,10},{6,14},... | collective-permute-start | bytes 983048 | tf_op jit(solution)/shard_map/ppermute | solution.py:541
  257.7 27.8 %collective-permute-start.43 = (bf16[640,256]{1,0:T(8,128)(2,1)S(1)}, bf16[640,256]{1,0:T(8,128)(2,1)S(1)}, u32[]{:S(2)}, u32[]{:S(2)}) collective-permute-start(bf16[640,256]{1,0:T(8,128)(2,1)S(1)} %get-tuple-element.320), channel_id=1, source_target_pairs={{0,4},{4,8},{8,12},{12,0},{1,5},{5,9},{9,13},{13,1},{2,6},{6,10},{... | collective-permute-start | bytes 983048 | tf_op jit(solution)/shard_map/ppermute | solution.py:541
  299.5 15.1 %collective-permute-start.47 = (bf16[1024,256]{1,0:T(8,128)(2,1)}, bf16[1024,256]{1,0:T(8,128)(2,1)}, u32[]{:S(2)}, u32[]{:S(2)}) collective-permute-start(bf16[1024,256]{1,0:T(8,128)(2,1)} %get-tuple-element.251), channel_id=1, source_target_pairs={{0,1},{1,0},{2,3},{3,2},{4,5},{5,4},{6,7},{7,6},{8,9},{9,8},{10,11... | collective-permute-start | bytes 1572872 | tf_op jit(solution)/shard_map/ppermute | solution.py:463
  299.9 24.9 %collective-permute-start.48 = (bf16[1024,256]{1,0:T(8,128)(2,1)}, bf16[1024,256]{1,0:T(8,128)(2,1)}, u32[]{:S(2)}, u32[]{:S(2)}) collective-permute-start(bf16[1024,256]{1,0:T(8,128)(2,1)} %get-tuple-element.252), channel_id=1, source_target_pairs={{0,2},{1,3},{2,0},{3,1},{4,6},{5,7},{6,4},{7,5},{8,10},{9,11},{10,... | collective-permute-start | bytes 1572872 | tf_op jit(solution)/shard_map/ppermute | solution.py:463
  301.6 23.9 %collective-permute-start.49 = (bf16[1024,256]{1,0:T(8,128)(2,1)}, bf16[1024,256]{1,0:T(8,128)(2,1)}, u32[]{:S(2)}, u32[]{:S(2)}) collective-permute-start(bf16[1024,256]{1,0:T(8,128)(2,1)} %get-tuple-element.253), channel_id=1, source_target_pairs={{0,3},{1,2},{2,1},{3,0},{4,7},{5,6},{6,5},{7,4},{8,11},{9,10},{10,... | collective-permute-start | bytes 1572872 | tf_op jit(solution)/shard_map/ppermute | solution.py:463
  305.0 20.5 %collective-permute-start.51 = (bf16[256,896]{1,0:T(8,128)(2,1)}, bf16[256,896]{1,0:T(8,128)(2,1)}, u32[]{:S(2)}, u32[]{:S(2)}) collective-permute-start(bf16[256,896]{1,0:T(8,128)(2,1)} %add_convert_fusion.9), channel_id=1, source_target_pairs={{0,4},{4,8},{8,12},{12,0},{1,5},{5,9},{9,13},{13,1},{2,6},{6,10},{... | collective-permute-start | bytes 1376264 | tf_op jit(solution)/shard_map/ppermute | solution.py:521
  331.2 13.7 %collective-permute-start.60 = (bf16[256,896]{1,0:T(8,128)(2,1)}, bf16[256,896]{1,0:T(8,128)(2,1)}, u32[]{:S(2)}, u32[]{:S(2)}) collective-permute-start(bf16[256,896]{1,0:T(8,128)(2,1)} %add_convert_fusion.7), channel_id=1, source_target_pairs={{0,4},{4,8},{8,12},{12,0},{1,5},{5,9},{9,13},{13,1},{2,6},{6,10},{... | collective-permute-start | bytes 1376264 | tf_op jit(solution)/shard_map/ppermute | solution.py:521
  340.4 18.7 %collective-permute-start.55 = (f32[1024,256]{1,0:T(8,128)S(1)}, f32[1024,256]{1,0:T(8,128)}, u32[]{:S(2)}, u32[]{:S(2)}) collective-permute-start(f32[1024,256]{1,0:T(8,128)S(1)} %get-tuple-element.317), channel_id=1, source_target_pairs={{0,16},{16,0},{1,17},{17,1},{2,18},{18,2},{3,19},{19,3},{4,20},{20... | collective-permute-start | bytes 3145736 | tf_op jit(solution)/shard_map/ppermute | solution.py:463
  340.4 18.6 %collective-permute-start.59 = (f32[17152]{0:T(1024)S(1)}, f32[17152]{0:T(1024)S(1)}, u32[]{:S(2)}, u32[]{:S(2)}) collective-permute-start(f32[17152]{0:T(1024)S(1)} %select_add_fusion), channel_id=1, source_target_pairs={{0,12},{4,0},{8,4},{12,8},{1,13},{5,1},{9,5},{13,9},{2,14},{6,2},{... | collective-permute-start | bytes 205832 | tf_op jit(solution)/shard_map/ppermute | solution.py:532
  341.6 18.7 %collective-permute-start.58 = (f32[17152]{0:T(1024)S(1)}, f32[17152]{0:T(1024)S(1)}, u32[]{:S(2)}, u32[]{:S(2)}) collective-permute-start(f32[17152]{0:T(1024)S(1)} %select_add_fusion), channel_id=1, source_target_pairs={{0,8},{4,12},{8,0},{12,4},{1,9},{5,13},{9,1},{13,5},{2,10},{6,14},... | collective-permute-start | bytes 205832 | tf_op jit(solution)/shard_map/ppermute | solution.py:532
  343.0 17.3 %collective-permute-start.57 = (f32[17152]{0:T(1024)S(1)}, f32[17152]{0:T(1024)S(1)}, u32[]{:S(2)}, u32[]{:S(2)}) collective-permute-start(f32[17152]{0:T(1024)S(1)} %select_add_fusion), channel_id=1, source_target_pairs={{0,4},{4,8},{8,12},{12,0},{1,5},{5,9},{9,13},{13,1},{2,6},{6,10},{... | collective-permute-start | bytes 205832 | tf_op jit(solution)/shard_map/ppermute | solution.py:532
  (103 other events, 1163.8 us)

commit v5 on v4

--- a/solution.py
+++ b/solution.py
@@ -575,7 +575,7 @@
         compiler_params=params(20),
         cost_estimate=pl.CostEstimate(flops=4 * rows * m * n, transcendentals=0, bytes_accessed=4 * (rows * (m + n) + m * n)),
     )(jnp.stack([section, place]).astype(jnp.int32), left, *rights)
-    return own, swap(other, "section", 1)
+    return own, other
 
 
 def dct_table(order):
@@ -680,13 +680,15 @@
         return jnp.concatenate([gain_part, bias_part, fsum[0], diagonal.reshape(-1)])
 
     saved1, saved0 = saved_of(all1), saved_of(all0)
-    out_blocks1 = block_sends(out_block(*weight_gradient(saved1[6], pieces_g, section, place)), "dp")
+    own, other = weight_gradient(saved1[6], pieces_g, section, place)
+    out_blocks1 = block_sends(out_block(own, swap(other, "section", 1)), "dp")
     grad1_b = after(pieces_g, out_blocks1[0])
     parts, stats, dcat1, dmix1, fsum1 = run_backward(metas[1], grad1_b, saved1, weights1, True)
     parts, stats, dcat1, dmix1, fsum1 = after((parts, stats, dcat1, dmix1, fsum1), *out_blocks1, *out_sent[:2])
-    arrived = scatter_start(parts)
+    arrived, own, other = lax.optimization_barrier(
+        (scatter_start(parts), *weight_gradient(saved1[0], (dcat1,), section, place)))
     turn = scatter_turn(parts, arrived)
-    steps1 = list(ring_scatter(in_block(*weight_gradient(saved1[0], (dcat1,), section, place)), "dp"))
+    steps1 = list(ring_scatter(in_block(own, swap(other, "section", 1)), "dp"))
     arrivals1, red_in1 = [arrival for arrival, _ in steps1], steps1[-1][1]
     d_normed = scatter_end(parts, arrived, *turn)
     sums = mp_total(after(stats, *turn))
@@ -696,15 +698,16 @@
     pieces_g0 = after(pieces_g0, *arrivals1[2:3])
     out = hidden.astype(F32) + out_kept + out_sent[0].astype(F32) + out_sent[1].astype(F32) + out_sent[2].astype(F32)
 
-    out_blocks0 = block_sends(out_block(*weight_gradient(saved0[6], pieces_g0, section, place)), "dp")
+    own, other = weight_gradient(saved0[6], pieces_g0, section, place)
+    out_blocks0 = block_sends(out_block(own, swap(other, "section", 1)), "dp")
     grad0_b = after(pieces_g0, out_blocks0[0])
     parts, stats, dcat0, dmix0, fsum0 = run_backward(metas[0], grad0_b, saved0, weights0, False)
     parts, stats, dcat0, dmix0, fsum0 = after((parts, stats, dcat0, dmix0, fsum0), *out_blocks0, out_sent[2])
     out_blocks1 = after(out_blocks1, dcat0)
     kept, sent = direct_sends(parts)
-    mine0, arrived0 = weight_gradient(saved0[0], (dcat0,), section, place)
-    block0 = in_block(mine0, arrived0)
-    meanwhile = list(sent)
+    sent[:2], own, other = lax.optimization_barrier((sent[:2], *weight_gradient(saved0[0], (dcat0,), section, place)))
+    block0 = in_block(own, swap(other, "section", 1))
+    meanwhile = sent[2:]
     ring0 = ring_scatter(block0, "dp", meanwhile)
     steps0 = [next(ring0)]
     meanwhile.clear()

time: 371 us -> 359 us (0.968)
  waiting for transfers between devices: 106 us -> 96.9 us
    ppermute x49, waiting for transfers between devices: 74.7 us -> 55.4 us  [swap(): lax.ppermute(value, axis, [(k, k ^ by) for k in range(lax.axis_size(axis))])]
    ppermute x6, waiting for transfers between devices: 30.2 us -> 39.9 us  [ring_scatter(): arrived = lax.ppermute(total, axis, pairs)]
    ppermute x6, starting transfers between devices: 9.52 us -> 5.06 us  [ring_scatter(): arrived = lax.ppermute(total, axis, pairs)]
    unnamed x143 -> x151, local copies, waits for them, and re-layouts: 10.1 us -> 11.1 us
  transfers between devices with their start and end apart: 64 -> 64, of which waited for: 26 -> 27; matrix products, arithmetic and copies ran while one was open for 14% -> 14% of each run, Pallas kernels for 26% -> 32%
where the time goes in v5:
time: 359 us; the launch traced here: 358 us
  Pallas kernels  130 us (36%)
  waiting for transfers between devices  96.9 us (27%)
  starting transfers between devices  58.2 us (16%)
  other arithmetic  37.7 us (11%)
  local copies, waits for them, and re-layouts  31.3 us (9%)
    ppermute x49, waiting for transfers between devices, swap(): lax.ppermute(value, axis, [(k, k ^ by) for k in range(lax.axis_size(axis))])  55.4 us
    pallas_call x2, Pallas kernels, backward_layer(): pl.pallas_call(functools.partial(backward_kernel, carry is not None, phas...  53.6 us
    pallas_call x2, Pallas kernels, forward_layer(): pl.pallas_call(functools.partial(forward_kernel, carry is not None, phase...  44.4 us
    ppermute x49, starting transfers between devices, swap(): lax.ppermute(value, axis, [(k, k ^ by) for k in range(lax.axis_size(axis))])  41.9 us
    ppermute x6, waiting for transfers between devices, ring_scatter(): arrived = lax.ppermute(total, axis, pairs)  39.9 us
    pallas_call x4, Pallas kernels, weight_gradient(): pl.pallas_call(functools.partial(product_kernel, steps), name='weight_gra...  32 us
    unnamed x151, local copies, waits for them, and re-layouts  11.1 us
  transfers between devices with their start and end apart: 64, of which 27 were waited for; matrix products, arithmetic and copies ran while one was open for 14% of the time, Pallas kernels for 32%

profile of v5, /device:TPU:0, one launch (start us, length us, event | category | flops | bytes accessed | tf_op | source)
XLA Modules:
  0.0 357.5 jit_solution(11952317366591114266)
XLA Ops:
  1.9 3.1 collective-permute-start.1
  11.4 2.9 multiply_select_fusion
  25.7 4.1 %collective-permute-done.5.refs_6_ = bf16[1024,128]{1,0:T(8,128)(2,1)S(1)} collective-permute-done((bf16[1024,128]{1,0:T(8,128)(2,1)S(1)}, bf16[1024,128]{1,0:T(8,128)(2,1)S(1)}, u32[]{:S(2)}, u32[]{:S(2)}) %collective-permute-start.5) | collective-permute-done | bytes 262176 | tf_op jit(solution)/shard_map/ppermute | solution.py:463
  32.5 22.5 %layer_forward.2 = (bf16[2,1024,128]{2,1,0:T(8,128)(2,1)}, bf16[2,1024,128]{2,1,0:T(8,128)(2,1)}, f32[1024,256]{1,0:T(8,128)}, f32[1024,128]{1,0:T(8,128)}, f32[...) custom-call(s32[2]{0:T(128)} %pad_add_fusion.2.refs_0_, ...), custom_call_target="tpu_custom_call" | custom-call | flops 20480000000 | bytes 25165824 | tf_op jit(solution)/shard_map/layer_forward/pallas_call | solution.py:407
  57.2 10.8 %collective-permute-done.11 = bf16[2,1024,128]{2,1,0:T(8,128)(2,1)S(1)} collective-permute-done((bf16[2,1024,128]{2,1,0:T(8,128)(2,1)}, bf16[2,1024,128]{2,1,0:T(8,128)(2,1)S(1)}, u32[]{:S(2)}, u32[]{:S(2)}) %collective-permute-start.11) | collective-permute-done | bytes 524320 | tf_op jit(solution)/shard_map/ppermute | solution.py:463
  72.7 2.9 collective-permute-done.12
  75.5 2.2 collective-permute-done.14
  80.4 8.2 %collective-permute-done.16.refs_4_ = bf16[1024,256]{1,0:T(8,128)(2,1)} collective-permute-done((bf16[1024,256]{1,0:T(8,128)(2,1)S(1)}, bf16[1024,256]{1,0:T(8,128)(2,1)}, u32[]{:S(2)}, u32[]{:S(2)}) %collective-permute-start.16) | collective-permute-done | bytes 524320 | tf_op jit(solution)/shard_map/ppermute | solution.py:463
  96.2 5.6 %collective-permute-done.17.refs_5_ = bf16[1024,128]{1,0:T(8,128)(2,1)} collective-permute-done((bf16[1024,128]{1,0:T(8,128)(2,1)}, bf16[1024,128]{1,0:T(8,128)(2,1)}, u32[]{:S(2)}, u32[]{:S(2)}) %collective-permute-start.17) | collective-permute-done | bytes 262176 | tf_op jit(solution)/shard_map/ppermute | solution.py:463
  102.2 2.5 collective-permute-start.19
  104.7 21.9 %layer_forward.3 = (f32[1024,256]{1,0:T(8,128)}, bf16[1024,256]{1,0:T(8,128)(2,1)}, bf16[1024,256]{1,0:T(8,128)(2,1)}, bf16[1024,256]{1,0:T(8,128)(2,1)}, bf16[1...) custom-call(s32[2]{0:T(128)} %pad_add_fusion.refs_0_, ...), custom_call_target="tpu_custom_call" | custom-call | flops 20480000000 | bytes 25165824 | tf_op jit(solution)/shard_map/layer_forward/pallas_call | solution.py:407
  128.6 7.8 %weight_gradient.4 = (bf16[640,1024]{1,0:T(8,128)(2,1)}, bf16[640,1024]{1,0:T(8,128)(2,1)S(1)}) custom-call(s32[2]{0:T(128)S(1)} %pad_add_fusion.3.meta, bf16[1024,1280]{1,0:T(8,128)(2,1)S(1)} %copy-done.16, bf16[1024,256]{1,0:T(8,128)(2,1)S(1)} %dynamic-slice_bitcast_fusion.1.refs_0_.refs_1_, bf16[1024,256]{1,0:T(8,128)(2,1)S(1)} %collective-permute-done.9.refs_1_.refs_2_, ...), custom_call_target="tpu_custom_call" | custom-call | flops 2684354560 | bytes 9437184 | tf_op jit(solution)/shard_map/weight_gradient/pallas_call | solution.py:565
  139.9 2.5 add_convert_fusion.21
  142.4 3.6 %collective-permute-start.24 = (bf16[640,256]{1,0:T(8,128)(2,1)S(1)}, bf16[640,256]{1,0:T(8,128)(2,1)S(1)}, u32[]{:S(2)}, u32[]{:S(2)}) collective-permute-start(bf16[640,256]{1,0:T(8,128)(2,1)S(1)} %get-tuple-element.338), channel_id=1, source_target_pairs={{0,12},{4,0},{8,4},{12,8},{1,13},{5,1},{9,5},{13,9},{2,14},{6,2},{... | collective-permute-start | bytes 983048 | tf_op jit(solution)/shard_map/ppermute | solution.py:541
  147.0 27.0 %layer_backward.2 = (bf16[2,1024,128]{2,1,0:T(8,128)(2,1)}, bf16[2,1024,128]{2,1,0:T(8,128)(2,1)}, f32[1024,256]{1,0:T(8,128)}, f32[1024,128]{1,0:T(8,128)}, f32...) custom-call(s32[2]{0:T(128)} %pad_add_fusion.refs_0_, ...), custom_call_target="tpu_custom_call" | custom-call | flops 25600000000 | bytes 25165824 | tf_op jit(solution)/shard_map/layer_backward/pallas_call | solution.py:447
  177.6 8.7 %weight_gradient.5 = (bf16[1024,896]{1,0:T(8,128)(2,1)}, bf16[1024,896]{1,0:T(8,128)(2,1)S(1)}) custom-call(s32[2]{0:T(128)S(1)} %pad_add_fusion.3.meta, bf16[1024,1024]{1,0:T(8,128)(2,1)S(1)} %copy-done.20, bf16[1024,1792]{1,0:T(8,128)(2,1)S(1)} %copy-done.18), custom_call_target="tpu_custom_call" | custom-call | flops 3758096384 | bytes 11534336 | tf_op jit(solution)/shard_map/weight_gradient/pallas_call | solution.py:565
  197.0 2.5 collective-permute-start.35
  201.3 9.6 %collective-permute-done.35 = bf16[256,896]{1,0:T(8,128)(2,1)S(1)} collective-permute-done((bf16[256,896]{1,0:T(8,128)(2,1)S(1)}, bf16[256,896]{1,0:T(8,128)(2,1)S(1)}, u32[]{:S(2)}, u32[]{:S(2)}) %collective-permute-start.35) | collective-permute-done | bytes 458784 | tf_op jit(solution)/shard_map/ppermute | solution.py:521
  215.7 9.5 %collective-permute-done.38 = bf16[256,896]{1,0:T(8,128)(2,1)S(1)} collective-permute-done((bf16[256,896]{1,0:T(8,128)(2,1)S(1)}, bf16[256,896]{1,0:T(8,128)(2,1)S(1)}, u32[]{:S(2)}, u32[]{:S(2)}) %collective-permute-start.38) | collective-permute-done | bytes 458784 | tf_op jit(solution)/shard_map/ppermute | solution.py:521
  229.5 3.8 %collective-permute-done.40.refs_4_.refs_5_ = bf16[1024,128]{1,0:T(8,128)(2,1)S(1)} collective-permute-done((bf16[1024,128]{1,0:T(8,128)(2,1)S(1)}, bf16[1024,128]{1,0:T(8,128)(2,1)S(1)}, u32[]{:S(2)}, u32[]{:S(2)}) %collective-permute-start.40) | collective-permute-done | bytes 262176 | tf_op jit(solution)/shard_map/ppermute | solution.py:463
  234.5 4.1 %collective-permute-done.41 = bf16[256,896]{1,0:T(8,128)(2,1)S(1)} collective-permute-done((bf16[256,896]{1,0:T(8,128)(2,1)S(1)}, bf16[256,896]{1,0:T(8,128)(2,1)S(1)}, u32[]{:S(2)}, u32[]{:S(2)}) %collective-permute-start.41) | collective-permute-done | bytes 458784 | tf_op jit(solution)/shard_map/ppermute | solution.py:521
  238.6 6.7 %weight_gradient.6 = (bf16[640,1024]{1,0:T(8,128)(2,1)S(1)}, bf16[640,1024]{1,0:T(8,128)(2,1)S(1)}) custom-call(s32[2]{0:T(128)S(1)} %pad_add_fusion.3.meta, bf16[1024,1280]{1,0:T(8,128)(2,1)S(1)} %copy-done.15, bf16[1024,256]{1,0:T(8,128)(2,1)S(1)} %get-tuple-element.237.refs_0_.refs_1_, bf16[1024,256]{1,0:T(8,128)(2,1)S(1)} %collective-permute-done.36.refs_1_.refs_2_, ...), custom_call_target="tpu_custom_call" | custom-call | flops 2684354560 | bytes 9437184 | tf_op jit(solution)/shard_map/weight_gradient/pallas_call | solution.py:565
  251.3 26.6 %layer_backward.3 = (f32[1024,256]{1,0:T(8,128)}, bf16[1024,256]{1,0:T(8,128)(2,1)}, bf16[1024,256]{1,0:T(8,128)(2,1)}, bf16[1024,256]{1,0:T(8,128)(2,1)}, f32[8...) custom-call(s32[2]{0:T(128)} %pad_add_fusion.2.refs_0_, ...), custom_call_target="tpu_custom_call" | custom-call | flops 25600000000 | bytes 25165824 | tf_op jit(solution)/shard_map/layer_backward/pallas_call | solution.py:447
  281.7 8.7 %weight_gradient.7 = (bf16[1024,896]{1,0:T(8,128)(2,1)}, bf16[1024,896]{1,0:T(8,128)(2,1)S(1)}) custom-call(s32[2]{0:T(128)S(1)} %pad_add_fusion.3.meta, bf16[1024,1024]{1,0:T(8,128)(2,1)S(1)} %copy-done.19, bf16[1024,1792]{1,0:T(8,128)(2,1)S(1)} %copy-done.17), custom_call_target="tpu_custom_call" | custom-call | flops 3758096384 | bytes 11534336 | tf_op jit(solution)/shard_map/weight_gradient/pallas_call | solution.py:565
  303.9 5.4 %collective-permute-done.49 = bf16[1024,256]{1,0:T(8,128)(2,1)} collective-permute-done((bf16[1024,256]{1,0:T(8,128)(2,1)}, bf16[1024,256]{1,0:T(8,128)(2,1)}, u32[]{:S(2)}, u32[]{:S(2)}) %collective-permute-start.49) | collective-permute-done | bytes 524320 | tf_op jit(solution)/shard_map/ppermute | solution.py:463
  309.3 4.0 %collective-permute-done.51 = bf16[256,896]{1,0:T(8,128)(2,1)} collective-permute-done((bf16[256,896]{1,0:T(8,128)(2,1)}, bf16[256,896]{1,0:T(8,128)(2,1)}, u32[]{:S(2)}, u32[]{:S(2)}) %collective-permute-start.51) | collective-permute-done | bytes 458784 | tf_op jit(solution)/shard_map/ppermute | solution.py:521
  313.2 2.2 add_convert_fusion.7
  319.3 2.1 multiply_reduce_fusion.1
  325.5 3.9 %collective-permute-start.59 = (f32[17152]{0:T(1024)S(1)}, f32[17152]{0:T(1024)S(1)}, u32[]{:S(2)}, u32[]{:S(2)}) collective-permute-start(f32[17152]{0:T(1024)S(1)} %select_add_fusion), channel_id=1, source_target_pairs={{0,12},{4,0},{8,4},{12,8},{1,13},{5,1},{9,5},{13,9},{2,14},{6,2},{... | collective-permute-start | bytes 205832 | tf_op jit(solution)/shard_map/ppermute | solution.py:532
  330.2 2.9 collective-permute-done.60
  336.4 9.8 %collective-permute-done.61 = bf16[256,896]{1,0:T(8,128)(2,1)S(1)} collective-permute-done((bf16[256,896]{1,0:T(8,128)(2,1)S(1)}, bf16[256,896]{1,0:T(8,128)(2,1)S(1)}, u32[]{:S(2)}, u32[]{:S(2)}) %collective-permute-start.61) | collective-permute-done | bytes 458784 | tf_op jit(solution)/shard_map/ppermute | solution.py:521
  351.5 3.1 maximum_select_fusion
  (350 shorter events, 114.3 us)
Async XLA Ops:
  1.9 15.0 %collective-permute-start.1 = (bf16[1024,256]{1,0:T(8,128)(2,1)S(1)}, bf16[1024,256]{1,0:T(8,128)(2,1)S(1)}, u32[]{:S(2)}, u32[]{:S(2)}) collective-permute-start(bf16[1024,256]{1,0:T(8,128)(2,1)S(1)} %dynamic-slice_bitcast_fusion.refs_2_), channel_id=1, source_target_pairs={{0,2},{1,3},{2,0},{3,1},{4,6},{5,7},{6,4},{7,5},{8,10},{9,11},{10,... | collective-permute-start | bytes 1572872 | tf_op jit(solution)/shard_map/ppermute | solution.py:463
  4.9 13.5 %collective-permute-start = (bf16[1024,256]{1,0:T(8,128)(2,1)S(1)}, bf16[1024,256]{1,0:T(8,128)(2,1)}, u32[]{:S(2)}, u32[]{:S(2)}) collective-permute-start(bf16[1024,256]{1,0:T(8,128)(2,1)S(1)} %dynamic-slice_bitcast_fusion.refs_2_), channel_id=1, source_target_pairs={{0,1},{1,0},{2,3},{3,2},{4,5},{5,4},{6,7},{7,6},{8,9},{9,8},{10,11... | collective-permute-start | bytes 1572872 | tf_op jit(solution)/shard_map/ppermute | solution.py:463
  8.9 23.6 %collective-permute-start.7 = (bf16[1,1024,1024]{2,1,0:T(8,128)(2,1)}, bf16[1,1024,1024]{2,1,0:T(8,128)(2,1)}, u32[]{:S(2)}, u32[]{:S(2)}) collective-permute-start(bf16[1,1024,1024]{2,1,0:T(8,128)(2,1)} %refs_23_.3), channel_id=1, source_target_pairs={{0,16},{16,0},{1,17},{17,1},{2,18},{18,2},{3,19},{19,3},{4,20},{20... | collective-permute-start | bytes 6291464 | tf_op jit(solution)/shard_map/ppermute | solution.py:463
  9.4 23.1 %collective-permute-start.8 = (bf16[1,1024,1024]{2,1,0:T(8,128)(2,1)}, bf16[1,1024,1024]{2,1,0:T(8,128)(2,1)}, u32[]{:S(2)}, u32[]{:S(2)}) collective-permute-start(bf16[1,1024,1024]{2,1,0:T(8,128)(2,1)} %refs_25_.3), channel_id=1, source_target_pairs={{0,16},{16,0},{1,17},{17,1},{2,18},{18,2},{3,19},{19,3},{4,20},{20... | collective-permute-start | bytes 6291464 | tf_op jit(solution)/shard_map/ppermute | solution.py:463
  15.5 17.0 %collective-permute-start.6 = (bf16[1,3,1024,256]{3,2,1,0:T(8,128)(2,1)}, bf16[1,3,1024,256]{3,2,1,0:T(8,128)(2,1)}, u32[]{:S(2)}, u32[]{:S(2)}) collective-permute-start(bf16[1,3,1024,256]{3,2,1,0:T(8,128)(2,1)} %refs_22_.3), channel_id=1, source_target_pairs={{0,16},{16,0},{1,17},{17,1},{2,18},{18,2},{3,19},{19,3},{4,20},{20... | collective-permute-start | bytes 4718600 | tf_op jit(solution)/shard_map/ppermute | solution.py:463
  30.4 24.6 %collective-permute-start.10 = (bf16[1024,256]{1,0:T(8,128)(2,1)S(1)}, bf16[1024,256]{1,0:T(8,128)(2,1)S(1)}, u32[]{:S(2)}, u32[]{:S(2)}) collective-permute-start(bf16[1024,256]{1,0:T(8,128)(2,1)S(1)} %dynamic-slice_bitcast_fusion.1.refs_0_.refs_1_), channel_id=1, source_target_pairs={{0,2},{1,3},{2,0},{3,1},{4,6},{5,7},{6,4},{7,5},{8,10},{9,11},{10,... | collective-permute-start | bytes 1572872 | tf_op jit(solution)/shard_map/ppermute | solution.py:463
  31.6 23.4 %collective-permute-start.9 = (bf16[1024,256]{1,0:T(8,128)(2,1)S(1)}, bf16[1024,256]{1,0:T(8,128)(2,1)S(1)}, u32[]{:S(2)}, u32[]{:S(2)}) collective-permute-start(bf16[1024,256]{1,0:T(8,128)(2,1)S(1)} %dynamic-slice_bitcast_fusion.1.refs_0_.refs_1_), channel_id=1, source_target_pairs={{0,1},{1,0},{2,3},{3,2},{4,5},{5,4},{6,7},{7,6},{8,9},{9,8},{10,11... | collective-permute-start | bytes 1572872 | tf_op jit(solution)/shard_map/ppermute | solution.py:463
  56.3 13.8 %collective-permute-start.13 = (bf16[2,1024,128]{2,1,0:T(8,128)(2,1)}, bf16[2,1024,128]{2,1,0:T(8,128)(2,1)S(1)}, u32[]{:S(2)}, u32[]{:S(2)}) collective-permute-start(bf16[2,1024,128]{2,1,0:T(8,128)(2,1)} %get-tuple-element.169), channel_id=1, source_target_pairs={{0,2},{1,3},{2,0},{3,1},{4,6},{5,7},{6,4},{7,5},{8,10},{9,11},{10,... | collective-permute-start | bytes 1572872 | tf_op jit(solution)/shard_map/ppermute | solution.py:463
  101.9 24.8 %collective-permute-start.20 = (bf16[1024,128]{1,0:T(8,128)(2,1)S(1)}, bf16[1024,128]{1,0:T(8,128)(2,1)S(1)}, u32[]{:S(2)}, u32[]{:S(2)}) collective-permute-start(bf16[1024,128]{1,0:T(8,128)(2,1)S(1)} %slice.192), channel_id=1, source_target_pairs={{0,1},{1,0},{2,3},{3,2},{4,5},{5,4},{6,7},{7,6},{8,9},{9,8},{10,11... | collective-permute-start | bytes 786440 | tf_op jit(solution)/shard_map/ppermute | solution.py:463
  102.2 24.5 %collective-permute-start.19 = (bf16[1024,128]{1,0:T(8,128)(2,1)S(1)}, bf16[1024,128]{1,0:T(8,128)(2,1)S(1)}, u32[]{:S(2)}, u32[]{:S(2)}) collective-permute-start(bf16[1024,128]{1,0:T(8,128)(2,1)S(1)} %slice.191), channel_id=1, source_target_pairs={{0,2},{1,3},{2,0},{3,1},{4,6},{5,7},{6,4},{7,5},{8,10},{9,11},{10,... | collective-permute-start | bytes 786440 | tf_op jit(solution)/shard_map/ppermute | solution.py:463
  136.5 37.5 %collective-permute-start.25 = (bf16[1024,256]{1,0:T(8,128)(2,1)}, bf16[1024,256]{1,0:T(8,128)(2,1)S(1)}, u32[]{:S(2)}, u32[]{:S(2)}) collective-permute-start(bf16[1024,256]{1,0:T(8,128)(2,1)} %get-tuple-element.206), channel_id=1, source_target_pairs={{0,1},{1,0},{2,3},{3,2},{4,5},{5,4},{6,7},{7,6},{8,9},{9,8},{10,11... | collective-permute-start | bytes 1572872 | tf_op jit(solution)/shard_map/ppermute | solution.py:463
  136.6 37.4 %collective-permute-start.26 = (bf16[1024,256]{1,0:T(8,128)(2,1)}, bf16[1024,256]{1,0:T(8,128)(2,1)S(1)}, u32[]{:S(2)}, u32[]{:S(2)}) collective-permute-start(bf16[1024,256]{1,0:T(8,128)(2,1)} %get-tuple-element.207), channel_id=1, source_target_pairs={{0,2},{1,3},{2,0},{3,1},{4,6},{5,7},{6,4},{7,5},{8,10},{9,11},{10,... | collective-permute-start | bytes 1572872 | tf_op jit(solution)/shard_map/ppermute | solution.py:463
  142.4 31.7 %collective-permute-start.24 = (bf16[640,256]{1,0:T(8,128)(2,1)S(1)}, bf16[640,256]{1,0:T(8,128)(2,1)S(1)}, u32[]{:S(2)}, u32[]{:S(2)}) collective-permute-start(bf16[640,256]{1,0:T(8,128)(2,1)S(1)} %get-tuple-element.338), channel_id=1, source_target_pairs={{0,12},{4,0},{8,4},{12,8},{1,13},{5,1},{9,5},{13,9},{2,14},{6,2},{... | collective-permute-start | bytes 983048 | tf_op jit(solution)/shard_map/ppermute | solution.py:541
  146.0 28.2 %collective-permute-start.23 = (bf16[640,256]{1,0:T(8,128)(2,1)S(1)}, bf16[640,256]{1,0:T(8,128)(2,1)S(1)}, u32[]{:S(2)}, u32[]{:S(2)}) collective-permute-start(bf16[640,256]{1,0:T(8,128)(2,1)S(1)} %get-tuple-element.339), channel_id=1, source_target_pairs={{0,8},{4,12},{8,0},{12,4},{1,9},{5,13},{9,1},{13,5},{2,10},{6,14},... | collective-permute-start | bytes 983048 | tf_op jit(solution)/shard_map/ppermute | solution.py:541
  146.0 28.2 %collective-permute-start.22 = (bf16[640,256]{1,0:T(8,128)(2,1)S(1)}, bf16[640,256]{1,0:T(8,128)(2,1)S(1)}, u32[]{:S(2)}, u32[]{:S(2)}) collective-permute-start(bf16[640,256]{1,0:T(8,128)(2,1)S(1)} %get-tuple-element.340), channel_id=1, source_target_pairs={{0,4},{4,8},{8,12},{12,0},{1,5},{5,9},{9,13},{13,1},{2,6},{6,10},{... | collective-permute-start | bytes 983048 | tf_op jit(solution)/shard_map/ppermute | solution.py:541
  174.2 13.4 %collective-permute-start.27 = (bf16[2,1024,128]{2,1,0:T(8,128)(2,1)}, bf16[2,1024,128]{2,1,0:T(8,128)(2,1)S(1)}, u32[]{:S(2)}, u32[]{:S(2)}) collective-permute-start(bf16[2,1024,128]{2,1,0:T(8,128)(2,1)} %get-tuple-element.209), channel_id=1, source_target_pairs={{0,1},{1,0},{2,3},{3,2},{4,5},{5,4},{6,7},{7,6},{8,9},{9,8},{10,11... | collective-permute-start | bytes 1572872 | tf_op jit(solution)/shard_map/ppermute | solution.py:463
  174.3 14.1 %collective-permute-start.28 = (bf16[2,1024,128]{2,1,0:T(8,128)(2,1)}, bf16[2,1024,128]{2,1,0:T(8,128)(2,1)S(1)}, u32[]{:S(2)}, u32[]{:S(2)}) collective-permute-start(bf16[2,1024,128]{2,1,0:T(8,128)(2,1)} %get-tuple-element.210), channel_id=1, source_target_pairs={{0,2},{1,3},{2,0},{3,1},{4,6},{5,7},{6,4},{7,5},{8,10},{9,11},{10,... | collective-permute-start | bytes 1572872 | tf_op jit(solution)/shard_map/ppermute | solution.py:463
  197.0 13.9 %collective-permute-start.35 = (bf16[256,896]{1,0:T(8,128)(2,1)S(1)}, bf16[256,896]{1,0:T(8,128)(2,1)S(1)}, u32[]{:S(2)}, u32[]{:S(2)}) collective-permute-start(bf16[256,896]{1,0:T(8,128)(2,1)S(1)} %add_convert_fusion.14), channel_id=1, source_target_pairs={{0,4},{4,8},{8,12},{12,0},{1,5},{5,9},{9,13},{13,1},{2,6},{6,10},{... | collective-permute-start | bytes 1376264 | tf_op jit(solution)/shard_map/ppermute | solution.py:521
  199.7 13.1 %collective-permute-start.29 = (bf16[1024,128]{1,0:T(8,128)(2,1)S(1)}, bf16[1024,128]{1,0:T(8,128)(2,1)S(1)}, u32[]{:S(2)}, u32[]{:S(2)}) collective-permute-start(bf16[1024,128]{1,0:T(8,128)(2,1)S(1)} %fusion.6), channel_id=1, source_target_pairs={{0,2},{1,3},{2,0},{3,1},{4,6},{5,7},{6,4},{7,5},{8,10},{9,11},{10,... | collective-permute-start | bytes 786440 | tf_op jit(solution)/shard_map/ppermute | solution.py:463
  245.5 32.5 %collective-permute-start.46 = (bf16[1024,256]{1,0:T(8,128)(2,1)S(1)}, bf16[1024,256]{1,0:T(8,128)(2,1)S(1)}, u32[]{:S(2)}, u32[]{:S(2)}) collective-permute-start(bf16[1024,256]{1,0:T(8,128)(2,1)S(1)} %copy-done.73), channel_id=1, source_target_pairs={{0,3},{1,2},{2,1},{3,0},{4,7},{5,6},{6,5},{7,4},{8,11},{9,10},{10,... | collective-permute-start | bytes 1572872 | tf_op jit(solution)/shard_map/ppermute | solution.py:463
  249.2 28.7 %collective-permute-start.45 = (bf16[640,256]{1,0:T(8,128)(2,1)S(1)}, bf16[640,256]{1,0:T(8,128)(2,1)S(1)}, u32[]{:S(2)}, u32[]{:S(2)}) collective-permute-start(bf16[640,256]{1,0:T(8,128)(2,1)S(1)} %get-tuple-element.334), channel_id=1, source_target_pairs={{0,12},{4,0},{8,4},{12,8},{1,13},{5,1},{9,5},{13,9},{2,14},{6,2},{... | collective-permute-start | bytes 983048 | tf_op jit(solution)/shard_map/ppermute | solution.py:541
  249.3 28.7 %collective-permute-start.44 = (bf16[640,256]{1,0:T(8,128)(2,1)S(1)}, bf16[640,256]{1,0:T(8,128)(2,1)S(1)}, u32[]{:S(2)}, u32[]{:S(2)}) collective-permute-start(bf16[640,256]{1,0:T(8,128)(2,1)S(1)} %get-tuple-element.335), channel_id=1, source_target_pairs={{0,8},{4,12},{8,0},{12,4},{1,9},{5,13},{9,1},{13,5},{2,10},{6,14},... | collective-permute-start | bytes 983048 | tf_op jit(solution)/shard_map/ppermute | solution.py:541
  249.3 28.6 %collective-permute-start.43 = (bf16[640,256]{1,0:T(8,128)(2,1)S(1)}, bf16[640,256]{1,0:T(8,128)(2,1)S(1)}, u32[]{:S(2)}, u32[]{:S(2)}) collective-permute-start(bf16[640,256]{1,0:T(8,128)(2,1)S(1)} %get-tuple-element.336), channel_id=1, source_target_pairs={{0,4},{4,8},{8,12},{12,0},{1,5},{5,9},{9,13},{13,1},{2,6},{6,10},{... | collective-permute-start | bytes 983048 | tf_op jit(solution)/shard_map/ppermute | solution.py:541
  278.0 13.7 %collective-permute-start.47 = (bf16[1024,256]{1,0:T(8,128)(2,1)}, bf16[1024,256]{1,0:T(8,128)(2,1)S(1)}, u32[]{:S(2)}, u32[]{:S(2)}) collective-permute-start(bf16[1024,256]{1,0:T(8,128)(2,1)} %get-tuple-element.263), channel_id=1, source_target_pairs={{0,1},{1,0},{2,3},{3,2},{4,5},{5,4},{6,7},{7,6},{8,9},{9,8},{10,11... | collective-permute-start | bytes 1572872 | tf_op jit(solution)/shard_map/ppermute | solution.py:463
  279.0 13.4 %collective-permute-start.48 = (bf16[1024,256]{1,0:T(8,128)(2,1)}, bf16[1024,256]{1,0:T(8,128)(2,1)}, u32[]{:S(2)}, u32[]{:S(2)}) collective-permute-start(bf16[1024,256]{1,0:T(8,128)(2,1)} %get-tuple-element.264), channel_id=1, source_target_pairs={{0,2},{1,3},{2,0},{3,1},{4,6},{5,7},{6,4},{7,5},{8,10},{9,11},{10,... | collective-permute-start | bytes 1572872 | tf_op jit(solution)/shard_map/ppermute | solution.py:463
  293.7 15.6 %collective-permute-start.49 = (bf16[1024,256]{1,0:T(8,128)(2,1)}, bf16[1024,256]{1,0:T(8,128)(2,1)}, u32[]{:S(2)}, u32[]{:S(2)}) collective-permute-start(bf16[1024,256]{1,0:T(8,128)(2,1)} %get-tuple-element.270), channel_id=1, source_target_pairs={{0,3},{1,2},{2,1},{3,0},{4,7},{5,6},{6,5},{7,4},{8,11},{9,10},{10,... | collective-permute-start | bytes 1572872 | tf_op jit(solution)/shard_map/ppermute | solution.py:463
  298.6 14.7 %collective-permute-start.51 = (bf16[256,896]{1,0:T(8,128)(2,1)}, bf16[256,896]{1,0:T(8,128)(2,1)}, u32[]{:S(2)}, u32[]{:S(2)}) collective-permute-start(bf16[256,896]{1,0:T(8,128)(2,1)} %add_convert_fusion.9), channel_id=1, source_target_pairs={{0,4},{4,8},{8,12},{12,0},{1,5},{5,9},{9,13},{13,1},{2,6},{6,10},{... | collective-permute-start | bytes 1376264 | tf_op jit(solution)/shard_map/ppermute | solution.py:521
  319.0 14.1 %collective-permute-start.60 = (bf16[256,896]{1,0:T(8,128)(2,1)}, bf16[256,896]{1,0:T(8,128)(2,1)}, u32[]{:S(2)}, u32[]{:S(2)}) collective-permute-start(bf16[256,896]{1,0:T(8,128)(2,1)} %add_convert_fusion.7), channel_id=1, source_target_pairs={{0,4},{4,8},{8,12},{12,0},{1,5},{5,9},{9,13},{13,1},{2,6},{6,10},{... | collective-permute-start | bytes 1376264 | tf_op jit(solution)/shard_map/ppermute | solution.py:521
  325.4 20.7 %collective-permute-start.55 = (f32[1024,256]{1,0:T(8,128)S(1)}, f32[1024,256]{1,0:T(8,128)}, u32[]{:S(2)}, u32[]{:S(2)}) collective-permute-start(f32[1024,256]{1,0:T(8,128)S(1)} %get-tuple-element.333), channel_id=1, source_target_pairs={{0,16},{16,0},{1,17},{17,1},{2,18},{18,2},{3,19},{19,3},{4,20},{20... | collective-permute-start | bytes 3145736 | tf_op jit(solution)/shard_map/ppermute | solution.py:463
  325.5 20.7 %collective-permute-start.59 = (f32[17152]{0:T(1024)S(1)}, f32[17152]{0:T(1024)S(1)}, u32[]{:S(2)}, u32[]{:S(2)}) collective-permute-start(f32[17152]{0:T(1024)S(1)} %select_add_fusion), channel_id=1, source_target_pairs={{0,12},{4,0},{8,4},{12,8},{1,13},{5,1},{9,5},{13,9},{2,14},{6,2},{... | collective-permute-start | bytes 205832 | tf_op jit(solution)/shard_map/ppermute | solution.py:532
  329.3 18.3 %collective-permute-start.58 = (f32[17152]{0:T(1024)S(1)}, f32[17152]{0:T(1024)S(1)}, u32[]{:S(2)}, u32[]{:S(2)}) collective-permute-start(f32[17152]{0:T(1024)S(1)} %select_add_fusion), channel_id=1, source_target_pairs={{0,8},{4,12},{8,0},{12,4},{1,9},{5,13},{9,1},{13,5},{2,10},{6,14},... | collective-permute-start | bytes 205832 | tf_op jit(solution)/shard_map/ppermute | solution.py:532
  329.5 18.2 %collective-permute-start.57 = (f32[17152]{0:T(1024)S(1)}, f32[17152]{0:T(1024)S(1)}, u32[]{:S(2)}, u32[]{:S(2)}) collective-permute-start(f32[17152]{0:T(1024)S(1)} %select_add_fusion), channel_id=1, source_target_pairs={{0,4},{4,8},{8,12},{12,0},{1,5},{5,9},{9,13},{13,1},{2,6},{6,10},{... | collective-permute-start | bytes 205832 | tf_op jit(solution)/shard_map/ppermute | solution.py:532
  (107 other events, 1170.6 us)

commit v6 on v5

--- a/solution.py
+++ b/solution.py
@@ -508,10 +508,6 @@
     return scatter_end(parts, arrived, *scatter_turn(parts, arrived))
 
 
-def mp_total(values):
-    return values + swap(values, "mp", 1) + swap(values, "mp", 2) + swap(values, "mp", 3)
-
-
 def ring_scatter(block_of, axis, meanwhile=()):
     count = lax.axis_size(axis)
     rank = lax.axis_index(axis)
@@ -685,13 +681,14 @@
     grad1_b = after(pieces_g, out_blocks1[0])
     parts, stats, dcat1, dmix1, fsum1 = run_backward(metas[1], grad1_b, saved1, weights1, True)
     parts, stats, dcat1, dmix1, fsum1 = after((parts, stats, dcat1, dmix1, fsum1), *out_blocks1, *out_sent[:2])
-    arrived, own, other = lax.optimization_barrier(
-        (scatter_start(parts), *weight_gradient(saved1[0], (dcat1,), section, place)))
+    row_sums = [swap(stats, "mp", r) for r in (1, 2, 3)]
+    arrived, row_sums, own, other = lax.optimization_barrier(
+        (scatter_start(parts), row_sums, *weight_gradient(saved1[0], (dcat1,), section, place)))
+    sums = sum(row_sums, stats)
     turn = scatter_turn(parts, arrived)
     steps1 = list(ring_scatter(in_block(own, swap(other, "section", 1)), "dp"))
     arrivals1, red_in1 = [arrival for arrival, _ in steps1], steps1[-1][1]
     d_normed = scatter_end(parts, arrived, *turn)
-    sums = mp_total(after(stats, *turn))
     g0 = norm_backward(cot, d_normed, sums, all1[1:3], weights1[0][0]).astype(BF16)
     small1 = small_gradients(d_normed, all1[1:3], dmix1, fsum1)
     pieces_g0 = gather_pieces(after(g0, arrivals1[0]), arrivals1[1:2])
@@ -705,13 +702,15 @@
     parts, stats, dcat0, dmix0, fsum0 = after((parts, stats, dcat0, dmix0, fsum0), *out_blocks0, out_sent[2])
     out_blocks1 = after(out_blocks1, dcat0)
     kept, sent = direct_sends(parts)
-    sent[:2], own, other = lax.optimization_barrier((sent[:2], *weight_gradient(saved0[0], (dcat0,), section, place)))
+    row_sums = [swap(stats, "mp", r) for r in (1, 2, 3)]
+    sent[:2], row_sums, own, other = lax.optimization_barrier(
+        (sent[:2], row_sums, *weight_gradient(saved0[0], (dcat0,), section, place)))
+    sums = sum(row_sums, stats)
     block0 = in_block(own, swap(other, "section", 1))
     meanwhile = sent[2:]
     ring0 = ring_scatter(block0, "dp", meanwhile)
     steps0 = [next(ring0)]
     meanwhile.clear()
-    sums = mp_total(after(stats, steps0[0][1]))
     sent, dmix0, out_blocks0, out_blocks1 = after((sent, dmix0, out_blocks0, out_blocks1), steps0[0][1])
     d_normed = kept + sent[0].astype(F32) + sent[1].astype(F32) + sent[2].astype(F32)
     d_input = norm_backward(g0, d_normed, sums, all0[1:3], weights0[0][0])

time: 359 us -> 360 us (level)
    unnamed x151 -> x143, local copies, waits for them, and re-layouts: 11.1 us -> 10 us
  transfers between devices with their start and end apart: 64 -> 64, of which waited for: 27 -> 25; matrix products, arithmetic and copies ran while one was open for 14% -> 15% of each run, Pallas kernels for 32% -> 32%
where the time goes in v6:
time: 360 us; the launch traced here: 359 us
  Pallas kernels  130 us (36%)
  waiting for transfers between devices  97 us (27%)
  starting transfers between devices  59.8 us (17%)
  other arithmetic  37.9 us (11%)
  local copies, waits for them, and re-layouts  31 us (9%)
    ppermute x49, waiting for transfers between devices, swap(): lax.ppermute(value, axis, [(k, k ^ by) for k in range(lax.axis_size(axis))])  57.2 us
    pallas_call x2, Pallas kernels, backward_layer(): pl.pallas_call(functools.partial(backward_kernel, carry is not None, phas...  53.6 us
    pallas_call x2, Pallas kernels, forward_layer(): pl.pallas_call(functools.partial(forward_kernel, carry is not None, phase...  44.4 us
    ppermute x49, starting transfers between devices, swap(): lax.ppermute(value, axis, [(k, k ^ by) for k in range(lax.axis_size(axis))])  44 us
    ppermute x6, waiting for transfers between devices, ring_scatter(): arrived = lax.ppermute(total, axis, pairs)  38.3 us
    pallas_call x4, Pallas kernels, weight_gradient(): pl.pallas_call(functools.partial(product_kernel, steps), name='weight_gra...  32 us
    unnamed x143, local copies, waits for them, and re-layouts  10 us
  transfers between devices with their start and end apart: 64, of which 25 were waited for; matrix products, arithmetic and copies ran while one was open for 15% of the time, Pallas kernels for 32%

profile of v6, /device:TPU:0, one launch (start us, length us, event | category | flops | bytes accessed | tf_op | source)
XLA Modules:
  0.0 359.1 jit_solution(8410550349965319252)
XLA Ops:
  1.9 3.1 collective-permute-start.1
  11.4 2.9 multiply_select_fusion
  25.7 4.2 %collective-permute-done.5.refs_6_ = bf16[1024,128]{1,0:T(8,128)(2,1)S(1)} collective-permute-done((bf16[1024,128]{1,0:T(8,128)(2,1)S(1)}, bf16[1024,128]{1,0:T(8,128)(2,1)S(1)}, u32[]{:S(2)}, u32[]{:S(2)}) %collective-permute-start.5) | collective-permute-done | bytes 262176 | tf_op jit(solution)/shard_map/ppermute | solution.py:463
  32.5 22.5 %layer_forward.2 = (bf16[2,1024,128]{2,1,0:T(8,128)(2,1)}, bf16[2,1024,128]{2,1,0:T(8,128)(2,1)}, f32[1024,256]{1,0:T(8,128)}, f32[1024,128]{1,0:T(8,128)}, f32[...) custom-call(s32[2]{0:T(128)} %pad_add_fusion.2.refs_0_, ...), custom_call_target="tpu_custom_call" | custom-call | flops 20480000000 | bytes 25165824 | tf_op jit(solution)/shard_map/layer_forward/pallas_call | solution.py:407
  57.3 10.6 %collective-permute-done.11 = bf16[2,1024,128]{2,1,0:T(8,128)(2,1)S(1)} collective-permute-done((bf16[2,1024,128]{2,1,0:T(8,128)(2,1)}, bf16[2,1024,128]{2,1,0:T(8,128)(2,1)S(1)}, u32[]{:S(2)}, u32[]{:S(2)}) %collective-permute-start.11) | collective-permute-done | bytes 524320 | tf_op jit(solution)/shard_map/ppermute | solution.py:463
  72.8 2.7 collective-permute-done.12
  75.5 2.3 collective-permute-done.14
  80.5 8.3 %collective-permute-done.16.refs_4_ = bf16[1024,256]{1,0:T(8,128)(2,1)} collective-permute-done((bf16[1024,256]{1,0:T(8,128)(2,1)S(1)}, bf16[1024,256]{1,0:T(8,128)(2,1)}, u32[]{:S(2)}, u32[]{:S(2)}) %collective-permute-start.16) | collective-permute-done | bytes 524320 | tf_op jit(solution)/shard_map/ppermute | solution.py:463
  96.4 5.6 %collective-permute-done.17.refs_5_ = bf16[1024,128]{1,0:T(8,128)(2,1)} collective-permute-done((bf16[1024,128]{1,0:T(8,128)(2,1)}, bf16[1024,128]{1,0:T(8,128)(2,1)}, u32[]{:S(2)}, u32[]{:S(2)}) %collective-permute-start.17) | collective-permute-done | bytes 262176 | tf_op jit(solution)/shard_map/ppermute | solution.py:463
  102.1 2.5 collective-permute-start.19
  104.6 21.9 %layer_forward.3 = (f32[1024,256]{1,0:T(8,128)}, bf16[1024,256]{1,0:T(8,128)(2,1)}, bf16[1024,256]{1,0:T(8,128)(2,1)}, bf16[1024,256]{1,0:T(8,128)(2,1)}, bf16[1...) custom-call(s32[2]{0:T(128)} %pad_add_fusion.refs_0_, ...), custom_call_target="tpu_custom_call" | custom-call | flops 20480000000 | bytes 25165824 | tf_op jit(solution)/shard_map/layer_forward/pallas_call | solution.py:407
  128.5 7.8 %weight_gradient.4 = (bf16[640,1024]{1,0:T(8,128)(2,1)}, bf16[640,1024]{1,0:T(8,128)(2,1)S(1)}) custom-call(s32[2]{0:T(128)S(1)} %pad_add_fusion.3.meta, bf16[1024,1280]{1,0:T(8,128)(2,1)S(1)} %copy-done.16, bf16[1024,256]{1,0:T(8,128)(2,1)S(1)} %dynamic-slice_bitcast_fusion.1.refs_0_.refs_1_, bf16[1024,256]{1,0:T(8,128)(2,1)S(1)} %collective-permute-done.9.refs_1_.refs_2_, ...), custom_call_target="tpu_custom_call" | custom-call | flops 2684354560 | bytes 9437184 | tf_op jit(solution)/shard_map/weight_gradient/pallas_call | solution.py:561
  139.7 2.5 add_convert_fusion.21
  142.3 3.7 %collective-permute-start.24 = (bf16[640,256]{1,0:T(8,128)(2,1)S(1)}, bf16[640,256]{1,0:T(8,128)(2,1)S(1)}, u32[]{:S(2)}, u32[]{:S(2)}) collective-permute-start(bf16[640,256]{1,0:T(8,128)(2,1)S(1)} %get-tuple-element.346), channel_id=1, source_target_pairs={{0,12},{4,0},{8,4},{12,8},{1,13},{5,1},{9,5},{13,9},{2,14},{6,2},{... | collective-permute-start | bytes 983048 | tf_op jit(solution)/shard_map/ppermute | solution.py:537
  146.9 27.0 %layer_backward.2 = (bf16[2,1024,128]{2,1,0:T(8,128)(2,1)}, bf16[2,1024,128]{2,1,0:T(8,128)(2,1)}, f32[1024,256]{1,0:T(8,128)}, f32[1024,128]{1,0:T(8,128)}, f32...) custom-call(s32[2]{0:T(128)} %pad_add_fusion.refs_0_, ...), custom_call_target="tpu_custom_call" | custom-call | flops 25600000000 | bytes 25165824 | tf_op jit(solution)/shard_map/layer_backward/pallas_call | solution.py:447
  181.3 8.7 %weight_gradient.5 = (bf16[1024,896]{1,0:T(8,128)(2,1)}, bf16[1024,896]{1,0:T(8,128)(2,1)S(1)}) custom-call(s32[2]{0:T(128)S(1)} %pad_add_fusion.3.meta, bf16[1024,1024]{1,0:T(8,128)(2,1)S(1)} %copy-done.20, bf16[1024,1792]{1,0:T(8,128)(2,1)S(1)} %copy-done.18), custom_call_target="tpu_custom_call" | custom-call | flops 3758096384 | bytes 11534336 | tf_op jit(solution)/shard_map/weight_gradient/pallas_call | solution.py:561
  195.5 2.3 collective-permute-start.35
  199.6 10.3 %collective-permute-done.35 = bf16[256,896]{1,0:T(8,128)(2,1)S(1)} collective-permute-done((bf16[256,896]{1,0:T(8,128)(2,1)S(1)}, bf16[256,896]{1,0:T(8,128)(2,1)S(1)}, u32[]{:S(2)}, u32[]{:S(2)}) %collective-permute-start.35) | collective-permute-done | bytes 458784 | tf_op jit(solution)/shard_map/ppermute | solution.py:517
  216.0 8.6 %collective-permute-done.38 = bf16[256,896]{1,0:T(8,128)(2,1)S(1)} collective-permute-done((bf16[256,896]{1,0:T(8,128)(2,1)S(1)}, bf16[256,896]{1,0:T(8,128)(2,1)S(1)}, u32[]{:S(2)}, u32[]{:S(2)}) %collective-permute-start.38) | collective-permute-done | bytes 458784 | tf_op jit(solution)/shard_map/ppermute | solution.py:517
  229.1 4.3 %collective-permute-done.40.refs_4_.refs_5_ = bf16[1024,128]{1,0:T(8,128)(2,1)S(1)} collective-permute-done((bf16[1024,128]{1,0:T(8,128)(2,1)S(1)}, bf16[1024,128]{1,0:T(8,128)(2,1)S(1)}, u32[]{:S(2)}, u32[]{:S(2)}) %collective-permute-start.40) | collective-permute-done | bytes 262176 | tf_op jit(solution)/shard_map/ppermute | solution.py:463
  235.1 3.4 collective-permute-done.41
  238.5 6.7 %weight_gradient.6 = (bf16[640,1024]{1,0:T(8,128)(2,1)S(1)}, bf16[640,1024]{1,0:T(8,128)(2,1)S(1)}) custom-call(s32[2]{0:T(128)S(1)} %pad_add_fusion.3.meta, bf16[1024,1280]{1,0:T(8,128)(2,1)S(1)} %copy-done.15, bf16[1024,256]{1,0:T(8,128)(2,1)S(1)} %get-tuple-element.243.refs_0_.refs_1_, bf16[1024,256]{1,0:T(8,128)(2,1)S(1)} %collective-permute-done.36.refs_1_.refs_2_, ...), custom_call_target="tpu_custom_call" | custom-call | flops 2684354560 | bytes 9437184 | tf_op jit(solution)/shard_map/weight_gradient/pallas_call | solution.py:561
  251.2 26.6 %layer_backward.3 = (f32[1024,256]{1,0:T(8,128)}, bf16[1024,256]{1,0:T(8,128)(2,1)}, bf16[1024,256]{1,0:T(8,128)(2,1)}, bf16[1024,256]{1,0:T(8,128)(2,1)}, f32[8...) custom-call(s32[2]{0:T(128)} %pad_add_fusion.2.refs_0_, ...), custom_call_target="tpu_custom_call" | custom-call | flops 25600000000 | bytes 25165824 | tf_op jit(solution)/shard_map/layer_backward/pallas_call | solution.py:447
  285.9 8.7 %weight_gradient.7 = (bf16[1024,896]{1,0:T(8,128)(2,1)}, bf16[1024,896]{1,0:T(8,128)(2,1)S(1)}) custom-call(s32[2]{0:T(128)S(1)} %pad_add_fusion.3.meta, bf16[1024,1024]{1,0:T(8,128)(2,1)S(1)} %copy-done.19, bf16[1024,1792]{1,0:T(8,128)(2,1)S(1)} %copy-done.17), custom_call_target="tpu_custom_call" | custom-call | flops 3758096384 | bytes 11534336 | tf_op jit(solution)/shard_map/weight_gradient/pallas_call | solution.py:561
  306.4 8.7 %collective-permute-done.52 = bf16[1024,256]{1,0:T(8,128)(2,1)} collective-permute-done((bf16[1024,256]{1,0:T(8,128)(2,1)}, bf16[1024,256]{1,0:T(8,128)(2,1)}, u32[]{:S(2)}, u32[]{:S(2)}) %collective-permute-start.52) | collective-permute-done | bytes 524320 | tf_op jit(solution)/shard_map/ppermute | solution.py:463
  315.1 2.3 collective-permute-done.54
  317.4 2.2 add_convert_fusion.7
  319.9 2.1 multiply_reduce_fusion.1
  326.1 3.9 %collective-permute-start.59 = (f32[17152]{0:T(1024)S(1)}, f32[17152]{0:T(1024)S(1)}, u32[]{:S(2)}, u32[]{:S(2)}) collective-permute-start(f32[17152]{0:T(1024)S(1)} %select_add_fusion), channel_id=1, source_target_pairs={{0,12},{4,0},{8,4},{12,8},{1,13},{5,1},{9,5},{13,9},{2,14},{6,2},{... | collective-permute-start | bytes 205832 | tf_op jit(solution)/shard_map/ppermute | solution.py:528
  330.8 4.3 %collective-permute-done.60 = bf16[256,896]{1,0:T(8,128)(2,1)} collective-permute-done((bf16[256,896]{1,0:T(8,128)(2,1)}, bf16[256,896]{1,0:T(8,128)(2,1)}, u32[]{:S(2)}, u32[]{:S(2)}) %collective-permute-start.60) | collective-permute-done | bytes 458784 | tf_op jit(solution)/shard_map/ppermute | solution.py:517
  338.5 9.3 %collective-permute-done.61 = bf16[256,896]{1,0:T(8,128)(2,1)S(1)} collective-permute-done((bf16[256,896]{1,0:T(8,128)(2,1)S(1)}, bf16[256,896]{1,0:T(8,128)(2,1)S(1)}, u32[]{:S(2)}, u32[]{:S(2)}) %collective-permute-start.61) | collective-permute-done | bytes 458784 | tf_op jit(solution)/shard_map/ppermute | solution.py:517
  353.1 3.1 maximum_select_fusion
  (342 shorter events, 113.8 us)
Async XLA Ops:
  1.9 15.0 %collective-permute-start.1 = (bf16[1024,256]{1,0:T(8,128)(2,1)S(1)}, bf16[1024,256]{1,0:T(8,128)(2,1)S(1)}, u32[]{:S(2)}, u32[]{:S(2)}) collective-permute-start(bf16[1024,256]{1,0:T(8,128)(2,1)S(1)} %dynamic-slice_bitcast_fusion.refs_2_), channel_id=1, source_target_pairs={{0,2},{1,3},{2,0},{3,1},{4,6},{5,7},{6,4},{7,5},{8,10},{9,11},{10,... | collective-permute-start | bytes 1572872 | tf_op jit(solution)/shard_map/ppermute | solution.py:463
  8.9 23.6 %collective-permute-start.7 = (bf16[1,1024,1024]{2,1,0:T(8,128)(2,1)}, bf16[1,1024,1024]{2,1,0:T(8,128)(2,1)}, u32[]{:S(2)}, u32[]{:S(2)}) collective-permute-start(bf16[1,1024,1024]{2,1,0:T(8,128)(2,1)} %refs_23_.3), channel_id=1, source_target_pairs={{0,16},{16,0},{1,17},{17,1},{2,18},{18,2},{3,19},{19,3},{4,20},{20... | collective-permute-start | bytes 6291464 | tf_op jit(solution)/shard_map/ppermute | solution.py:463
  9.4 23.1 %collective-permute-start.8 = (bf16[1,1024,1024]{2,1,0:T(8,128)(2,1)}, bf16[1,1024,1024]{2,1,0:T(8,128)(2,1)}, u32[]{:S(2)}, u32[]{:S(2)}) collective-permute-start(bf16[1,1024,1024]{2,1,0:T(8,128)(2,1)} %refs_25_.3), channel_id=1, source_target_pairs={{0,16},{16,0},{1,17},{17,1},{2,18},{18,2},{3,19},{19,3},{4,20},{20... | collective-permute-start | bytes 6291464 | tf_op jit(solution)/shard_map/ppermute | solution.py:463
  15.6 16.8 %collective-permute-start.6 = (bf16[1,3,1024,256]{3,2,1,0:T(8,128)(2,1)}, bf16[1,3,1024,256]{3,2,1,0:T(8,128)(2,1)}, u32[]{:S(2)}, u32[]{:S(2)}) collective-permute-start(bf16[1,3,1024,256]{3,2,1,0:T(8,128)(2,1)} %refs_22_.3), channel_id=1, source_target_pairs={{0,16},{16,0},{1,17},{17,1},{2,18},{18,2},{3,19},{19,3},{4,20},{20... | collective-permute-start | bytes 4718600 | tf_op jit(solution)/shard_map/ppermute | solution.py:463
  30.6 24.4 %collective-permute-start.10 = (bf16[1024,256]{1,0:T(8,128)(2,1)S(1)}, bf16[1024,256]{1,0:T(8,128)(2,1)S(1)}, u32[]{:S(2)}, u32[]{:S(2)}) collective-permute-start(bf16[1024,256]{1,0:T(8,128)(2,1)S(1)} %dynamic-slice_bitcast_fusion.1.refs_0_.refs_1_), channel_id=1, source_target_pairs={{0,2},{1,3},{2,0},{3,1},{4,6},{5,7},{6,4},{7,5},{8,10},{9,11},{10,... | collective-permute-start | bytes 1572872 | tf_op jit(solution)/shard_map/ppermute | solution.py:463
  31.6 23.4 %collective-permute-start.9 = (bf16[1024,256]{1,0:T(8,128)(2,1)S(1)}, bf16[1024,256]{1,0:T(8,128)(2,1)S(1)}, u32[]{:S(2)}, u32[]{:S(2)}) collective-permute-start(bf16[1024,256]{1,0:T(8,128)(2,1)S(1)} %dynamic-slice_bitcast_fusion.1.refs_0_.refs_1_), channel_id=1, source_target_pairs={{0,1},{1,0},{2,3},{3,2},{4,5},{5,4},{6,7},{7,6},{8,9},{9,8},{10,11... | collective-permute-start | bytes 1572872 | tf_op jit(solution)/shard_map/ppermute | solution.py:463
  102.0 24.5 %collective-permute-start.20 = (bf16[1024,128]{1,0:T(8,128)(2,1)S(1)}, bf16[1024,128]{1,0:T(8,128)(2,1)S(1)}, u32[]{:S(2)}, u32[]{:S(2)}) collective-permute-start(bf16[1024,128]{1,0:T(8,128)(2,1)S(1)} %slice.192), channel_id=1, source_target_pairs={{0,1},{1,0},{2,3},{3,2},{4,5},{5,4},{6,7},{7,6},{8,9},{9,8},{10,11... | collective-permute-start | bytes 786440 | tf_op jit(solution)/shard_map/ppermute | solution.py:463
  102.1 24.5 %collective-permute-start.19 = (bf16[1024,128]{1,0:T(8,128)(2,1)S(1)}, bf16[1024,128]{1,0:T(8,128)(2,1)S(1)}, u32[]{:S(2)}, u32[]{:S(2)}) collective-permute-start(bf16[1024,128]{1,0:T(8,128)(2,1)S(1)} %slice.191), channel_id=1, source_target_pairs={{0,2},{1,3},{2,0},{3,1},{4,6},{5,7},{6,4},{7,5},{8,10},{9,11},{10,... | collective-permute-start | bytes 786440 | tf_op jit(solution)/shard_map/ppermute | solution.py:463
  136.4 37.5 %collective-permute-start.25 = (bf16[1024,256]{1,0:T(8,128)(2,1)}, bf16[1024,256]{1,0:T(8,128)(2,1)S(1)}, u32[]{:S(2)}, u32[]{:S(2)}) collective-permute-start(bf16[1024,256]{1,0:T(8,128)(2,1)} %get-tuple-element.210), channel_id=1, source_target_pairs={{0,1},{1,0},{2,3},{3,2},{4,5},{5,4},{6,7},{7,6},{8,9},{9,8},{10,11... | collective-permute-start | bytes 1572872 | tf_op jit(solution)/shard_map/ppermute | solution.py:463
  136.6 37.4 %collective-permute-start.26 = (bf16[1024,256]{1,0:T(8,128)(2,1)}, bf16[1024,256]{1,0:T(8,128)(2,1)S(1)}, u32[]{:S(2)}, u32[]{:S(2)}) collective-permute-start(bf16[1024,256]{1,0:T(8,128)(2,1)} %get-tuple-element.211), channel_id=1, source_target_pairs={{0,2},{1,3},{2,0},{3,1},{4,6},{5,7},{6,4},{7,5},{8,10},{9,11},{10,... | collective-permute-start | bytes 1572872 | tf_op jit(solution)/shard_map/ppermute | solution.py:463
  142.3 31.7 %collective-permute-start.24 = (bf16[640,256]{1,0:T(8,128)(2,1)S(1)}, bf16[640,256]{1,0:T(8,128)(2,1)S(1)}, u32[]{:S(2)}, u32[]{:S(2)}) collective-permute-start(bf16[640,256]{1,0:T(8,128)(2,1)S(1)} %get-tuple-element.346), channel_id=1, source_target_pairs={{0,12},{4,0},{8,4},{12,8},{1,13},{5,1},{9,5},{13,9},{2,14},{6,2},{... | collective-permute-start | bytes 983048 | tf_op jit(solution)/shard_map/ppermute | solution.py:537
  145.9 28.1 %collective-permute-start.23 = (bf16[640,256]{1,0:T(8,128)(2,1)S(1)}, bf16[640,256]{1,0:T(8,128)(2,1)S(1)}, u32[]{:S(2)}, u32[]{:S(2)}) collective-permute-start(bf16[640,256]{1,0:T(8,128)(2,1)S(1)} %get-tuple-element.347), channel_id=1, source_target_pairs={{0,8},{4,12},{8,0},{12,4},{1,9},{5,13},{9,1},{13,5},{2,10},{6,14},... | collective-permute-start | bytes 983048 | tf_op jit(solution)/shard_map/ppermute | solution.py:537
  145.9 28.1 %collective-permute-start.22 = (bf16[640,256]{1,0:T(8,128)(2,1)S(1)}, bf16[640,256]{1,0:T(8,128)(2,1)S(1)}, u32[]{:S(2)}, u32[]{:S(2)}) collective-permute-start(bf16[640,256]{1,0:T(8,128)(2,1)S(1)} %get-tuple-element.348), channel_id=1, source_target_pairs={{0,4},{4,8},{8,12},{12,0},{1,5},{5,9},{9,13},{13,1},{2,6},{6,10},{... | collective-permute-start | bytes 983048 | tf_op jit(solution)/shard_map/ppermute | solution.py:537
  174.1 16.0 %collective-permute-start.27 = (bf16[2,1024,128]{2,1,0:T(8,128)(2,1)}, bf16[2,1024,128]{2,1,0:T(8,128)(2,1)}, u32[]{:S(2)}, u32[]{:S(2)}) collective-permute-start(bf16[2,1024,128]{2,1,0:T(8,128)(2,1)} %get-tuple-element.213), channel_id=1, source_target_pairs={{0,1},{1,0},{2,3},{3,2},{4,5},{5,4},{6,7},{7,6},{8,9},{9,8},{10,11... | collective-permute-start | bytes 1572872 | tf_op jit(solution)/shard_map/ppermute | solution.py:463
  174.2 15.9 %collective-permute-start.28 = (bf16[2,1024,128]{2,1,0:T(8,128)(2,1)}, bf16[2,1024,128]{2,1,0:T(8,128)(2,1)}, u32[]{:S(2)}, u32[]{:S(2)}) collective-permute-start(bf16[2,1024,128]{2,1,0:T(8,128)(2,1)} %get-tuple-element.214), channel_id=1, source_target_pairs={{0,2},{1,3},{2,0},{3,1},{4,6},{5,7},{6,4},{7,5},{8,10},{9,11},{10,... | collective-permute-start | bytes 1572872 | tf_op jit(solution)/shard_map/ppermute | solution.py:463
  192.4 19.3 %collective-permute-start.32 = (bf16[1024,128]{1,0:T(8,128)(2,1)S(1)}, bf16[1024,128]{1,0:T(8,128)(2,1)S(1)}, u32[]{:S(2)}, u32[]{:S(2)}) collective-permute-start(bf16[1024,128]{1,0:T(8,128)(2,1)S(1)} %fusion.6), channel_id=1, source_target_pairs={{0,2},{1,3},{2,0},{3,1},{4,6},{5,7},{6,4},{7,5},{8,10},{9,11},{10,... | collective-permute-start | bytes 786440 | tf_op jit(solution)/shard_map/ppermute | solution.py:463
  195.5 14.4 %collective-permute-start.35 = (bf16[256,896]{1,0:T(8,128)(2,1)S(1)}, bf16[256,896]{1,0:T(8,128)(2,1)S(1)}, u32[]{:S(2)}, u32[]{:S(2)}) collective-permute-start(bf16[256,896]{1,0:T(8,128)(2,1)S(1)} %add_convert_fusion.14), channel_id=1, source_target_pairs={{0,4},{4,8},{8,12},{12,0},{1,5},{5,9},{9,13},{13,1},{2,6},{6,10},{... | collective-permute-start | bytes 1376264 | tf_op jit(solution)/shard_map/ppermute | solution.py:517
  245.4 32.5 %collective-permute-start.46 = (bf16[1024,256]{1,0:T(8,128)(2,1)S(1)}, bf16[1024,256]{1,0:T(8,128)(2,1)S(1)}, u32[]{:S(2)}, u32[]{:S(2)}) collective-permute-start(bf16[1024,256]{1,0:T(8,128)(2,1)S(1)} %copy-done.69), channel_id=1, source_target_pairs={{0,3},{1,2},{2,1},{3,0},{4,7},{5,6},{6,5},{7,4},{8,11},{9,10},{10,... | collective-permute-start | bytes 1572872 | tf_op jit(solution)/shard_map/ppermute | solution.py:463
  249.1 28.8 %collective-permute-start.45 = (bf16[640,256]{1,0:T(8,128)(2,1)S(1)}, bf16[640,256]{1,0:T(8,128)(2,1)S(1)}, u32[]{:S(2)}, u32[]{:S(2)}) collective-permute-start(bf16[640,256]{1,0:T(8,128)(2,1)S(1)} %get-tuple-element.342), channel_id=1, source_target_pairs={{0,12},{4,0},{8,4},{12,8},{1,13},{5,1},{9,5},{13,9},{2,14},{6,2},{... | collective-permute-start | bytes 983048 | tf_op jit(solution)/shard_map/ppermute | solution.py:537
  249.2 28.7 %collective-permute-start.44 = (bf16[640,256]{1,0:T(8,128)(2,1)S(1)}, bf16[640,256]{1,0:T(8,128)(2,1)S(1)}, u32[]{:S(2)}, u32[]{:S(2)}) collective-permute-start(bf16[640,256]{1,0:T(8,128)(2,1)S(1)} %get-tuple-element.343), channel_id=1, source_target_pairs={{0,8},{4,12},{8,0},{12,4},{1,9},{5,13},{9,1},{13,5},{2,10},{6,14},... | collective-permute-start | bytes 983048 | tf_op jit(solution)/shard_map/ppermute | solution.py:537
  249.2 28.7 %collective-permute-start.43 = (bf16[640,256]{1,0:T(8,128)(2,1)S(1)}, bf16[640,256]{1,0:T(8,128)(2,1)S(1)}, u32[]{:S(2)}, u32[]{:S(2)}) collective-permute-start(bf16[640,256]{1,0:T(8,128)(2,1)S(1)} %get-tuple-element.344), channel_id=1, source_target_pairs={{0,4},{4,8},{8,12},{12,0},{1,5},{5,9},{9,13},{13,1},{2,6},{6,10},{... | collective-permute-start | bytes 983048 | tf_op jit(solution)/shard_map/ppermute | solution.py:537
  277.9 18.0 %collective-permute-start.47 = (bf16[1024,256]{1,0:T(8,128)(2,1)}, bf16[1024,256]{1,0:T(8,128)(2,1)S(1)}, u32[]{:S(2)}, u32[]{:S(2)}) collective-permute-start(bf16[1024,256]{1,0:T(8,128)(2,1)} %get-tuple-element.269), channel_id=1, source_target_pairs={{0,1},{1,0},{2,3},{3,2},{4,5},{5,4},{6,7},{7,6},{8,9},{9,8},{10,11... | collective-permute-start | bytes 1572872 | tf_op jit(solution)/shard_map/ppermute | solution.py:463
  278.6 17.3 %collective-permute-start.48 = (bf16[1024,256]{1,0:T(8,128)(2,1)}, bf16[1024,256]{1,0:T(8,128)(2,1)}, u32[]{:S(2)}, u32[]{:S(2)}) collective-permute-start(bf16[1024,256]{1,0:T(8,128)(2,1)} %get-tuple-element.270), channel_id=1, source_target_pairs={{0,2},{1,3},{2,0},{3,1},{4,6},{5,7},{6,4},{7,5},{8,10},{9,11},{10,... | collective-permute-start | bytes 1572872 | tf_op jit(solution)/shard_map/ppermute | solution.py:463
  280.4 15.5 %collective-permute-start.51 = (f32[8,1024]{1,0:T(8,128)}, f32[8,1024]{1,0:T(8,128)S(1)}, u32[]{:S(2)}, u32[]{:S(2)}) collective-permute-start(f32[8,1024]{1,0:T(8,128)} %get-tuple-element.271), channel_id=1, source_target_pairs={{0,3},{1,2},{2,1},{3,0},{4,7},{5,6},{6,5},{7,4},{8,11},{9,10},{10,... | collective-permute-start | bytes 98312 | tf_op jit(solution)/shard_map/ppermute | solution.py:463
  281.5 14.4 %collective-permute-start.50 = (f32[8,1024]{1,0:T(8,128)}, f32[8,1024]{1,0:T(8,128)S(1)}, u32[]{:S(2)}, u32[]{:S(2)}) collective-permute-start(f32[8,1024]{1,0:T(8,128)} %get-tuple-element.271), channel_id=1, source_target_pairs={{0,2},{1,3},{2,0},{3,1},{4,6},{5,7},{6,4},{7,5},{8,10},{9,11},{10,... | collective-permute-start | bytes 98312 | tf_op jit(solution)/shard_map/ppermute | solution.py:463
  299.5 15.6 %collective-permute-start.52 = (bf16[1024,256]{1,0:T(8,128)(2,1)}, bf16[1024,256]{1,0:T(8,128)(2,1)}, u32[]{:S(2)}, u32[]{:S(2)}) collective-permute-start(bf16[1024,256]{1,0:T(8,128)(2,1)} %get-tuple-element.277), channel_id=1, source_target_pairs={{0,3},{1,2},{2,1},{3,0},{4,7},{5,6},{6,5},{7,4},{8,11},{9,10},{10,... | collective-permute-start | bytes 1572872 | tf_op jit(solution)/shard_map/ppermute | solution.py:463
  302.7 14.7 %collective-permute-start.54 = (bf16[256,896]{1,0:T(8,128)(2,1)}, bf16[256,896]{1,0:T(8,128)(2,1)}, u32[]{:S(2)}, u32[]{:S(2)}) collective-permute-start(bf16[256,896]{1,0:T(8,128)(2,1)} %add_convert_fusion.9), channel_id=1, source_target_pairs={{0,4},{4,8},{8,12},{12,0},{1,5},{5,9},{9,13},{13,1},{2,6},{6,10},{... | collective-permute-start | bytes 1376264 | tf_op jit(solution)/shard_map/ppermute | solution.py:517
  319.7 15.5 %collective-permute-start.60 = (bf16[256,896]{1,0:T(8,128)(2,1)}, bf16[256,896]{1,0:T(8,128)(2,1)}, u32[]{:S(2)}, u32[]{:S(2)}) collective-permute-start(bf16[256,896]{1,0:T(8,128)(2,1)} %add_convert_fusion.7), channel_id=1, source_target_pairs={{0,4},{4,8},{8,12},{12,0},{1,5},{5,9},{9,13},{13,1},{2,6},{6,10},{... | collective-permute-start | bytes 1376264 | tf_op jit(solution)/shard_map/ppermute | solution.py:517
  326.1 21.7 %collective-permute-start.55 = (f32[1024,256]{1,0:T(8,128)S(1)}, f32[1024,256]{1,0:T(8,128)}, u32[]{:S(2)}, u32[]{:S(2)}) collective-permute-start(f32[1024,256]{1,0:T(8,128)S(1)} %get-tuple-element.341), channel_id=1, source_target_pairs={{0,16},{16,0},{1,17},{17,1},{2,18},{18,2},{3,19},{19,3},{4,20},{20... | collective-permute-start | bytes 3145736 | tf_op jit(solution)/shard_map/ppermute | solution.py:463
  326.1 21.6 %collective-permute-start.59 = (f32[17152]{0:T(1024)S(1)}, f32[17152]{0:T(1024)S(1)}, u32[]{:S(2)}, u32[]{:S(2)}) collective-permute-start(f32[17152]{0:T(1024)S(1)} %select_add_fusion), channel_id=1, source_target_pairs={{0,12},{4,0},{8,4},{12,8},{1,13},{5,1},{9,5},{13,9},{2,14},{6,2},{... | collective-permute-start | bytes 205832 | tf_op jit(solution)/shard_map/ppermute | solution.py:528
  330.0 19.2 %collective-permute-start.58 = (f32[17152]{0:T(1024)S(1)}, f32[17152]{0:T(1024)S(1)}, u32[]{:S(2)}, u32[]{:S(2)}) collective-permute-start(f32[17152]{0:T(1024)S(1)} %select_add_fusion), channel_id=1, source_target_pairs={{0,8},{4,12},{8,0},{12,4},{1,9},{5,13},{9,1},{13,5},{2,10},{6,14},... | collective-permute-start | bytes 205832 | tf_op jit(solution)/shard_map/ppermute | solution.py:528
  330.0 19.2 %collective-permute-start.57 = (f32[17152]{0:T(1024)S(1)}, f32[17152]{0:T(1024)S(1)}, u32[]{:S(2)}, u32[]{:S(2)}) collective-permute-start(f32[17152]{0:T(1024)S(1)} %select_add_fusion), channel_id=1, source_target_pairs={{0,4},{4,8},{8,12},{12,0},{1,5},{5,9},{9,13},{13,1},{2,6},{6,10},{... | collective-permute-start | bytes 205832 | tf_op jit(solution)/shard_map/ppermute | solution.py:528
  (103 other events, 1203.8 us)

commit v7 on v5

--- a/solution.py
+++ b/solution.py
@@ -572,7 +572,7 @@
             out_specs=[pl.BlockSpec((block, n), lambda i, meta: (jnp.minimum(i, steps - 1), 0)),
                        pl.BlockSpec((block, n), lambda i, meta: (jnp.maximum(i - steps, 0), 0))],
             scratch_shapes=[] if whole else [pltpu.VMEM((rows, n), BF16)]),
-        compiler_params=params(20),
+        compiler_params=params(58 if whole else 20),
         cost_estimate=pl.CostEstimate(flops=4 * rows * m * n, transcendentals=0, bytes_accessed=4 * (rows * (m + n) + m * n)),
     )(jnp.stack([section, place]).astype(jnp.int32), left, *rights)
     return own, other

time: 359 us -> 359 us (level)
  Pallas kernels: 130 us -> 136 us
  waiting for transfers between devices: 96.9 us -> 91.8 us
    pallas_call x4, Pallas kernels: 32 us -> 37.8 us  [weight_gradient(): pl.pallas_call(functools.partial(product_kernel, steps), name='weight_gra...]
    ppermute x49, waiting for transfers between devices: 55.4 us -> 51.2 us  [swap(): lax.ppermute(value, axis, [(k, k ^ by) for k in range(lax.axis_size(axis))])]
    unnamed x151 -> x149, local copies, waits for them, and re-layouts: 11.1 us -> 7.6 us
  transfers between devices with their start and end apart: 64 -> 64, of which waited for: 27 -> 29; matrix products, arithmetic and copies ran while one was open for 14% -> 14% of each run, Pallas kernels for 32% -> 34%
where the time goes in v7:
time: 359 us; the launch traced here: 357 us
  Pallas kernels  136 us (38%)
  waiting for transfers between devices  91.8 us (26%)
  starting transfers between devices  61 us (17%)
  other arithmetic  36.3 us (10%)
  local copies, waits for them, and re-layouts  29.4 us (8%)
    pallas_call x2, Pallas kernels, backward_layer(): pl.pallas_call(functools.partial(backward_kernel, carry is not None, phas...  53.3 us
    ppermute x49, waiting for transfers between devices, swap(): lax.ppermute(value, axis, [(k, k ^ by) for k in range(lax.axis_size(axis))])  51.2 us
    ppermute x49, starting transfers between devices, swap(): lax.ppermute(value, axis, [(k, k ^ by) for k in range(lax.axis_size(axis))])  45 us
    pallas_call x2, Pallas kernels, forward_layer(): pl.pallas_call(functools.partial(forward_kernel, carry is not None, phase...  44.4 us
    ppermute x6, waiting for transfers between devices, ring_scatter(): arrived = lax.ppermute(total, axis, pairs)  38.6 us
    pallas_call x4, Pallas kernels, weight_gradient(): pl.pallas_call(functools.partial(product_kernel, steps), name='weight_gra...  37.8 us
    unnamed x149, local copies, waits for them, and re-layouts  7.6 us
  transfers between devices with their start and end apart: 64, of which 29 were waited for; matrix products, arithmetic and copies ran while one was open for 14% of the time, Pallas kernels for 34%

profile of v7, /device:TPU:0, one launch (start us, length us, event | category | flops | bytes accessed | tf_op | source)
XLA Modules:
  0.0 357.5 jit_solution(2542435797148519757)
XLA Ops:
  1.9 3.1 collective-permute-start.1
  11.4 2.8 multiply_select_fusion
  25.7 4.2 %collective-permute-done.5.refs_6_ = bf16[1024,128]{1,0:T(8,128)(2,1)S(1)} collective-permute-done((bf16[1024,128]{1,0:T(8,128)(2,1)S(1)}, bf16[1024,128]{1,0:T(8,128)(2,1)S(1)}, u32[]{:S(2)}, u32[]{:S(2)}) %collective-permute-start.5) | collective-permute-done | bytes 262176 | tf_op jit(solution)/shard_map/ppermute | solution.py:463
  32.1 22.5 %layer_forward.2 = (bf16[2,1024,128]{2,1,0:T(8,128)(2,1)}, bf16[2,1024,128]{2,1,0:T(8,128)(2,1)}, f32[1024,256]{1,0:T(8,128)}, f32[1024,128]{1,0:T(8,128)}, f32[...) custom-call(s32[2]{0:T(128)} %pad_add_fusion.2.refs_0_, ...), custom_call_target="tpu_custom_call" | custom-call | flops 20480000000 | bytes 25165824 | tf_op jit(solution)/shard_map/layer_forward/pallas_call | solution.py:407
  56.9 10.4 %collective-permute-done.11 = bf16[2,1024,128]{2,1,0:T(8,128)(2,1)S(1)} collective-permute-done((bf16[2,1024,128]{2,1,0:T(8,128)(2,1)}, bf16[2,1024,128]{2,1,0:T(8,128)(2,1)S(1)}, u32[]{:S(2)}, u32[]{:S(2)}) %collective-permute-start.11) | collective-permute-done | bytes 524320 | tf_op jit(solution)/shard_map/ppermute | solution.py:463
  72.0 2.8 collective-permute-done.12
  74.8 3.2 collective-permute-done.14
  80.4 8.2 %collective-permute-done.16.refs_4_ = bf16[1024,256]{1,0:T(8,128)(2,1)} collective-permute-done((bf16[1024,256]{1,0:T(8,128)(2,1)S(1)}, bf16[1024,256]{1,0:T(8,128)(2,1)}, u32[]{:S(2)}, u32[]{:S(2)}) %collective-permute-start.16) | collective-permute-done | bytes 524320 | tf_op jit(solution)/shard_map/ppermute | solution.py:463
  97.0 3.1 collective-permute-done.17.refs_5_
  103.3 21.9 %layer_forward.3 = (f32[1024,256]{1,0:T(8,128)}, bf16[1024,256]{1,0:T(8,128)(2,1)}, bf16[1024,256]{1,0:T(8,128)(2,1)}, bf16[1024,256]{1,0:T(8,128)(2,1)}, bf16[1...) custom-call(s32[2]{0:T(128)} %pad_add_fusion.refs_0_, ...), custom_call_target="tpu_custom_call" | custom-call | flops 20480000000 | bytes 25165824 | tf_op jit(solution)/shard_map/layer_forward/pallas_call | solution.py:407
  127.2 7.8 %weight_gradient.4 = (bf16[640,1024]{1,0:T(8,128)(2,1)}, bf16[640,1024]{1,0:T(8,128)(2,1)S(1)}) custom-call(s32[2]{0:T(128)S(1)} %pad_add_fusion.3.meta, bf16[1024,1280]{1,0:T(8,128)(2,1)S(1)} %copy-done.17, bf16[1024,256]{1,0:T(8,128)(2,1)S(1)} %dynamic-slice_bitcast_fusion.1.refs_0_.refs_1_, bf16[1024,256]{1,0:T(8,128)(2,1)S(1)} %collective-permute-done.9.refs_1_.refs_2_, ...), custom_call_target="tpu_custom_call" | custom-call | flops 2684354560 | bytes 9437184 | tf_op jit(solution)/shard_map/weight_gradient/pallas_call | solution.py:565
  136.2 2.2 collective-permute-done.21
  140.2 3.5 collective-permute-start.24
  144.8 26.8 %layer_backward.2 = (bf16[2,1024,128]{2,1,0:T(8,128)(2,1)}, bf16[2,1024,128]{2,1,0:T(8,128)(2,1)}, f32[1024,256]{1,0:T(8,128)}, f32[1024,128]{1,0:T(8,128)}, f32...) custom-call(s32[2]{0:T(128)} %pad_add_fusion.refs_0_, ...), custom_call_target="tpu_custom_call" | custom-call | flops 25600000000 | bytes 25165824 | tf_op jit(solution)/shard_map/layer_backward/pallas_call | solution.py:447
  173.6 11.6 %weight_gradient.5 = (bf16[1024,896]{1,0:T(8,128)(2,1)}, bf16[1024,896]{1,0:T(8,128)(2,1)}) custom-call(s32[2]{0:T(128)} %copy-done.14, bf16[1024,1024]{1,0:T(8,128)(2,1)} %get-tuple-element.186.refs_6_.left, bf16[1024,1792]{1,0:T(8,128)(2,1)} %get-tuple-element.211.refs_0_), custom_call_target="tpu_custom_call" | custom-call | flops 3758096384 | bytes 11534336 | tf_op jit(solution)/shard_map/weight_gradient/pallas_call | solution.py:565
  195.3 2.5 collective-permute-start.35
  200.5 8.7 %collective-permute-done.35 = bf16[256,896]{1,0:T(8,128)(2,1)S(1)} collective-permute-done((bf16[256,896]{1,0:T(8,128)(2,1)S(1)}, bf16[256,896]{1,0:T(8,128)(2,1)S(1)}, u32[]{:S(2)}, u32[]{:S(2)}) %collective-permute-start.35) | collective-permute-done | bytes 458784 | tf_op jit(solution)/shard_map/ppermute | solution.py:521
  214.9 8.7 %collective-permute-done.38 = bf16[256,896]{1,0:T(8,128)(2,1)S(1)} collective-permute-done((bf16[256,896]{1,0:T(8,128)(2,1)S(1)}, bf16[256,896]{1,0:T(8,128)(2,1)S(1)}, u32[]{:S(2)}, u32[]{:S(2)}) %collective-permute-start.38) | collective-permute-done | bytes 458784 | tf_op jit(solution)/shard_map/ppermute | solution.py:521
  228.0 4.7 %collective-permute-done.40.refs_4_.refs_5_ = bf16[1024,128]{1,0:T(8,128)(2,1)S(1)} collective-permute-done((bf16[1024,128]{1,0:T(8,128)(2,1)S(1)}, bf16[1024,128]{1,0:T(8,128)(2,1)S(1)}, u32[]{:S(2)}, u32[]{:S(2)}) %collective-permute-start.40) | collective-permute-done | bytes 262176 | tf_op jit(solution)/shard_map/ppermute | solution.py:463
  233.7 3.3 collective-permute-done.41
  237.8 6.7 %weight_gradient.6 = (bf16[640,1024]{1,0:T(8,128)(2,1)S(1)}, bf16[640,1024]{1,0:T(8,128)(2,1)S(1)}) custom-call(s32[2]{0:T(128)S(1)} %copy-done.15, bf16[1024,1280]{1,0:T(8,128)(2,1)S(1)} %copy-done.16, bf16[1024,256]{1,0:T(8,128)(2,1)S(1)} %get-tuple-element.237.refs_0_.refs_1_, bf16[1024,256]{1,0:T(8,128)(2,1)S(1)} %collective-permute-done.36.refs_1_.refs_2_, ...), custom_call_target="tpu_custom_call" | custom-call | flops 2684354560 | bytes 9437184 | tf_op jit(solution)/shard_map/weight_gradient/pallas_call | solution.py:565
  250.4 26.5 %layer_backward.3 = (f32[1024,256]{1,0:T(8,128)}, bf16[1024,256]{1,0:T(8,128)(2,1)}, bf16[1024,256]{1,0:T(8,128)(2,1)}, bf16[1024,256]{1,0:T(8,128)(2,1)}, f32[8...) custom-call(s32[2]{0:T(128)} %pad_add_fusion.2.refs_0_, ...), custom_call_target="tpu_custom_call" | custom-call | flops 25600000000 | bytes 25165824 | tf_op jit(solution)/shard_map/layer_backward/pallas_call | solution.py:447
  280.1 11.7 %weight_gradient.7 = (bf16[1024,896]{1,0:T(8,128)(2,1)}, bf16[1024,896]{1,0:T(8,128)(2,1)}) custom-call(s32[2]{0:T(128)} %copy-done.14, bf16[1024,1024]{1,0:T(8,128)(2,1)} %get-tuple-element.242.refs_6_.left, bf16[1024,1792]{1,0:T(8,128)(2,1)} %get-tuple-element.265.refs_0_), custom_call_target="tpu_custom_call" | custom-call | flops 3758096384 | bytes 11534336 | tf_op jit(solution)/shard_map/weight_gradient/pallas_call | solution.py:565
  296.9 2.2 add_convert_fusion.9
  307.2 2.6 collective-permute-done.49
  309.8 4.0 %collective-permute-done.51 = bf16[256,896]{1,0:T(8,128)(2,1)} collective-permute-done((bf16[256,896]{1,0:T(8,128)(2,1)}, bf16[256,896]{1,0:T(8,128)(2,1)}, u32[]{:S(2)}, u32[]{:S(2)}) %collective-permute-start.51) | collective-permute-done | bytes 458784 | tf_op jit(solution)/shard_map/ppermute | solution.py:521
  313.8 2.1 add_convert_fusion.7
  319.7 2.1 multiply_reduce_fusion.1
  324.8 3.9 %collective-permute-start.59 = (f32[17152]{0:T(1024)S(1)}, f32[17152]{0:T(1024)S(1)}, u32[]{:S(2)}, u32[]{:S(2)}) collective-permute-start(f32[17152]{0:T(1024)S(1)} %select_add_fusion), channel_id=1, source_target_pairs={{0,12},{4,0},{8,4},{12,8},{1,13},{5,1},{9,5},{13,9},{2,14},{6,2},{... | collective-permute-start | bytes 205832 | tf_op jit(solution)/shard_map/ppermute | solution.py:532
  329.5 4.8 %collective-permute-done.60 = bf16[256,896]{1,0:T(8,128)(2,1)} collective-permute-done((bf16[256,896]{1,0:T(8,128)(2,1)}, bf16[256,896]{1,0:T(8,128)(2,1)}, u32[]{:S(2)}, u32[]{:S(2)}) %collective-permute-start.60) | collective-permute-done | bytes 458784 | tf_op jit(solution)/shard_map/ppermute | solution.py:521
  337.6 9.0 %collective-permute-done.61 = bf16[256,896]{1,0:T(8,128)(2,1)S(1)} collective-permute-done((bf16[256,896]{1,0:T(8,128)(2,1)S(1)}, bf16[256,896]{1,0:T(8,128)(2,1)S(1)}, u32[]{:S(2)}, u32[]{:S(2)}) %collective-permute-start.61) | collective-permute-done | bytes 458784 | tf_op jit(solution)/shard_map/ppermute | solution.py:521
  348.9 2.1 broadcast_select_fusion.2
  (348 shorter events, 115.5 us)
Async XLA Ops:
  1.9 15.0 %collective-permute-start.1 = (bf16[1024,256]{1,0:T(8,128)(2,1)S(1)}, bf16[1024,256]{1,0:T(8,128)(2,1)S(1)}, u32[]{:S(2)}, u32[]{:S(2)}) collective-permute-start(bf16[1024,256]{1,0:T(8,128)(2,1)S(1)} %dynamic-slice_bitcast_fusion.refs_2_), channel_id=1, source_target_pairs={{0,2},{1,3},{2,0},{3,1},{4,6},{5,7},{6,4},{7,5},{8,10},{9,11},{10,... | collective-permute-start | bytes 1572872 | tf_op jit(solution)/shard_map/ppermute | solution.py:463
  4.9 13.5 %collective-permute-start = (bf16[1024,256]{1,0:T(8,128)(2,1)S(1)}, bf16[1024,256]{1,0:T(8,128)(2,1)}, u32[]{:S(2)}, u32[]{:S(2)}) collective-permute-start(bf16[1024,256]{1,0:T(8,128)(2,1)S(1)} %dynamic-slice_bitcast_fusion.refs_2_), channel_id=1, source_target_pairs={{0,1},{1,0},{2,3},{3,2},{4,5},{5,4},{6,7},{7,6},{8,9},{9,8},{10,11... | collective-permute-start | bytes 1572872 | tf_op jit(solution)/shard_map/ppermute | solution.py:463
  8.9 23.2 %collective-permute-start.7 = (bf16[1,1024,1024]{2,1,0:T(8,128)(2,1)}, bf16[1,1024,1024]{2,1,0:T(8,128)(2,1)}, u32[]{:S(2)}, u32[]{:S(2)}) collective-permute-start(bf16[1,1024,1024]{2,1,0:T(8,128)(2,1)} %refs_23_.3), channel_id=1, source_target_pairs={{0,16},{16,0},{1,17},{17,1},{2,18},{18,2},{3,19},{19,3},{4,20},{20... | collective-permute-start | bytes 6291464 | tf_op jit(solution)/shard_map/ppermute | solution.py:463
  9.4 22.7 %collective-permute-start.8 = (bf16[1,1024,1024]{2,1,0:T(8,128)(2,1)}, bf16[1,1024,1024]{2,1,0:T(8,128)(2,1)}, u32[]{:S(2)}, u32[]{:S(2)}) collective-permute-start(bf16[1,1024,1024]{2,1,0:T(8,128)(2,1)} %refs_25_.3), channel_id=1, source_target_pairs={{0,16},{16,0},{1,17},{17,1},{2,18},{18,2},{3,19},{19,3},{4,20},{20... | collective-permute-start | bytes 6291464 | tf_op jit(solution)/shard_map/ppermute | solution.py:463
  15.6 16.5 %collective-permute-start.6 = (bf16[1,3,1024,256]{3,2,1,0:T(8,128)(2,1)}, bf16[1,3,1024,256]{3,2,1,0:T(8,128)(2,1)}, u32[]{:S(2)}, u32[]{:S(2)}) collective-permute-start(bf16[1,3,1024,256]{3,2,1,0:T(8,128)(2,1)} %refs_22_.3), channel_id=1, source_target_pairs={{0,16},{16,0},{1,17},{17,1},{2,18},{18,2},{3,19},{19,3},{4,20},{20... | collective-permute-start | bytes 4718600 | tf_op jit(solution)/shard_map/ppermute | solution.py:463
  30.1 24.5 %collective-permute-start.10 = (bf16[1024,256]{1,0:T(8,128)(2,1)S(1)}, bf16[1024,256]{1,0:T(8,128)(2,1)S(1)}, u32[]{:S(2)}, u32[]{:S(2)}) collective-permute-start(bf16[1024,256]{1,0:T(8,128)(2,1)S(1)} %dynamic-slice_bitcast_fusion.1.refs_0_.refs_1_), channel_id=1, source_target_pairs={{0,2},{1,3},{2,0},{3,1},{4,6},{5,7},{6,4},{7,5},{8,10},{9,11},{10,... | collective-permute-start | bytes 1572872 | tf_op jit(solution)/shard_map/ppermute | solution.py:463
  31.5 23.2 %collective-permute-start.9 = (bf16[1024,256]{1,0:T(8,128)(2,1)S(1)}, bf16[1024,256]{1,0:T(8,128)(2,1)S(1)}, u32[]{:S(2)}, u32[]{:S(2)}) collective-permute-start(bf16[1024,256]{1,0:T(8,128)(2,1)S(1)} %dynamic-slice_bitcast_fusion.1.refs_0_.refs_1_), channel_id=1, source_target_pairs={{0,1},{1,0},{2,3},{3,2},{4,5},{5,4},{6,7},{7,6},{8,9},{9,8},{10,11... | collective-permute-start | bytes 1572872 | tf_op jit(solution)/shard_map/ppermute | solution.py:463
  56.2 13.9 %collective-permute-start.13 = (bf16[2,1024,128]{2,1,0:T(8,128)(2,1)}, bf16[2,1024,128]{2,1,0:T(8,128)(2,1)S(1)}, u32[]{:S(2)}, u32[]{:S(2)}) collective-permute-start(bf16[2,1024,128]{2,1,0:T(8,128)(2,1)} %get-tuple-element.169), channel_id=1, source_target_pairs={{0,2},{1,3},{2,0},{3,1},{4,6},{5,7},{6,4},{7,5},{8,10},{9,11},{10,... | collective-permute-start | bytes 1572872 | tf_op jit(solution)/shard_map/ppermute | solution.py:463
  100.2 25.1 %collective-permute-start.20 = (bf16[1024,128]{1,0:T(8,128)(2,1)S(1)}, bf16[1024,128]{1,0:T(8,128)(2,1)S(1)}, u32[]{:S(2)}, u32[]{:S(2)}) collective-permute-start(bf16[1024,128]{1,0:T(8,128)(2,1)S(1)} %slice.192), channel_id=1, source_target_pairs={{0,1},{1,0},{2,3},{3,2},{4,5},{5,4},{6,7},{7,6},{8,9},{9,8},{10,11... | collective-permute-start | bytes 786440 | tf_op jit(solution)/shard_map/ppermute | solution.py:463
  101.5 23.7 %collective-permute-start.19 = (bf16[1024,128]{1,0:T(8,128)(2,1)S(1)}, bf16[1024,128]{1,0:T(8,128)(2,1)S(1)}, u32[]{:S(2)}, u32[]{:S(2)}) collective-permute-start(bf16[1024,128]{1,0:T(8,128)(2,1)S(1)} %slice.191), channel_id=1, source_target_pairs={{0,2},{1,3},{2,0},{3,1},{4,6},{5,7},{6,4},{7,5},{8,10},{9,11},{10,... | collective-permute-start | bytes 786440 | tf_op jit(solution)/shard_map/ppermute | solution.py:463
  135.1 36.6 %collective-permute-start.25 = (bf16[1024,256]{1,0:T(8,128)(2,1)}, bf16[1024,256]{1,0:T(8,128)(2,1)S(1)}, u32[]{:S(2)}, u32[]{:S(2)}) collective-permute-start(bf16[1024,256]{1,0:T(8,128)(2,1)} %get-tuple-element.206), channel_id=1, source_target_pairs={{0,1},{1,0},{2,3},{3,2},{4,5},{5,4},{6,7},{7,6},{8,9},{9,8},{10,11... | collective-permute-start | bytes 1572872 | tf_op jit(solution)/shard_map/ppermute | solution.py:463
  136.1 35.6 %collective-permute-start.26 = (bf16[1024,256]{1,0:T(8,128)(2,1)}, bf16[1024,256]{1,0:T(8,128)(2,1)S(1)}, u32[]{:S(2)}, u32[]{:S(2)}) collective-permute-start(bf16[1024,256]{1,0:T(8,128)(2,1)} %get-tuple-element.207), channel_id=1, source_target_pairs={{0,2},{1,3},{2,0},{3,1},{4,6},{5,7},{6,4},{7,5},{8,10},{9,11},{10,... | collective-permute-start | bytes 1572872 | tf_op jit(solution)/shard_map/ppermute | solution.py:463
  140.2 31.5 %collective-permute-start.24 = (bf16[640,256]{1,0:T(8,128)(2,1)S(1)}, bf16[640,256]{1,0:T(8,128)(2,1)S(1)}, u32[]{:S(2)}, u32[]{:S(2)}) collective-permute-start(bf16[640,256]{1,0:T(8,128)(2,1)S(1)} %get-tuple-element.338), channel_id=1, source_target_pairs={{0,12},{4,0},{8,4},{12,8},{1,13},{5,1},{9,5},{13,9},{2,14},{6,2},{... | collective-permute-start | bytes 983048 | tf_op jit(solution)/shard_map/ppermute | solution.py:541
  143.8 28.4 %collective-permute-start.23 = (bf16[640,256]{1,0:T(8,128)(2,1)S(1)}, bf16[640,256]{1,0:T(8,128)(2,1)S(1)}, u32[]{:S(2)}, u32[]{:S(2)}) collective-permute-start(bf16[640,256]{1,0:T(8,128)(2,1)S(1)} %get-tuple-element.339), channel_id=1, source_target_pairs={{0,8},{4,12},{8,0},{12,4},{1,9},{5,13},{9,1},{13,5},{2,10},{6,14},... | collective-permute-start | bytes 983048 | tf_op jit(solution)/shard_map/ppermute | solution.py:541
  143.8 28.4 %collective-permute-start.22 = (bf16[640,256]{1,0:T(8,128)(2,1)S(1)}, bf16[640,256]{1,0:T(8,128)(2,1)S(1)}, u32[]{:S(2)}, u32[]{:S(2)}) collective-permute-start(bf16[640,256]{1,0:T(8,128)(2,1)S(1)} %get-tuple-element.340), channel_id=1, source_target_pairs={{0,4},{4,8},{8,12},{12,0},{1,5},{5,9},{9,13},{13,1},{2,6},{6,10},{... | collective-permute-start | bytes 983048 | tf_op jit(solution)/shard_map/ppermute | solution.py:541
  172.5 13.3 %collective-permute-start.27 = (bf16[2,1024,128]{2,1,0:T(8,128)(2,1)}, bf16[2,1024,128]{2,1,0:T(8,128)(2,1)S(1)}, u32[]{:S(2)}, u32[]{:S(2)}) collective-permute-start(bf16[2,1024,128]{2,1,0:T(8,128)(2,1)} %get-tuple-element.209), channel_id=1, source_target_pairs={{0,1},{1,0},{2,3},{3,2},{4,5},{5,4},{6,7},{7,6},{8,9},{9,8},{10,11... | collective-permute-start | bytes 1572872 | tf_op jit(solution)/shard_map/ppermute | solution.py:463
  173.6 13.1 %collective-permute-start.28 = (bf16[2,1024,128]{2,1,0:T(8,128)(2,1)}, bf16[2,1024,128]{2,1,0:T(8,128)(2,1)S(1)}, u32[]{:S(2)}, u32[]{:S(2)}) collective-permute-start(bf16[2,1024,128]{2,1,0:T(8,128)(2,1)} %get-tuple-element.210), channel_id=1, source_target_pairs={{0,2},{1,3},{2,0},{3,1},{4,6},{5,7},{6,4},{7,5},{8,10},{9,11},{10,... | collective-permute-start | bytes 1572872 | tf_op jit(solution)/shard_map/ppermute | solution.py:463
  195.3 13.9 %collective-permute-start.35 = (bf16[256,896]{1,0:T(8,128)(2,1)S(1)}, bf16[256,896]{1,0:T(8,128)(2,1)S(1)}, u32[]{:S(2)}, u32[]{:S(2)}) collective-permute-start(bf16[256,896]{1,0:T(8,128)(2,1)S(1)} %add_convert_fusion.14), channel_id=1, source_target_pairs={{0,4},{4,8},{8,12},{12,0},{1,5},{5,9},{9,13},{13,1},{2,6},{6,10},{... | collective-permute-start | bytes 1376264 | tf_op jit(solution)/shard_map/ppermute | solution.py:521
  198.0 13.1 %collective-permute-start.29 = (bf16[1024,128]{1,0:T(8,128)(2,1)S(1)}, bf16[1024,128]{1,0:T(8,128)(2,1)S(1)}, u32[]{:S(2)}, u32[]{:S(2)}) collective-permute-start(bf16[1024,128]{1,0:T(8,128)(2,1)S(1)} %fusion.6), channel_id=1, source_target_pairs={{0,2},{1,3},{2,0},{3,1},{4,6},{5,7},{6,4},{7,5},{8,10},{9,11},{10,... | collective-permute-start | bytes 786440 | tf_op jit(solution)/shard_map/ppermute | solution.py:463
  244.6 32.3 %collective-permute-start.46 = (bf16[1024,256]{1,0:T(8,128)(2,1)S(1)}, bf16[1024,256]{1,0:T(8,128)(2,1)S(1)}, u32[]{:S(2)}, u32[]{:S(2)}) collective-permute-start(bf16[1024,256]{1,0:T(8,128)(2,1)S(1)} %copy-done.71), channel_id=1, source_target_pairs={{0,3},{1,2},{2,1},{3,0},{4,7},{5,6},{6,5},{7,4},{8,11},{9,10},{10,... | collective-permute-start | bytes 1572872 | tf_op jit(solution)/shard_map/ppermute | solution.py:463
  248.3 28.6 %collective-permute-start.45 = (bf16[640,256]{1,0:T(8,128)(2,1)S(1)}, bf16[640,256]{1,0:T(8,128)(2,1)S(1)}, u32[]{:S(2)}, u32[]{:S(2)}) collective-permute-start(bf16[640,256]{1,0:T(8,128)(2,1)S(1)} %get-tuple-element.334), channel_id=1, source_target_pairs={{0,12},{4,0},{8,4},{12,8},{1,13},{5,1},{9,5},{13,9},{2,14},{6,2},{... | collective-permute-start | bytes 983048 | tf_op jit(solution)/shard_map/ppermute | solution.py:541
  248.3 28.8 %collective-permute-start.44 = (bf16[640,256]{1,0:T(8,128)(2,1)S(1)}, bf16[640,256]{1,0:T(8,128)(2,1)S(1)}, u32[]{:S(2)}, u32[]{:S(2)}) collective-permute-start(bf16[640,256]{1,0:T(8,128)(2,1)S(1)} %get-tuple-element.335), channel_id=1, source_target_pairs={{0,8},{4,12},{8,0},{12,4},{1,9},{5,13},{9,1},{13,5},{2,10},{6,14},... | collective-permute-start | bytes 983048 | tf_op jit(solution)/shard_map/ppermute | solution.py:541
  248.4 28.7 %collective-permute-start.43 = (bf16[640,256]{1,0:T(8,128)(2,1)S(1)}, bf16[640,256]{1,0:T(8,128)(2,1)S(1)}, u32[]{:S(2)}, u32[]{:S(2)}) collective-permute-start(bf16[640,256]{1,0:T(8,128)(2,1)S(1)} %get-tuple-element.336), channel_id=1, source_target_pairs={{0,4},{4,8},{8,12},{12,0},{1,5},{5,9},{9,13},{13,1},{2,6},{6,10},{... | collective-permute-start | bytes 983048 | tf_op jit(solution)/shard_map/ppermute | solution.py:541
  277.7 14.2 %collective-permute-start.47 = (bf16[1024,256]{1,0:T(8,128)(2,1)}, bf16[1024,256]{1,0:T(8,128)(2,1)S(1)}, u32[]{:S(2)}, u32[]{:S(2)}) collective-permute-start(bf16[1024,256]{1,0:T(8,128)(2,1)} %get-tuple-element.263), channel_id=1, source_target_pairs={{0,1},{1,0},{2,3},{3,2},{4,5},{5,4},{6,7},{7,6},{8,9},{9,8},{10,11... | collective-permute-start | bytes 1572872 | tf_op jit(solution)/shard_map/ppermute | solution.py:463
  278.7 13.3 %collective-permute-start.48 = (bf16[1024,256]{1,0:T(8,128)(2,1)}, bf16[1024,256]{1,0:T(8,128)(2,1)S(1)}, u32[]{:S(2)}, u32[]{:S(2)}) collective-permute-start(bf16[1024,256]{1,0:T(8,128)(2,1)} %get-tuple-element.264), channel_id=1, source_target_pairs={{0,2},{1,3},{2,0},{3,1},{4,6},{5,7},{6,4},{7,5},{8,10},{9,11},{10,... | collective-permute-start | bytes 1572872 | tf_op jit(solution)/shard_map/ppermute | solution.py:463
  294.2 15.6 %collective-permute-start.49 = (bf16[1024,256]{1,0:T(8,128)(2,1)}, bf16[1024,256]{1,0:T(8,128)(2,1)}, u32[]{:S(2)}, u32[]{:S(2)}) collective-permute-start(bf16[1024,256]{1,0:T(8,128)(2,1)} %get-tuple-element.270), channel_id=1, source_target_pairs={{0,3},{1,2},{2,1},{3,0},{4,7},{5,6},{6,5},{7,4},{8,11},{9,10},{10,... | collective-permute-start | bytes 1572872 | tf_op jit(solution)/shard_map/ppermute | solution.py:463
  299.1 14.7 %collective-permute-start.51 = (bf16[256,896]{1,0:T(8,128)(2,1)}, bf16[256,896]{1,0:T(8,128)(2,1)}, u32[]{:S(2)}, u32[]{:S(2)}) collective-permute-start(bf16[256,896]{1,0:T(8,128)(2,1)} %add_convert_fusion.9), channel_id=1, source_target_pairs={{0,4},{4,8},{8,12},{12,0},{1,5},{5,9},{9,13},{13,1},{2,6},{6,10},{... | collective-permute-start | bytes 1376264 | tf_op jit(solution)/shard_map/ppermute | solution.py:521
  319.4 15.0 %collective-permute-start.60 = (bf16[256,896]{1,0:T(8,128)(2,1)}, bf16[256,896]{1,0:T(8,128)(2,1)}, u32[]{:S(2)}, u32[]{:S(2)}) collective-permute-start(bf16[256,896]{1,0:T(8,128)(2,1)} %add_convert_fusion.7), channel_id=1, source_target_pairs={{0,4},{4,8},{8,12},{12,0},{1,5},{5,9},{9,13},{13,1},{2,6},{6,10},{... | collective-permute-start | bytes 1376264 | tf_op jit(solution)/shard_map/ppermute | solution.py:521
  324.7 22.0 %collective-permute-start.55 = (f32[1024,256]{1,0:T(8,128)S(1)}, f32[1024,256]{1,0:T(8,128)S(1)}, u32[]{:S(2)}, u32[]{:S(2)}) collective-permute-start(f32[1024,256]{1,0:T(8,128)S(1)} %get-tuple-element.333), channel_id=1, source_target_pairs={{0,16},{16,0},{1,17},{17,1},{2,18},{18,2},{3,19},{19,3},{4,20},{20... | collective-permute-start | bytes 3145736 | tf_op jit(solution)/shard_map/ppermute | solution.py:463
  324.8 21.9 %collective-permute-start.59 = (f32[17152]{0:T(1024)S(1)}, f32[17152]{0:T(1024)S(1)}, u32[]{:S(2)}, u32[]{:S(2)}) collective-permute-start(f32[17152]{0:T(1024)S(1)} %select_add_fusion), channel_id=1, source_target_pairs={{0,12},{4,0},{8,4},{12,8},{1,13},{5,1},{9,5},{13,9},{2,14},{6,2},{... | collective-permute-start | bytes 205832 | tf_op jit(solution)/shard_map/ppermute | solution.py:532
  328.7 19.4 %collective-permute-start.58 = (f32[17152]{0:T(1024)S(1)}, f32[17152]{0:T(1024)S(1)}, u32[]{:S(2)}, u32[]{:S(2)}) collective-permute-start(f32[17152]{0:T(1024)S(1)} %select_add_fusion), channel_id=1, source_target_pairs={{0,8},{4,12},{8,0},{12,4},{1,9},{5,13},{9,1},{13,5},{2,10},{6,14},... | collective-permute-start | bytes 205832 | tf_op jit(solution)/shard_map/ppermute | solution.py:532
  328.7 19.4 %collective-permute-start.57 = (f32[17152]{0:T(1024)S(1)}, f32[17152]{0:T(1024)S(1)}, u32[]{:S(2)}, u32[]{:S(2)}) collective-permute-start(f32[17152]{0:T(1024)S(1)} %select_add_fusion), channel_id=1, source_target_pairs={{0,4},{4,8},{8,12},{12,0},{1,5},{5,9},{9,13},{13,1},{2,6},{6,10},{... | collective-permute-start | bytes 205832 | tf_op jit(solution)/shard_map/ppermute | solution.py:532
  (106 other events, 1093.9 us)
